TPU v7x, 32 devices: a whole 2x2x4 slice. The times are simulated.
32 devices in a mesh: dp: 2 (over x), expert: 16 (over z, y, core).
Axes of the slice: x: 2, y: 2, z: 4, core: 2. Of those that a mesh axis runs over, the one named last changes fastest.
Arguments:
- hidden: bfloat16 [2, 1024, 2, 2048], P('dp', 'expert'), may hold values from -6 to 6
- queries: bfloat16 [2, 1024, 2, 4096], P('dp', 'expert'), may hold values from -45 to 45
- latents: bfloat16 [2, 1024, 2, 512], P('dp', 'expert'), may hold values from -165 to 165
- mem_latents: bfloat16 [2, 32, 2, 512], P('dp'), may hold values from -6 to 6
- lengths: int32 [2, 2], P('dp'), may hold values from 512 to 1024
- ids: int32 [2, 1024, 2, 6], P('dp', 'expert'), may hold values from 0 to 15, all different within a row; in each aligned block of 128 rows (0 to 127, 128 to 255, ..., all dimensions but the last counted through in order) at most 50 rows name the same one
- gates: bfloat16 [2, 1024, 2, 6], P('dp', 'expert'), may hold values from 0.049804688 to 0.5
- norm_gain: bfloat16 [2048], replicated, may hold values from 0.25 to 1.75
- w_uv: bfloat16 [8, 512, 128], P('dp'), may hold values from -0.25 to 0.25
- w_out: bfloat16 [1024, 2048], P('dp'), may hold values from -0.1875 to 0.1875
- w_gate: bfloat16 [16, 2048, 704], P('expert'), may hold values from -0.125 to 0.125
- w_up: bfloat16 [16, 2048, 704], P('expert'), may hold values from -0.125 to 0.125
- w_down: bfloat16 [16, 704, 2048], P('expert'), may hold values from -0.21875 to 0.21875
Outputs:
- layer_out: bfloat16 [2, 1024, 2, 2048], P('dp', 'expert')
Inputs may be any that keep to these rules, and one draw needn't show every extreme that they name: `ids`: each row names 6 different experts; the rows of one device (aligned blocks of 128 rows in the order of the leading dimensions) name any one expert at most 50 times, a bound that some block reaches.
All inputs are finite; a program needn't handle non-finite values.
Results may differ from a plain program's by a relative error of at most 0.007.
Values may be sent and summed in bfloat16 or wider, within the bound.
No kernel may reach another device: no remote copies, remote signals or barrier semaphores. Data moves between devices by JAX's collectives and lax.ppermute only.
A program may use at most 128 MiB of HBM per device.

v0:
```python
import functools

import jax
import jax.numpy as jnp
from jax import lax
from jax.experimental import pallas as pl
from jax.experimental.pallas import tpu as pltpu
from jax.sharding import PartitionSpec as P


score_scale = 192.0 ** (-0.5)
norm_eps = 1e-06


cuts = 2

bf16, f32, i32 = jnp.bfloat16, jnp.float32, jnp.int32
VMEM = pl.BlockSpec(memory_space=pltpu.VMEM)
SMEM = pl.BlockSpec(memory_space=pltpu.SMEM)
ANY = pl.BlockSpec(memory_space=pl.ANY)


def flip(value, mask, size):
    return lax.ppermute(value, "expert", [(i, i ^ mask) for i in range(size)])


def call(body, in_specs, outs, operands, flops=0, scratch=(), limit=24):
    return pl.pallas_call(
        body,
        in_specs=in_specs,
        out_specs=[VMEM] * len(outs),
        out_shape=[jax.ShapeDtypeStruct(s, d) for s, d in outs],
        scratch_shapes=list(scratch),
        compiler_params=pltpu.CompilerParams(vmem_limit_bytes=limit * 1024 * 1024),
        cost_estimate=pl.CostEstimate(flops=flops, bytes_accessed=0, transcendentals=0),
    )(*operands)


def gather_latents(own, size):
    pieces = {0: own}
    quarter = size // 4
    for mask in (2 * quarter, 3 * quarter, quarter):
        pieces[mask] = flip(own, mask, size)
    step = quarter // 2
    while step:
        for mask in list(pieces):
            pieces[mask ^ step] = flip(pieces[mask], step, size)
        step //= 2
    return [pieces[m] for m in range(size)]


def fetch_weights(w_uv, w_out, core, size):
    dp = lax.axis_size("dp")
    heads = w_uv.shape[0]
    half = heads // 2
    width = w_out.shape[0] // heads
    uv_half = lax.dynamic_slice_in_dim(w_uv, core * half, half, 0)
    out_half = lax.dynamic_slice_in_dim(w_out, core * half * width, half * width, 0)
    parts = [(w_uv, w_out)]
    for turn in range(1, dp):
        source = [((i + turn) % dp, i) for i in range(dp)]
        uv_got = lax.ppermute(uv_half, "dp", source)
        out_got = lax.ppermute(out_half, "dp", source)
        parts.append((uv_got, out_got))
        parts.append((flip(uv_got, 1, size), flip(out_got, 1, size)))
    return parts


def head_order(core, heads):
    dp = lax.axis_size("dp")
    index = lax.axis_index("dp")
    half = heads // 2
    order = [index * heads + h for h in range(heads)]
    for turn in range(1, dp):
        first = ((index + turn) % dp) * heads
        order += [first + core * half + h for h in range(half)]
        order += [first + (1 - core) * half + h for h in range(half)]
    return jnp.stack(order).astype(i32)


def attend_body(size, local_len, seq_count, latent, heads, group, *refs):
    info, lengths, queries, memory = refs[:4]
    pieces = refs[4 : 4 + size]
    out, keys, rows = refs[4 + size :]
    seg_len = size * local_len
    total_len = seg_len + memory.shape[0]
    shift = local_len.bit_length() - 1
    index = info[0]
    at = lax.broadcasted_iota(i32, (local_len, total_len), 1)
    row = lax.broadcasted_iota(i32, (local_len, total_len), 0)
    pos = jnp.left_shift(jnp.bitwise_xor(jnp.right_shift(at, shift), index), shift) + jnp.bitwise_and(
        at, local_len - 1
    )
    pos = jnp.where(at < seg_len, pos, -1)
    causal = pos <= index * local_len + row
    for s in range(seq_count):
        cols = pl.ds(s * latent, latent)
        for m in range(size):
            keys[pl.ds(m * local_len, local_len), :] = pieces[m][:, cols]
        keys[pl.ds(seg_len, memory.shape[0]), :] = memory[:, cols]
        bias = jnp.where(causal & (pos < lengths[0, s]), 0.0, -jnp.inf)
        bias = jnp.concatenate([bias] * group, axis=0)
        for first in range(0, heads, group):
            for h in range(group):
                rows[pl.ds(h * local_len, local_len), :] = queries[
                    :, pl.ds((s * heads + first + h) * latent, latent)
                ]
            scores = lax.dot_general(
                rows[...], keys[...], (((1,), (1,)), ((), ())), preferred_element_type=f32
            )
            scores = scores * score_scale + bias
            top = jnp.max(scores, axis=1, keepdims=True)
            weights = jnp.exp(scores - top)
            total = jnp.sum(weights, axis=1, keepdims=True)
            got = jnp.dot(weights.astype(bf16), keys[...], preferred_element_type=f32) / total
            got = got.astype(bf16)
            for h in range(group):
                out[pl.ds(s * local_len, local_len), pl.ds((first + h) * latent, latent)] = got[
                    h * local_len : (h + 1) * local_len
                ]


def routes(info, table, top, half, capacity):
    rows = table.shape[0]
    table = table[...]
    names, gates = table[:, :top], table[:, top : 2 * top]
    lane = lax.broadcasted_iota(i32, (rows, half), 1)
    named = jnp.zeros((rows, half), f32)
    weight = jnp.zeros((rows, half), f32)
    for m in range(half):
        hit = names == info[2 + m].astype(f32)
        count = jnp.sum(jnp.where(hit, 1.0, 0.0), axis=1, keepdims=True)
        share = jnp.sum(jnp.where(hit, gates, 0.0), axis=1, keepdims=True)
        named = jnp.where(lane == m, count, named)
        weight = jnp.where(lane == m, share, weight)
    r = lax.broadcasted_iota(i32, (rows, rows), 0)
    c = lax.broadcasted_iota(i32, (rows, rows), 1)
    upto = jnp.where(c <= r, 1.0, 0.0).astype(bf16)
    rank = named * jnp.dot(upto, named.astype(bf16), preferred_element_type=f32)
    wide = half * capacity
    col = lax.broadcasted_iota(i32, (half, wide), 1)
    start = lax.broadcasted_iota(i32, (half, wide), 0) * capacity
    inside = (col >= start) & (col < start + capacity)
    spread = jnp.where(inside, 1.0, 0.0).astype(bf16)
    slot = jnp.sum(jnp.where(inside, col - start + 1, 0), axis=0, keepdims=True).astype(f32)
    rank = jnp.dot(rank.astype(bf16), spread, preferred_element_type=f32)
    weight = jnp.dot(weight.astype(bf16), spread, preferred_element_type=f32)
    place = rank == slot
    return jnp.where(place, 1.0, 0.0).astype(bf16), jnp.where(place, weight, 0.0).astype(bf16)


def routes_body(half, capacity, top, info, near_table, far_table, near_place, near_mix, far_place, far_mix):
    near_place[...], near_mix[...] = routes(info, near_table, top, half, capacity)
    far_place[...], far_mix[...] = routes(info, far_table, top, half, capacity)


def place_body(capacity, cuts, placing, *refs):
    across = (((0,), (0,)), ((), ()))
    rows = jnp.concatenate([r[...] for r in refs[:cuts]], axis=1)
    sent = lax.dot_general(placing[...], rows, across, preferred_element_type=f32).astype(bf16)
    for m, block in enumerate(refs[cuts:]):
        block[...] = sent[m * capacity : (m + 1) * capacity]


def norm_body(parts, seq_count, latent, *refs):
    order, attended, hidden, gain = refs[:4]
    maps = refs[4 : 4 + 2 * parts]
    residual = refs[4 + 2 * parts]
    chunks = refs[5 + 2 * parts :]
    width = gain.shape[1]
    acc = jnp.concatenate([hidden[:, s * width : (s + 1) * width] for s in range(seq_count)], axis=0).astype(f32)
    slot = 0
    for part in range(parts):
        uv, proj = maps[2 * part], maps[2 * part + 1]
        values = []
        for h in range(uv.shape[0]):
            at = pl.multiple_of(order[slot] * latent, latent)
            got = jnp.dot(attended[:, pl.ds(at, latent)], uv[h], preferred_element_type=f32)
            values.append(got.astype(bf16))
            slot += 1
        acc = acc + jnp.dot(jnp.concatenate(values, axis=1), proj[...], preferred_element_type=f32)
    residual[...] = acc
    mean_square = jnp.mean(acc * acc, axis=1, keepdims=True)
    scaled = (acc * lax.rsqrt(mean_square + norm_eps) * gain[...].astype(f32)).astype(bf16)
    step = width // len(chunks)
    for c, chunk in enumerate(chunks):
        chunk[...] = scaled[:, c * step : (c + 1) * step]


def expert_body(half, capacity, cuts, *refs):
    gate_hbm, up_hbm, down_hbm = refs[:3]
    count = half * cuts
    taken = refs[3 : 3 + count]
    given = refs[3 + count : 3 + 2 * count]
    gate, up, down, rows, sems = refs[3 + 2 * count :]
    step = rows.shape[1] // cuts
    copies = [
        pltpu.make_async_copy(source.at[0], target, sems.at[i])
        for i, (source, target) in enumerate(((gate_hbm, gate), (up_hbm, up), (down_hbm, down)))
    ]
    for copy in copies:
        copy.start()
    for c in range(cuts):
        for m in range(half):
            rows[pl.ds(m * capacity, capacity), pl.ds(c * step, step)] = taken[c * half + m][...]
    across = (((1,), (1,)), ((), ()))
    copies[0].wait()
    gate_h = lax.dot_general(rows[...], gate[...], across, preferred_element_type=f32)
    copies[1].wait()
    up_h = lax.dot_general(rows[...], up[...], across, preferred_element_type=f32)
    act = (gate_h / (1.0 + jnp.exp(-gate_h)) * up_h).astype(bf16)
    copies[2].wait()
    for c in range(cuts):
        out = jnp.dot(act, down[:, c * step : (c + 1) * step], preferred_element_type=f32).astype(bf16)
        for m in range(half):
            given[c * half + m][...] = out[m * capacity : (m + 1) * capacity]


def mix_body(half, capacity, mixing, *refs):
    taken, out, rows = refs[:half], refs[half], refs[half + 1]
    for m in range(half):
        rows[pl.ds(m * capacity, capacity), :] = taken[m][...]
    out[...] = jnp.dot(mixing[...], rows[...], preferred_element_type=f32).astype(bf16)


def last_body(half, capacity, cuts, local_len, seq_count, mixing, residual, *refs):
    others, taken, out, rows = refs[:cuts], refs[cuts : cuts + half], refs[cuts + half], refs[cuts + half + 1]
    for m in range(half):
        rows[pl.ds(m * capacity, capacity), :] = taken[m][...]
    total = jnp.dot(mixing[...], rows[...], preferred_element_type=f32)
    other = jnp.concatenate([o[...] for o in others], axis=1)
    total = (residual[...] + total + other.astype(f32)).astype(bf16)
    width = total.shape[1]
    for s in range(seq_count):
        out[:, s * width : (s + 1) * width] = total[s * local_len : (s + 1) * local_len]


def layer(
    hidden,
    queries,
    latents,
    mem_latents,
    lengths,
    ids,
    gates,
    norm_gain,
    w_uv,
    w_out,
    w_gate,
    w_up,
    w_down,
):
    local_len, seq_count, width = hidden.shape[1:]
    latent = latents.shape[3]
    heads = queries.shape[3] // latent
    rows = local_len * seq_count
    top = ids.shape[3]
    size = lax.axis_size("expert")
    index = lax.axis_index("expert")
    core = index & 1
    half = size // 2
    capacity = min(rows, rows * top // size + 2)
    capacity = -(-capacity // 8) * 8
    index_here = index % half
    owners = index - index_here + (index_here ^ jnp.arange(half, dtype=i32))
    info = jnp.concatenate([jnp.stack([index, core]).astype(i32), owners])

    parts = fetch_weights(w_uv, w_out, core, size)
    pieces = gather_latents(latents[0].reshape(local_len, seq_count * latent), size)
    table = jnp.concatenate([ids[0].astype(f32), gates[0].astype(f32)], axis=2)
    table = jnp.transpose(table, (1, 0, 2)).reshape(rows, 2 * top)
    far_table = flip(table, half, size)
    wide = half * capacity
    near_placing, near_mix, far_placing, far_mix = call(
        functools.partial(routes_body, half, capacity, top),
        [SMEM, VMEM, VMEM],
        [((rows, wide), bf16)] * 4,
        [info, table, far_table],
        flops=4 * rows * rows * wide,
    )

    group = max(1, min(heads, 256 // local_len))
    total_len = size * local_len + mem_latents.shape[1]
    (attended,) = call(
        functools.partial(attend_body, size, local_len, seq_count, latent, heads, group),
        [SMEM, SMEM, VMEM, VMEM] + [VMEM] * size,
        [((rows, heads * latent), bf16)],
        [
            info,
            lengths,
            queries[0].reshape(local_len, seq_count * heads * latent),
            mem_latents[0].reshape(-1, seq_count * latent),
            *pieces,
        ],
        flops=4 * rows * heads * latent * total_len,
        scratch=[pltpu.VMEM((total_len, latent), bf16), pltpu.VMEM((group * local_len, latent), bf16)],
        limit=16 + total_len * 9 // 1024,
    )
    step = width // cuts
    residual, *normed = call(
        functools.partial(norm_body, len(parts), seq_count, latent),
        [SMEM] + [VMEM] * (3 + 2 * len(parts)),
        [((rows, width), f32)] + [((rows, step), bf16)] * cuts,
        [
            head_order(core, w_uv.shape[0]),
            attended,
            hidden[0].reshape(local_len, seq_count * width),
            norm_gain.reshape(1, width),
            *[w for part in parts for w in part],
        ],
        flops=2 * rows * width * heads * w_uv.shape[2],
    )

    def swap(blocks):
        return [blocks[0]] + [flip(blocks[m], m, size) for m in range(1, half)]

    def place(placing, chunks):
        return call(
            functools.partial(place_body, capacity, len(chunks)),
            [VMEM] * (1 + len(chunks)),
            [((capacity, sum(c.shape[1] for c in chunks)), bf16)] * half,
            [placing, *chunks],
            flops=2 * rows * width * wide,
        )

    def experts(blocks):
        return call(
            functools.partial(expert_body, half, capacity, len(blocks) // half),
            [ANY] * 3 + [VMEM] * len(blocks),
            [(b.shape, bf16) for b in blocks],
            [jnp.swapaxes(w_gate, 1, 2), jnp.swapaxes(w_up, 1, 2), w_down, *blocks],
            flops=6 * wide * width * w_gate.shape[2],
            scratch=[pltpu.VMEM(w_down.shape[1:], bf16)] * 3
            + [pltpu.VMEM((wide, width), bf16), pltpu.SemaphoreType.DMA((3,))],
            limit=32,
        )

    hops = [flip(chunk, half, size) for chunk in normed]
    near_in = swap(place(near_placing, normed))
    far_in = []
    for c in range(cuts):
        far_in += swap(place(far_placing, [hops[c]]))
    near_out = swap(experts(near_in))
    far_out = experts(far_in)
    others = []
    for c in range(cuts):
        (far_sum,) = call(
            functools.partial(mix_body, half, capacity),
            [VMEM] * (1 + half),
            [((rows, step), bf16)],
            [far_mix, *swap(far_out[c * half : (c + 1) * half])],
            flops=2 * rows * step * wide,
            scratch=[pltpu.VMEM((wide, step), bf16)],
        )
        others.append(flip(far_sum, half, size))
    (out,) = call(
        functools.partial(last_body, half, capacity, cuts, local_len, seq_count),
        [VMEM] * (2 + cuts + half),
        [((local_len, seq_count * width), bf16)],
        [near_mix, residual, *others, *near_out],
        flops=2 * rows * width * wide,
        scratch=[pltpu.VMEM((wide, width), bf16)],
    )
    return out.reshape(1, local_len, seq_count, width)


def solution(mesh):
    return spread(mesh)


def spread(mesh):
    return jax.shard_map(
        layer,
        mesh=mesh,
        in_specs=(
            P("dp", "expert", None, None),
            P("dp", "expert", None, None),
            P("dp", "expert", None, None),
            P("dp", None, None, None),
            P("dp", None),
            P("dp", "expert", None, None),
            P("dp", "expert", None, None),
            P(),
            P("dp", None, None),
            P("dp", None),
            P("expert", None, None),
            P("expert", None, None),
            P("expert", None, None),
        ),
        out_specs=P("dp", "expert", None, None),
        check_vma=False,
    )
```

profile of v0, /device:TPU:0, one launch (start us, length us, event | category | flops | bytes accessed | tf_op | source)
XLA Modules:
  0.0 210.2 jit_solution(12646654341702261925)
XLA Ops:
  1.3 3.0 %collective-permute-start.17 = (bf16[256,2048]{1,0:T(8,128)(2,1)S(1)}, bf16[256,2048]{1,0:T(8,128)(2,1)S(1)}, u32[]{:S(2)}, u32[]{:S(2)}) collective-permute-start(bf16[256,2048]{1,0:T(8,128)(2,1)S(1)} %constant_dynamic-slice_fusion), channel_id=1, source_target_pairs={{16,0},{0,16},{17,1},{1,17},{18,2},{2,18},{19,3},{3,19},{20,4},{4,... | collective-permute-start | bytes 3145736 | tf_op jit(solution)/shard_map/ppermute | solution.py:63
  5.4 1.6 collective-permute-start.4
  8.5 2.6 %collective-permute-start.8 = (bf16[64,1024]{1,0:T(8,128)(2,1)S(1)}, bf16[64,1024]{1,0:T(8,128)(2,1)S(1)}, u32[]{:S(2)}, u32[]{:S(2)}) collective-permute-start(bf16[64,1024]{1,0:T(8,128)(2,1)S(1)} %bitcast.39), channel_id=1, source_target_pairs={{0,8},{1,9},{2,10},{3,11},{4,12},{5,13},{6,14},{7,15},{8,0},{9,1},... | collective-permute-start | bytes 393224 | tf_op jit(solution)/shard_map/ppermute | solution.py:24
  11.4 16.2 %collective-permute-done.17.refs_7_ = bf16[256,2048]{1,0:T(8,128)(2,1)S(1)} collective-permute-done((bf16[256,2048]{1,0:T(8,128)(2,1)S(1)}, bf16[256,2048]{1,0:T(8,128)(2,1)S(1)}, u32[]{:S(2)}, u32[]{:S(2)}) %collective-permute-start.17) | collective-permute-done | bytes 1048608 | tf_op jit(solution)/shard_map/ppermute | solution.py:63
  28.1 1.8 collective-permute-start.6
  34.7 1.6 collective-permute-start.14
  36.3 4.4 %collective-permute-done.10.refs_14_ = bf16[64,1024]{1,0:T(8,128)(2,1)} collective-permute-done((bf16[64,1024]{1,0:T(8,128)(2,1)S(1)}, bf16[64,1024]{1,0:T(8,128)(2,1)}, u32[]{:S(2)}, u32[]{:S(2)}) %collective-permute-start.10) | collective-permute-done | bytes 131104 | tf_op jit(solution)/shard_map/ppermute | solution.py:24
  43.0 1.8 copy.15
  54.3 5.5 %shard_map.128.refs_1_ = bf16[128,4096]{1,0:T(8,128)(2,1)S(1)} custom-call(s32[10]{0:T(128)S(1)} %pad_add_fusion.info.refs_0_, s32[1,2]{1,0:T(1,128)S(1)} %copy-done.24, bf16[64,8192]{1,0:T(8,128)(2,1)S(1)} %bitcast.33, bf16[32,1024]{1,0:T(8,128)(2,1)S(1)} %bitcast.42, bf16[64,1024]{1,0:T(8,128)(2,1)S(1)} %bitcast.41, ...), custom_call_target="tpu_custom_call" | custom-call | flops 2214592512 | tf_op jit(solution)/shard_map/pallas_call | solution.py:28
  59.8 3.5 %shard_map.129 = (f32[128,2048]{1,0:T(8,128)S(1)}, bf16[128,1024]{1,0:T(8,128)(2,1)}, bf16[128,1024]{1,0:T(8,128)(2,1)}) custom-call(s32[8]{0:T(128)S(1)} %stack.43.refs_0_, bf16[128,4096]{1,0:T(8,128)(2,1)S(1)} %shard_map.128.refs_1_, bf16[64,4096]{1,0:T(8,128)(2,1)S(1)} %bitcast.32, bf16[1,2048]{1,0:T(2,128)(2,1)S(1)} %reshape.13.refs_3_, ...), custom_call_target="tpu_custom_call" | custom-call | flops 536870912 | tf_op jit(solution)/shard_map/pallas_call | solution.py:28
  63.3 2.6 %collective-permute-start.20 = (bf16[128,1024]{1,0:T(8,128)(2,1)}, bf16[128,1024]{1,0:T(8,128)(2,1)S(1)}, u32[]{:S(2)}, u32[]{:S(2)}) collective-permute-start(bf16[128,1024]{1,0:T(8,128)(2,1)} %get-tuple-element.64.refs_0_), channel_id=1, source_target_pairs={{0,8},{1,9},{2,10},{3,11},{4,12},{5,13},{6,14},{7,15},{8,0},{9,1},... | collective-permute-start | bytes 786440 | tf_op jit(solution)/shard_map/ppermute | solution.py:24
  66.4 2.6 %collective-permute-start = (f32[128,12]{1,0:T(8,128)S(1)}, f32[128,12]{1,0:T(8,128)S(1)}, u32[]{:S(2)}, u32[]{:S(2)}) collective-permute-start(f32[128,12]{1,0:T(8,128)S(1)} %bitcast.34), channel_id=1, source_target_pairs={{0,8},{1,9},{2,10},{3,11},{4,12},{5,13},{6,14},{7,15},{8,0},{9,1},... | collective-permute-start | bytes 18440 | tf_op jit(solution)/shard_map/ppermute | solution.py:24
  69.0 23.3 %collective-permute-done.far_table = f32[128,12]{1,0:T(8,128)S(1)} collective-permute-done((f32[128,12]{1,0:T(8,128)S(1)}, f32[128,12]{1,0:T(8,128)S(1)}, u32[]{:S(2)}, u32[]{:S(2)}) %collective-permute-start) | collective-permute-done | bytes 6176 | tf_op jit(solution)/shard_map/ppermute | solution.py:24
  93.8 1.7 shard_map.135
  96.8 1.5 collective-permute-start.22
  99.6 4.5 %collective-permute-done.53.refs_5_ = bf16[56,2048]{1,0:T(8,128)(2,1)S(1)} collective-permute-done((bf16[56,2048]{1,0:T(8,128)(2,1)S(1)}, bf16[56,2048]{1,0:T(8,128)(2,1)S(1)}, u32[]{:S(2)}, u32[]{:S(2)}) %collective-permute-start.53) | collective-permute-done | bytes 229408 | tf_op jit(solution)/shard_map/ppermute | solution.py:24
  104.7 1.8 collective-permute-done.22.refs_5_
  116.2 1.9 collective-permute-start.35
  122.5 1.5 collective-permute-start.57
  126.0 1.8 copy-done.2
  127.8 1.8 copy-done.4
  129.6 1.8 copy-done.6
  131.4 6.5 %shard_map.132 = (bf16[56,1024]{1,0:T(8,128)(2,1)S(1)}, bf16[56,1024]{1,0:T(8,128)(2,1)S(1)}, bf16[56,1024]{1,0:T(8,128)(2,1)S(1)}, bf16[56,1024]{1,0:T(8,128)(2...) custom-call(bf16[1,704,2048]{2,1,0:T(8,128)(2,1)S(1)} %bitcast.43, ...), custom_call_target="tpu_custom_call" | custom-call | flops 3875536896 | tf_op jit(solution)/shard_map/pallas_call | solution.py:28
  141.4 3.4 %collective-permute-done.58.refs_10_ = bf16[56,2048]{1,0:T(8,128)(2,1)S(1)} collective-permute-done((bf16[56,2048]{1,0:T(8,128)(2,1)S(1)}, bf16[56,2048]{1,0:T(8,128)(2,1)S(1)}, u32[]{:S(2)}, u32[]{:S(2)}) %collective-permute-start.58) | collective-permute-done | bytes 229408 | tf_op jit(solution)/shard_map/ppermute | solution.py:24
  155.9 1.8 collective-permute-start.49
  157.8 6.5 %shard_map.136 = (bf16[56,2048]{1,0:T(8,128)(2,1)S(1)}, bf16[56,2048]{1,0:T(8,128)(2,1)S(1)}, bf16[56,2048]{1,0:T(8,128)(2,1)S(1)}, bf16[56,2048]{1,0:T(8,128)(2...) custom-call(bf16[1,704,2048]{2,1,0:T(8,128)(2,1)S(1)} %bitcast.44, ...), custom_call_target="tpu_custom_call" | custom-call | flops 3875536896 | tf_op jit(solution)/shard_map/pallas_call | solution.py:28
  168.1 7.8 %collective-permute-done.50.refs_7_ = bf16[56,1024]{1,0:T(8,128)(2,1)S(1)} collective-permute-done((bf16[56,1024]{1,0:T(8,128)(2,1)S(1)}, bf16[56,1024]{1,0:T(8,128)(2,1)S(1)}, u32[]{:S(2)}, u32[]{:S(2)}) %collective-permute-start.50) | collective-permute-done | bytes 114720 | tf_op jit(solution)/shard_map/ppermute | solution.py:24
  175.9 2.7 %collective-permute-start.43 = (bf16[128,1024]{1,0:T(8,128)(2,1)S(1)}, bf16[128,1024]{1,0:T(8,128)(2,1)S(1)}, u32[]{:S(2)}, u32[]{:S(2)}) collective-permute-start(bf16[128,1024]{1,0:T(8,128)(2,1)S(1)} %shard_map.133), channel_id=1, source_target_pairs={{0,8},{1,9},{2,10},{3,11},{4,12},{5,13},{6,14},{7,15},{8,0},{9,1},... | collective-permute-start | bytes 786440 | tf_op jit(solution)/shard_map/ppermute | solution.py:24
  180.2 1.6 collective-permute-start.64
  183.0 12.9 %collective-permute-done.63.refs_7_ = bf16[56,2048]{1,0:T(8,128)(2,1)S(1)} collective-permute-done((bf16[56,2048]{1,0:T(8,128)(2,1)S(1)}, bf16[56,2048]{1,0:T(8,128)(2,1)S(1)}, u32[]{:S(2)}, u32[]{:S(2)}) %collective-permute-start.63) | collective-permute-done | bytes 229408 | tf_op jit(solution)/shard_map/ppermute | solution.py:24
  195.8 7.8 %collective-permute-done.64.refs_8_ = bf16[56,2048]{1,0:T(8,128)(2,1)S(1)} collective-permute-done((bf16[56,2048]{1,0:T(8,128)(2,1)S(1)}, bf16[56,2048]{1,0:T(8,128)(2,1)S(1)}, u32[]{:S(2)}, u32[]{:S(2)}) %collective-permute-start.64) | collective-permute-done | bytes 229408 | tf_op jit(solution)/shard_map/ppermute | solution.py:24
  203.6 5.0 %collective-permute-done.65.refs_9_ = bf16[56,2048]{1,0:T(8,128)(2,1)S(1)} collective-permute-done((bf16[56,2048]{1,0:T(8,128)(2,1)S(1)}, bf16[56,2048]{1,0:T(8,128)(2,1)S(1)}, u32[]{:S(2)}, u32[]{:S(2)}) %collective-permute-start.65) | collective-permute-done | bytes 229408 | tf_op jit(solution)/shard_map/ppermute | solution.py:24
  (180 shorter events, 64.9 us)
Async XLA Ops:
  1.3 26.2 %collective-permute-start.17 = (bf16[256,2048]{1,0:T(8,128)(2,1)S(1)}, bf16[256,2048]{1,0:T(8,128)(2,1)S(1)}, u32[]{:S(2)}, u32[]{:S(2)}) collective-permute-start(bf16[256,2048]{1,0:T(8,128)(2,1)S(1)} %constant_dynamic-slice_fusion), channel_id=1, source_target_pairs={{16,0},{0,16},{17,1},{1,17},{18,2},{2,18},{19,3},{3,19},{20,4},{4,... | collective-permute-start | bytes 3145736 | tf_op jit(solution)/shard_map/ppermute | solution.py:63
  5.4 22.2 %collective-permute-start.4 = (bf16[64,1024]{1,0:T(8,128)(2,1)S(1)}, bf16[64,1024]{1,0:T(8,128)(2,1)S(1)}, u32[]{:S(2)}, u32[]{:S(2)}) collective-permute-start(bf16[64,1024]{1,0:T(8,128)(2,1)S(1)} %bitcast.37), channel_id=1, source_target_pairs={{0,4},{1,5},{2,6},{3,7},{4,0},{5,1},{6,2},{7,3},{8,12},{9,13},{10,... | collective-permute-start | bytes 393224 | tf_op jit(solution)/shard_map/ppermute | solution.py:24
  7.0 21.0 %collective-permute-start.2 = (bf16[64,1024]{1,0:T(8,128)(2,1)S(1)}, bf16[64,1024]{1,0:T(8,128)(2,1)S(1)}, u32[]{:S(2)}, u32[]{:S(2)}) collective-permute-start(bf16[64,1024]{1,0:T(8,128)(2,1)S(1)} %bitcast.38), channel_id=1, source_target_pairs={{0,2},{1,3},{2,0},{3,1},{4,6},{5,7},{6,4},{7,5},{8,10},{9,11},{10,... | collective-permute-start | bytes 393224 | tf_op jit(solution)/shard_map/ppermute | solution.py:24
  8.5 21.3 %collective-permute-start.8 = (bf16[64,1024]{1,0:T(8,128)(2,1)S(1)}, bf16[64,1024]{1,0:T(8,128)(2,1)S(1)}, u32[]{:S(2)}, u32[]{:S(2)}) collective-permute-start(bf16[64,1024]{1,0:T(8,128)(2,1)S(1)} %bitcast.39), channel_id=1, source_target_pairs={{0,8},{1,9},{2,10},{3,11},{4,12},{5,13},{6,14},{7,15},{8,0},{9,1},... | collective-permute-start | bytes 393224 | tf_op jit(solution)/shard_map/ppermute | solution.py:24
  11.1 18.7 %collective-permute-start.12 = (bf16[64,1024]{1,0:T(8,128)(2,1)S(1)}, bf16[64,1024]{1,0:T(8,128)(2,1)S(1)}, u32[]{:S(2)}, u32[]{:S(2)}) collective-permute-start(bf16[64,1024]{1,0:T(8,128)(2,1)S(1)} %bitcast.40), channel_id=1, source_target_pairs={{0,12},{1,13},{2,14},{3,15},{4,8},{5,9},{6,10},{7,11},{8,4},{9,5},... | collective-permute-start | bytes 393224 | tf_op jit(solution)/shard_map/ppermute | solution.py:24
  27.5 32.3 %collective-permute-start.19 = (bf16[256,2048]{1,0:T(8,128)(2,1)S(1)}, bf16[256,2048]{1,0:T(8,128)(2,1)}, u32[]{:S(2)}, u32[]{:S(2)}) collective-permute-start(bf16[256,2048]{1,0:T(8,128)(2,1)S(1)} %collective-permute-done.17.refs_7_), channel_id=1, source_target_pairs={{0,1},{1,0},{2,3},{3,2},{4,5},{5,4},{6,7},{7,6},{8,9},{9,8},{10,11... | collective-permute-start | bytes 3145736 | tf_op jit(solution)/shard_map/ppermute | solution.py:24
  42.3 17.5 %collective-permute-start.18 = (bf16[2,512,128]{2,1,0:T(8,128)(2,1)S(1)}, bf16[2,512,128]{2,1,0:T(8,128)(2,1)S(1)}, u32[]{:S(2)}, u32[]{:S(2)}) collective-permute-start(bf16[2,512,128]{2,1,0:T(8,128)(2,1)S(1)} %collective-permute-done.16.refs_6_), channel_id=1, source_target_pairs={{0,1},{1,0},{2,3},{3,2},{4,5},{5,4},{6,7},{7,6},{8,9},{9,8},{10,11... | collective-permute-start | bytes 786440 | tf_op jit(solution)/shard_map/ppermute | solution.py:24
  63.3 32.8 %collective-permute-start.20 = (bf16[128,1024]{1,0:T(8,128)(2,1)}, bf16[128,1024]{1,0:T(8,128)(2,1)S(1)}, u32[]{:S(2)}, u32[]{:S(2)}) collective-permute-start(bf16[128,1024]{1,0:T(8,128)(2,1)} %get-tuple-element.64.refs_0_), channel_id=1, source_target_pairs={{0,8},{1,9},{2,10},{3,11},{4,12},{5,13},{6,14},{7,15},{8,0},{9,1},... | collective-permute-start | bytes 786440 | tf_op jit(solution)/shard_map/ppermute | solution.py:24
  65.9 32.6 %collective-permute-start.28 = (bf16[128,1024]{1,0:T(8,128)(2,1)}, bf16[128,1024]{1,0:T(8,128)(2,1)S(1)}, u32[]{:S(2)}, u32[]{:S(2)}) collective-permute-start(bf16[128,1024]{1,0:T(8,128)(2,1)} %get-tuple-element.73.refs_1_), channel_id=1, source_target_pairs={{0,8},{1,9},{2,10},{3,11},{4,12},{5,13},{6,14},{7,15},{8,0},{9,1},... | collective-permute-start | bytes 786440 | tf_op jit(solution)/shard_map/ppermute | solution.py:24
  66.4 26.0 %collective-permute-start = (f32[128,12]{1,0:T(8,128)S(1)}, f32[128,12]{1,0:T(8,128)S(1)}, u32[]{:S(2)}, u32[]{:S(2)}) collective-permute-start(f32[128,12]{1,0:T(8,128)S(1)} %bitcast.34), channel_id=1, source_target_pairs={{0,8},{1,9},{2,10},{3,11},{4,12},{5,13},{6,14},{7,15},{8,0},{9,1},... | collective-permute-start | bytes 18440 | tf_op jit(solution)/shard_map/ppermute | solution.py:24
  96.8 9.8 %collective-permute-start.22 = (bf16[56,1024]{1,0:T(8,128)(2,1)S(1)}, bf16[56,1024]{1,0:T(8,128)(2,1)S(1)}, u32[]{:S(2)}, u32[]{:S(2)}) collective-permute-start(bf16[56,1024]{1,0:T(8,128)(2,1)S(1)} %get-tuple-element.67), channel_id=1, source_target_pairs={{0,2},{1,3},{2,0},{3,1},{4,6},{5,7},{6,4},{7,5},{8,10},{9,11},{10,... | collective-permute-start | bytes 344072 | tf_op jit(solution)/shard_map/ppermute | solution.py:24
  98.5 10.1 %collective-permute-start.24 = (bf16[56,1024]{1,0:T(8,128)(2,1)S(1)}, bf16[56,1024]{1,0:T(8,128)(2,1)S(1)}, u32[]{:S(2)}, u32[]{:S(2)}) collective-permute-start(bf16[56,1024]{1,0:T(8,128)(2,1)S(1)} %get-tuple-element.69), channel_id=1, source_target_pairs={{0,4},{1,5},{2,6},{3,7},{4,0},{5,1},{6,2},{7,3},{8,12},{9,13},{10,... | collective-permute-start | bytes 344072 | tf_op jit(solution)/shard_map/ppermute | solution.py:24
  118.5 19.5 %collective-permute-start.54 = (bf16[56,2048]{1,0:T(8,128)(2,1)S(1)}, bf16[56,2048]{1,0:T(8,128)(2,1)S(1)}, u32[]{:S(2)}, u32[]{:S(2)}) collective-permute-start(bf16[56,2048]{1,0:T(8,128)(2,1)S(1)} %get-tuple-element.102), channel_id=1, source_target_pairs={{0,3},{1,2},{2,1},{3,0},{4,7},{5,6},{6,5},{7,4},{8,11},{9,10},{10,... | collective-permute-start | bytes 688136 | tf_op jit(solution)/shard_map/ppermute | solution.py:24
  119.8 18.6 %collective-permute-start.55 = (bf16[56,2048]{1,0:T(8,128)(2,1)S(1)}, bf16[56,2048]{1,0:T(8,128)(2,1)S(1)}, u32[]{:S(2)}, u32[]{:S(2)}) collective-permute-start(bf16[56,2048]{1,0:T(8,128)(2,1)S(1)} %get-tuple-element.103), channel_id=1, source_target_pairs={{0,4},{1,5},{2,6},{3,7},{4,0},{5,1},{6,2},{7,3},{8,12},{9,13},{10,... | collective-permute-start | bytes 688136 | tf_op jit(solution)/shard_map/ppermute | solution.py:24
  121.2 18.8 %collective-permute-start.56 = (bf16[56,2048]{1,0:T(8,128)(2,1)S(1)}, bf16[56,2048]{1,0:T(8,128)(2,1)S(1)}, u32[]{:S(2)}, u32[]{:S(2)}) collective-permute-start(bf16[56,2048]{1,0:T(8,128)(2,1)S(1)} %get-tuple-element.104), channel_id=1, source_target_pairs={{0,5},{1,4},{2,7},{3,6},{4,1},{5,0},{6,3},{7,2},{8,13},{9,12},{10,... | collective-permute-start | bytes 688136 | tf_op jit(solution)/shard_map/ppermute | solution.py:24
  122.5 17.4 %collective-permute-start.57 = (bf16[56,2048]{1,0:T(8,128)(2,1)S(1)}, bf16[56,2048]{1,0:T(8,128)(2,1)S(1)}, u32[]{:S(2)}, u32[]{:S(2)}) collective-permute-start(bf16[56,2048]{1,0:T(8,128)(2,1)S(1)} %get-tuple-element.105), channel_id=1, source_target_pairs={{0,6},{1,7},{2,4},{3,5},{4,2},{5,3},{6,0},{7,1},{8,14},{9,15},{10,... | collective-permute-start | bytes 688136 | tf_op jit(solution)/shard_map/ppermute | solution.py:24
  125.1 19.7 %collective-permute-start.58 = (bf16[56,2048]{1,0:T(8,128)(2,1)S(1)}, bf16[56,2048]{1,0:T(8,128)(2,1)S(1)}, u32[]{:S(2)}, u32[]{:S(2)}) collective-permute-start(bf16[56,2048]{1,0:T(8,128)(2,1)S(1)} %get-tuple-element.106), channel_id=1, source_target_pairs={{0,7},{1,6},{2,5},{3,4},{4,3},{5,2},{6,1},{7,0},{8,15},{9,14},{10,... | collective-permute-start | bytes 688136 | tf_op jit(solution)/shard_map/ppermute | solution.py:24
  140.0 9.7 %collective-permute-start.39 = (bf16[56,1024]{1,0:T(8,128)(2,1)S(1)}, bf16[56,1024]{1,0:T(8,128)(2,1)S(1)}, u32[]{:S(2)}, u32[]{:S(2)}) collective-permute-start(bf16[56,1024]{1,0:T(8,128)(2,1)S(1)} %get-tuple-element.86), channel_id=1, source_target_pairs={{0,4},{1,5},{2,6},{3,7},{4,0},{5,1},{6,2},{7,3},{8,12},{9,13},{10,... | collective-permute-start | bytes 344072 | tf_op jit(solution)/shard_map/ppermute | solution.py:24
  149.7 14.5 %collective-permute-start.45 = (bf16[56,1024]{1,0:T(8,128)(2,1)S(1)}, bf16[56,1024]{1,0:T(8,128)(2,1)S(1)}, u32[]{:S(2)}, u32[]{:S(2)}) collective-permute-start(bf16[56,1024]{1,0:T(8,128)(2,1)S(1)} %get-tuple-element.92), channel_id=1, source_target_pairs={{0,2},{1,3},{2,0},{3,1},{4,6},{5,7},{6,4},{7,5},{8,10},{9,11},{10,... | collective-permute-start | bytes 344072 | tf_op jit(solution)/shard_map/ppermute | solution.py:24
  150.3 14.2 %collective-permute-start.46 = (bf16[56,1024]{1,0:T(8,128)(2,1)S(1)}, bf16[56,1024]{1,0:T(8,128)(2,1)S(1)}, u32[]{:S(2)}, u32[]{:S(2)}) collective-permute-start(bf16[56,1024]{1,0:T(8,128)(2,1)S(1)} %get-tuple-element.93), channel_id=1, source_target_pairs={{0,3},{1,2},{2,1},{3,0},{4,7},{5,6},{6,5},{7,4},{8,11},{9,10},{10,... | collective-permute-start | bytes 344072 | tf_op jit(solution)/shard_map/ppermute | solution.py:24
  152.9 12.0 %collective-permute-start.47 = (bf16[56,1024]{1,0:T(8,128)(2,1)S(1)}, bf16[56,1024]{1,0:T(8,128)(2,1)S(1)}, u32[]{:S(2)}, u32[]{:S(2)}) collective-permute-start(bf16[56,1024]{1,0:T(8,128)(2,1)S(1)} %get-tuple-element.94), channel_id=1, source_target_pairs={{0,4},{1,5},{2,6},{3,7},{4,0},{5,1},{6,2},{7,3},{8,12},{9,13},{10,... | collective-permute-start | bytes 344072 | tf_op jit(solution)/shard_map/ppermute | solution.py:24
  154.9 11.3 %collective-permute-start.48 = (bf16[56,1024]{1,0:T(8,128)(2,1)S(1)}, bf16[56,1024]{1,0:T(8,128)(2,1)S(1)}, u32[]{:S(2)}, u32[]{:S(2)}) collective-permute-start(bf16[56,1024]{1,0:T(8,128)(2,1)S(1)} %get-tuple-element.95), channel_id=1, source_target_pairs={{0,5},{1,4},{2,7},{3,6},{4,1},{5,0},{6,3},{7,2},{8,13},{9,12},{10,... | collective-permute-start | bytes 344072 | tf_op jit(solution)/shard_map/ppermute | solution.py:24
  155.9 11.5 %collective-permute-start.49 = (bf16[56,1024]{1,0:T(8,128)(2,1)S(1)}, bf16[56,1024]{1,0:T(8,128)(2,1)S(1)}, u32[]{:S(2)}, u32[]{:S(2)}) collective-permute-start(bf16[56,1024]{1,0:T(8,128)(2,1)S(1)} %get-tuple-element.96), channel_id=1, source_target_pairs={{0,6},{1,7},{2,4},{3,5},{4,2},{5,3},{6,0},{7,1},{8,14},{9,15},{10,... | collective-permute-start | bytes 344072 | tf_op jit(solution)/shard_map/ppermute | solution.py:24
  164.3 14.6 %collective-permute-start.59 = (bf16[56,2048]{1,0:T(8,128)(2,1)S(1)}, bf16[56,2048]{1,0:T(8,128)(2,1)S(1)}, u32[]{:S(2)}, u32[]{:S(2)}) collective-permute-start(bf16[56,2048]{1,0:T(8,128)(2,1)S(1)} %get-tuple-element.108), channel_id=1, source_target_pairs={{0,1},{1,0},{2,3},{3,2},{4,5},{5,4},{6,7},{7,6},{8,9},{9,8},{10,11... | collective-permute-start | bytes 688136 | tf_op jit(solution)/shard_map/ppermute | solution.py:24
  164.5 14.7 %collective-permute-start.60 = (bf16[56,2048]{1,0:T(8,128)(2,1)S(1)}, bf16[56,2048]{1,0:T(8,128)(2,1)S(1)}, u32[]{:S(2)}, u32[]{:S(2)}) collective-permute-start(bf16[56,2048]{1,0:T(8,128)(2,1)S(1)} %get-tuple-element.109), channel_id=1, source_target_pairs={{0,2},{1,3},{2,0},{3,1},{4,6},{5,7},{6,4},{7,5},{8,10},{9,11},{10,... | collective-permute-start | bytes 688136 | tf_op jit(solution)/shard_map/ppermute | solution.py:24
  164.8 15.3 %collective-permute-start.61 = (bf16[56,2048]{1,0:T(8,128)(2,1)S(1)}, bf16[56,2048]{1,0:T(8,128)(2,1)S(1)}, u32[]{:S(2)}, u32[]{:S(2)}) collective-permute-start(bf16[56,2048]{1,0:T(8,128)(2,1)S(1)} %get-tuple-element.110), channel_id=1, source_target_pairs={{0,3},{1,2},{2,1},{3,0},{4,7},{5,6},{6,5},{7,4},{8,11},{9,10},{10,... | collective-permute-start | bytes 688136 | tf_op jit(solution)/shard_map/ppermute | solution.py:24
  166.2 15.6 %collective-permute-start.62 = (bf16[56,2048]{1,0:T(8,128)(2,1)S(1)}, bf16[56,2048]{1,0:T(8,128)(2,1)S(1)}, u32[]{:S(2)}, u32[]{:S(2)}) collective-permute-start(bf16[56,2048]{1,0:T(8,128)(2,1)S(1)} %get-tuple-element.111), channel_id=1, source_target_pairs={{0,4},{1,5},{2,6},{3,7},{4,0},{5,1},{6,2},{7,3},{8,12},{9,13},{10,... | collective-permute-start | bytes 688136 | tf_op jit(solution)/shard_map/ppermute | solution.py:24
  175.9 32.7 %collective-permute-start.43 = (bf16[128,1024]{1,0:T(8,128)(2,1)S(1)}, bf16[128,1024]{1,0:T(8,128)(2,1)S(1)}, u32[]{:S(2)}, u32[]{:S(2)}) collective-permute-start(bf16[128,1024]{1,0:T(8,128)(2,1)S(1)} %shard_map.133), channel_id=1, source_target_pairs={{0,8},{1,9},{2,10},{3,11},{4,12},{5,13},{6,14},{7,15},{8,0},{9,1},... | collective-permute-start | bytes 786440 | tf_op jit(solution)/shard_map/ppermute | solution.py:24
  178.9 29.7 %collective-permute-start.51 = (bf16[128,1024]{1,0:T(8,128)(2,1)S(1)}, bf16[128,1024]{1,0:T(8,128)(2,1)S(1)}, u32[]{:S(2)}, u32[]{:S(2)}) collective-permute-start(bf16[128,1024]{1,0:T(8,128)(2,1)S(1)} %shard_map.134), channel_id=1, source_target_pairs={{0,8},{1,9},{2,10},{3,11},{4,12},{5,13},{6,14},{7,15},{8,0},{9,1},... | collective-permute-start | bytes 786440 | tf_op jit(solution)/shard_map/ppermute | solution.py:24
  179.2 16.6 %collective-permute-start.63 = (bf16[56,2048]{1,0:T(8,128)(2,1)S(1)}, bf16[56,2048]{1,0:T(8,128)(2,1)S(1)}, u32[]{:S(2)}, u32[]{:S(2)}) collective-permute-start(bf16[56,2048]{1,0:T(8,128)(2,1)S(1)} %get-tuple-element.112), channel_id=1, source_target_pairs={{0,5},{1,4},{2,7},{3,6},{4,1},{5,0},{6,3},{7,2},{8,13},{9,12},{10,... | collective-permute-start | bytes 688136 | tf_op jit(solution)/shard_map/ppermute | solution.py:24
  180.2 23.4 %collective-permute-start.64 = (bf16[56,2048]{1,0:T(8,128)(2,1)S(1)}, bf16[56,2048]{1,0:T(8,128)(2,1)S(1)}, u32[]{:S(2)}, u32[]{:S(2)}) collective-permute-start(bf16[56,2048]{1,0:T(8,128)(2,1)S(1)} %get-tuple-element.113), channel_id=1, source_target_pairs={{0,6},{1,7},{2,4},{3,5},{4,2},{5,3},{6,0},{7,1},{8,14},{9,15},{10,... | collective-permute-start | bytes 688136 | tf_op jit(solution)/shard_map/ppermute | solution.py:24
  181.8 26.7 %collective-permute-start.65 = (bf16[56,2048]{1,0:T(8,128)(2,1)S(1)}, bf16[56,2048]{1,0:T(8,128)(2,1)S(1)}, u32[]{:S(2)}, u32[]{:S(2)}) collective-permute-start(bf16[56,2048]{1,0:T(8,128)(2,1)S(1)} %get-tuple-element.114), channel_id=1, source_target_pairs={{0,7},{1,6},{2,5},{3,4},{4,3},{5,2},{6,1},{7,0},{8,15},{9,14},{10,... | collective-permute-start | bytes 688136 | tf_op jit(solution)/shard_map/ppermute | solution.py:24
  (61 other events, 555.4 us)
where the time goes:
time: 211 us; the launch traced here: 210 us
  waiting for transfers between devices  98 us (46%)
  starting transfers between devices  61.6 us (29%)
  Pallas kernels  27 us (13%)
  local copies, waits for them, and re-layouts  22.5 us (11%)
    ppermute x64, waiting for transfers between devices, flip(): return lax.ppermute(value, 'expert', [(i, i ^ mask) for i in range(size)])  81.8 us
    ppermute x64, starting transfers between devices, flip(): return lax.ppermute(value, 'expert', [(i, i ^ mask) for i in range(size)])  57 us
    pallas_call x11, Pallas kernels, call(): pl.pallas_call(body, in_specs=in_specs, out_specs=[VMEM] * len(outs), out...  27 us
    unnamed x58, local copies, waits for them, and re-layouts  18.8 us
    ppermute x1, waiting for transfers between devices, fetch_weights(): out_got = lax.ppermute(out_half, 'dp', source)  16.2 us
  transfers between devices with their start and end apart: 66, of which 23 were waited for; matrix products, arithmetic and copies ran while one was open for 3% of the time, Pallas kernels for 11%

commit v1 on v0

--- a/solution.py
+++ b/solution.py
@@ -36,17 +36,18 @@
     )(*operands)
 
 
-def gather_latents(own, size):
+def gather_latents(own, size, beside):
     pieces = {0: own}
     quarter = size // 4
     for mask in (2 * quarter, 3 * quarter, quarter):
         pieces[mask] = flip(own, mask, size)
+    pieces[3 * quarter], beside = lax.optimization_barrier((pieces[3 * quarter], beside))
     step = quarter // 2
     while step:
         for mask in list(pieces):
             pieces[mask ^ step] = flip(pieces[mask], step, size)
         step //= 2
-    return [pieces[m] for m in range(size)]
+    return [pieces[m] for m in range(size)], beside
 
 
 def fetch_weights(w_uv, w_out, core, size):
@@ -120,7 +121,20 @@
                 ]
 
 
-def routes(info, table, top, half, capacity):
+def pack(block, value, capacity):
+    lanes = block.shape[1]
+    for j in range(value.shape[1] // lanes):
+        block[j * capacity : (j + 1) * capacity, :] = value[:capacity, j * lanes : (j + 1) * lanes]
+
+
+def unpack(rows, at, column, block, capacity):
+    lanes = block.shape[1]
+    for j in range(block.shape[0] // capacity):
+        first = column + j * lanes
+        rows[at : at + capacity, first : first + lanes] = block[j * capacity : (j + 1) * capacity, :]
+
+
+def routes(info, table, top, half, pitch):
     rows = table.shape[0]
     table = table[...]
     names, gates = table[:, :top], table[:, top : 2 * top]
@@ -137,10 +151,10 @@
     c = lax.broadcasted_iota(i32, (rows, rows), 1)
     upto = jnp.where(c <= r, 1.0, 0.0).astype(bf16)
     rank = named * jnp.dot(upto, named.astype(bf16), preferred_element_type=f32)
-    wide = half * capacity
+    wide = half * pitch
     col = lax.broadcasted_iota(i32, (half, wide), 1)
-    start = lax.broadcasted_iota(i32, (half, wide), 0) * capacity
-    inside = (col >= start) & (col < start + capacity)
+    start = lax.broadcasted_iota(i32, (half, wide), 0) * pitch
+    inside = (col >= start) & (col < start + pitch)
     spread = jnp.where(inside, 1.0, 0.0).astype(bf16)
     slot = jnp.sum(jnp.where(inside, col - start + 1, 0), axis=0, keepdims=True).astype(f32)
     rank = jnp.dot(rank.astype(bf16), spread, preferred_element_type=f32)
@@ -149,17 +163,18 @@
     return jnp.where(place, 1.0, 0.0).astype(bf16), jnp.where(place, weight, 0.0).astype(bf16)
 
 
-def routes_body(half, capacity, top, info, near_table, far_table, near_place, near_mix, far_place, far_mix):
-    near_place[...], near_mix[...] = routes(info, near_table, top, half, capacity)
-    far_place[...], far_mix[...] = routes(info, far_table, top, half, capacity)
-
-
-def place_body(capacity, cuts, placing, *refs):
+def routes_body(half, quarter, pitch, top, info, *refs):
+    count = len(refs) // 3
+    for i, here in enumerate((half, quarter, half)):
+        refs[count + 2 * i][...], refs[count + 2 * i + 1][...] = routes(info, refs[i], top, here, pitch)
+
+
+def place_body(pitch, capacity, cuts, placing, *refs):
     across = (((0,), (0,)), ((), ()))
     rows = jnp.concatenate([r[...] for r in refs[:cuts]], axis=1)
     sent = lax.dot_general(placing[...], rows, across, preferred_element_type=f32).astype(bf16)
     for m, block in enumerate(refs[cuts:]):
-        block[...] = sent[m * capacity : (m + 1) * capacity]
+        pack(block, sent[m * pitch : (m + 1) * pitch], capacity)
 
 
 def norm_body(parts, seq_count, latent, *refs):
@@ -187,12 +202,11 @@
         chunk[...] = scaled[:, c * step : (c + 1) * step]
 
 
-def expert_body(half, capacity, cuts, *refs):
+def expert_body(count, pitch, capacity, cuts, *refs):
     gate_hbm, up_hbm, down_hbm = refs[:3]
-    count = half * cuts
-    taken = refs[3 : 3 + count]
-    given = refs[3 + count : 3 + 2 * count]
-    gate, up, down, rows, sems = refs[3 + 2 * count :]
+    taken = refs[3 : 3 + count * cuts]
+    given = refs[3 + count * cuts : -5]
+    gate, up, down, rows, sems = refs[-5:]
     step = rows.shape[1] // cuts
     copies = [
         pltpu.make_async_copy(source.at[0], target, sems.at[i])
@@ -201,8 +215,8 @@
     for copy in copies:
         copy.start()
     for c in range(cuts):
-        for m in range(half):
-            rows[pl.ds(m * capacity, capacity), pl.ds(c * step, step)] = taken[c * half + m][...]
+        for m in range(count):
+            unpack(rows, m * pitch, c * step, taken[c * count + m], capacity)
     across = (((1,), (1,)), ((), ()))
     copies[0].wait()
     gate_h = lax.dot_general(rows[...], gate[...], across, preferred_element_type=f32)
@@ -212,27 +226,33 @@
     copies[2].wait()
     for c in range(cuts):
         out = jnp.dot(act, down[:, c * step : (c + 1) * step], preferred_element_type=f32).astype(bf16)
-        for m in range(half):
-            given[c * half + m][...] = out[m * capacity : (m + 1) * capacity]
-
-
-def mix_body(half, capacity, mixing, *refs):
+        for m in range(count):
+            pack(given[c * count + m], out[m * pitch : (m + 1) * pitch], capacity)
+
+
+def mix_body(half, pitch, capacity, mixing, *refs):
     taken, out, rows = refs[:half], refs[half], refs[half + 1]
+    rows[...] = jnp.zeros(rows.shape, bf16)
     for m in range(half):
-        rows[pl.ds(m * capacity, capacity), :] = taken[m][...]
+        unpack(rows, m * pitch, 0, taken[m], capacity)
     out[...] = jnp.dot(mixing[...], rows[...], preferred_element_type=f32).astype(bf16)
 
 
-def last_body(half, capacity, cuts, local_len, seq_count, mixing, residual, *refs):
-    others, taken, out, rows = refs[:cuts], refs[cuts : cuts + half], refs[cuts + half], refs[cuts + half + 1]
+def near_mix_body(half, pitch, capacity, mixing, residual, *refs):
+    taken, total, rows = refs[:half], refs[half], refs[half + 1]
+    rows[...] = jnp.zeros(rows.shape, bf16)
     for m in range(half):
-        rows[pl.ds(m * capacity, capacity), :] = taken[m][...]
-    total = jnp.dot(mixing[...], rows[...], preferred_element_type=f32)
-    other = jnp.concatenate([o[...] for o in others], axis=1)
-    total = (residual[...] + total + other.astype(f32)).astype(bf16)
-    width = total.shape[1]
+        unpack(rows, m * pitch, 0, taken[m], capacity)
+    total[...] = residual[...] + jnp.dot(mixing[...], rows[...], preferred_element_type=f32)
+
+
+def last_body(local_len, seq_count, total, *refs):
+    others, out = refs[:-1], refs[-1]
+    other = jnp.concatenate([o[...] for o in others], axis=1).astype(f32)
+    done = (total[...] + other).astype(bf16)
+    width = done.shape[1]
     for s in range(seq_count):
-        out[:, s * width : (s + 1) * width] = total[s * local_len : (s + 1) * local_len]
+        out[:, s * width : (s + 1) * width] = done[s * local_len : (s + 1) * local_len]
 
 
 def layer(
@@ -260,22 +280,32 @@
     core = index & 1
     half = size // 2
     capacity = min(rows, rows * top // size + 2)
-    capacity = -(-capacity // 8) * 8
+    pitch = -(-capacity // 8) * 8
+    lanes = 128
     index_here = index % half
     owners = index - index_here + (index_here ^ jnp.arange(half, dtype=i32))
     info = jnp.concatenate([jnp.stack([index, core]).astype(i32), owners])
 
+    quarter = half // 2
     parts = fetch_weights(w_uv, w_out, core, size)
-    pieces = gather_latents(latents[0].reshape(local_len, seq_count * latent), size)
+    beside = (
+        queries[0].reshape(local_len, seq_count * heads * latent),
+        hidden[0].reshape(local_len, seq_count * width),
+        mem_latents[0].reshape(-1, seq_count * latent),
+    )
+    own_latents = latents[0].reshape(local_len, seq_count * latent)
+    pieces, (query_rows, hidden_rows, memory) = gather_latents(own_latents, size, beside)
     table = jnp.concatenate([ids[0].astype(f32), gates[0].astype(f32)], axis=2)
     table = jnp.transpose(table, (1, 0, 2)).reshape(rows, 2 * top)
     far_table = flip(table, half, size)
-    wide = half * capacity
-    near_placing, near_mix, far_placing, far_mix = call(
-        functools.partial(routes_body, half, capacity, top),
-        [SMEM, VMEM, VMEM],
-        [((rows, wide), bf16)] * 4,
-        [info, table, far_table],
+    side_table = flip(table, quarter, size)
+    wide = half * pitch
+    short = quarter * pitch
+    near_placing, near_mix, side_placing, _, far_placing, far_mix = call(
+        functools.partial(routes_body, half, quarter, pitch, top),
+        [SMEM] + [VMEM] * 3,
+        [((rows, wide), bf16)] * 2 + [((rows, short), bf16)] * 2 + [((rows, wide), bf16)] * 2,
+        [info, table, side_table, far_table],
         flops=4 * rows * rows * wide,
     )
 
@@ -288,8 +318,8 @@
         [
             info,
             lengths,
-            queries[0].reshape(local_len, seq_count * heads * latent),
-            mem_latents[0].reshape(-1, seq_count * latent),
+            query_rows,
+            memory,
             *pieces,
         ],
         flops=4 * rows * heads * latent * total_len,
@@ -304,7 +334,7 @@
         [
             head_order(core, w_uv.shape[0]),
             attended,
-            hidden[0].reshape(local_len, seq_count * width),
+            hidden_rows,
             norm_gain.reshape(1, width),
             *[w for part in parts for w in part],
         ],
@@ -312,40 +342,47 @@
     )
 
     def swap(blocks):
-        return [blocks[0]] + [flip(blocks[m], m, size) for m in range(1, half)]
+        return [blocks[0]] + [flip(blocks[m], m, size) for m in range(1, len(blocks))]
 
     def place(placing, chunks):
+        count = placing.shape[1] // pitch
+        sent = (capacity * sum(c.shape[1] for c in chunks) // lanes, lanes)
         return call(
-            functools.partial(place_body, capacity, len(chunks)),
+            functools.partial(place_body, pitch, capacity, len(chunks)),
             [VMEM] * (1 + len(chunks)),
-            [((capacity, sum(c.shape[1] for c in chunks)), bf16)] * half,
+            [(sent, bf16)] * count,
             [placing, *chunks],
             flops=2 * rows * width * wide,
         )
 
-    def experts(blocks):
+    def experts(blocks, column_cuts):
+        count = len(blocks) // column_cuts
         return call(
-            functools.partial(expert_body, half, capacity, len(blocks) // half),
+            functools.partial(expert_body, count, pitch, capacity, column_cuts),
             [ANY] * 3 + [VMEM] * len(blocks),
             [(b.shape, bf16) for b in blocks],
             [jnp.swapaxes(w_gate, 1, 2), jnp.swapaxes(w_up, 1, 2), w_down, *blocks],
             flops=6 * wide * width * w_gate.shape[2],
             scratch=[pltpu.VMEM(w_down.shape[1:], bf16)] * 3
-            + [pltpu.VMEM((wide, width), bf16), pltpu.SemaphoreType.DMA((3,))],
+            + [pltpu.VMEM((count * pitch, width), bf16), pltpu.SemaphoreType.DMA((3,))],
             limit=32,
         )
 
-    hops = [flip(chunk, half, size) for chunk in normed]
-    near_in = swap(place(near_placing, normed))
+    hops = [flip(normed[c], half, size) for c in range(cuts)]
+    sides = [flip(normed[c], quarter, size) for c in range(cuts)]
+    near_in = swap(place(near_placing[:, :short], normed))
+    near_in += swap(place(side_placing, sides))
     far_in = []
     for c in range(cuts):
         far_in += swap(place(far_placing, [hops[c]]))
-    near_out = swap(experts(near_in))
-    far_out = experts(far_in)
+    near_out = experts(near_in, 1)
+    near_back = [near_out[0]] + [flip(near_out[m], m, size) for m in range(1, quarter)]
+    near_back += [flip(near_out[m], m, size) for m in range(quarter, half)]
+    far_out = experts(far_in, cuts)
     others = []
     for c in range(cuts):
         (far_sum,) = call(
-            functools.partial(mix_body, half, capacity),
+            functools.partial(mix_body, half, pitch, capacity),
             [VMEM] * (1 + half),
             [((rows, step), bf16)],
             [far_mix, *swap(far_out[c * half : (c + 1) * half])],
@@ -353,13 +390,20 @@
             scratch=[pltpu.VMEM((wide, step), bf16)],
         )
         others.append(flip(far_sum, half, size))
-    (out,) = call(
-        functools.partial(last_body, half, capacity, cuts, local_len, seq_count),
-        [VMEM] * (2 + cuts + half),
-        [((local_len, seq_count * width), bf16)],
-        [near_mix, residual, *others, *near_out],
+    (total,) = call(
+        functools.partial(near_mix_body, half, pitch, capacity),
+        [VMEM] * (2 + half),
+        [((rows, width), f32)],
+        [near_mix, residual, *near_back],
         flops=2 * rows * width * wide,
         scratch=[pltpu.VMEM((wide, width), bf16)],
+    )
+    (out,) = call(
+        functools.partial(last_body, local_len, seq_count),
+        [VMEM] * (1 + cuts),
+        [((local_len, seq_count * width), bf16)],
+        [total, *others],
+        flops=8 * rows * width,
     )
     return out.reshape(1, local_len, seq_count, width)
 

time: 211 us -> 212 us (level)
  local copies, waits for them, and re-layouts: 22.5 us -> 16.8 us
  Pallas kernels: 27 us -> 30.1 us
  starting transfers between devices: 61.6 us -> 64.1 us
    unnamed x58 -> x54, local copies, waits for them, and re-layouts: 18.8 us -> 14 us
    pallas_call x11 -> x13, Pallas kernels: 27 us -> 30.1 us  [call(): pl.pallas_call(body, in_specs=in_specs, out_specs=[VMEM] * len(outs), out...]
    ppermute x64 -> x66, starting transfers between devices: 57 us -> 59.8 us  [flip(): return lax.ppermute(value, 'expert', [(i, i ^ mask) for i in range(size)])]
    ppermute x1, waiting for transfers between devices: 16.2 us -> 18.6 us  [fetch_weights(): out_got = lax.ppermute(out_half, 'dp', source)]
    ppermute x64 -> x66, waiting for transfers between devices: 81.8 us -> 81.2 us  [flip(): return lax.ppermute(value, 'expert', [(i, i ^ mask) for i in range(size)])]
  transfers between devices with their start and end apart: 66 -> 68, of which waited for: 23 -> 26; matrix products, arithmetic and copies ran while one was open for 3% -> 2% of each run, Pallas kernels for 11% -> 12%
where the time goes in v1:
time: 212 us
  waiting for transfers between devices  99.7 us (47%)
  starting transfers between devices  64.1 us (30%)
  Pallas kernels  30.1 us (14%)
  local copies, waits for them, and re-layouts  16.8 us (8%)
    ppermute x66, waiting for transfers between devices, flip(): return lax.ppermute(value, 'expert', [(i, i ^ mask) for i in range(size)])  81.2 us
    ppermute x66, starting transfers between devices, flip(): return lax.ppermute(value, 'expert', [(i, i ^ mask) for i in range(size)])  59.8 us
    pallas_call x13, Pallas kernels, call(): pl.pallas_call(body, in_specs=in_specs, out_specs=[VMEM] * len(outs), out...  30.1 us
    ppermute x1, waiting for transfers between devices, fetch_weights(): out_got = lax.ppermute(out_half, 'dp', source)  18.6 us
    unnamed x54, local copies, waits for them, and re-layouts  14 us
  transfers between devices with their start and end apart: 68, of which 26 were waited for; matrix products, arithmetic and copies ran while one was open for 2% of the time, Pallas kernels for 12%

profile of v1, /device:TPU:0, one launch (start us, length us, event | category | flops | bytes accessed | tf_op | source)
XLA Modules:
  0.0 211.9 jit_solution(8127768894051525597)
XLA Ops:
  1.5 3.0 %collective-permute-start.18 = (bf16[256,2048]{1,0:T(8,128)(2,1)S(1)}, bf16[256,2048]{1,0:T(8,128)(2,1)S(1)}, u32[]{:S(2)}, u32[]{:S(2)}) collective-permute-start(bf16[256,2048]{1,0:T(8,128)(2,1)S(1)} %constant_dynamic-slice_fusion), channel_id=1, source_target_pairs={{16,0},{0,16},{17,1},{1,17},{18,2},{2,18},{19,3},{3,19},{20,4},{4,... | collective-permute-start | bytes 3145736 | tf_op jit(solution)/shard_map/ppermute | solution.py:64
  5.4 3.7 %collective-permute-start.2 = (bf16[64,1024]{1,0:T(8,128)(2,1)S(1)}, bf16[64,1024]{1,0:T(8,128)(2,1)}, u32[]{:S(2)}, u32[]{:S(2)}) collective-permute-start(bf16[64,1024]{1,0:T(8,128)(2,1)S(1)} %bitcast.37), channel_id=1, source_target_pairs={{0,12},{1,13},{2,14},{3,15},{4,8},{5,9},{6,10},{7,11},{8,4},{9,5},... | collective-permute-start | bytes 393224 | tf_op jit(solution)/shard_map/ppermute | solution.py:24
  9.1 18.6 %collective-permute-done.18.refs_7_ = bf16[256,2048]{1,0:T(8,128)(2,1)S(1)} collective-permute-done((bf16[256,2048]{1,0:T(8,128)(2,1)S(1)}, bf16[256,2048]{1,0:T(8,128)(2,1)S(1)}, u32[]{:S(2)}, u32[]{:S(2)}) %collective-permute-start.18) | collective-permute-done | bytes 1048608 | tf_op jit(solution)/shard_map/ppermute | solution.py:64
  27.7 2.8 %collective-permute-start.10 = (bf16[64,1024]{1,0:T(8,128)(2,1)S(1)}, bf16[64,1024]{1,0:T(8,128)(2,1)}, u32[]{:S(2)}, u32[]{:S(2)}) collective-permute-start(bf16[64,1024]{1,0:T(8,128)(2,1)S(1)} %bitcast.38), channel_id=1, source_target_pairs={{0,8},{1,9},{2,10},{3,11},{4,12},{5,13},{6,14},{7,15},{8,0},{9,1},... | collective-permute-start | bytes 393224 | tf_op jit(solution)/shard_map/ppermute | solution.py:24
  35.1 2.7 %collective-permute-done.10.refs_12_ = bf16[64,1024]{1,0:T(8,128)(2,1)} collective-permute-done((bf16[64,1024]{1,0:T(8,128)(2,1)S(1)}, bf16[64,1024]{1,0:T(8,128)(2,1)}, u32[]{:S(2)}, u32[]{:S(2)}) %collective-permute-start.10) | collective-permute-done | bytes 131104 | tf_op jit(solution)/shard_map/ppermute | solution.py:24
  41.4 2.2 %collective-permute-done.15.refs_18_ = bf16[64,1024]{1,0:T(8,128)(2,1)} collective-permute-done((bf16[64,1024]{1,0:T(8,128)(2,1)}, bf16[64,1024]{1,0:T(8,128)(2,1)}, u32[]{:S(2)}, u32[]{:S(2)}) %collective-permute-start.15) | collective-permute-done | bytes 131104 | tf_op jit(solution)/shard_map/ppermute | solution.py:24
  46.4 2.3 %collective-permute-done.8.refs_10_ = bf16[64,1024]{1,0:T(8,128)(2,1)} collective-permute-done((bf16[64,1024]{1,0:T(8,128)(2,1)}, bf16[64,1024]{1,0:T(8,128)(2,1)}, u32[]{:S(2)}, u32[]{:S(2)}) %collective-permute-start.8) | collective-permute-done | bytes 131104 | tf_op jit(solution)/shard_map/ppermute | solution.py:24
  59.7 5.5 %shard_map.128.refs_1_ = bf16[128,4096]{1,0:T(8,128)(2,1)S(1)} custom-call(s32[10]{0:T(128)S(1)} %pad_add_fusion.info.refs_0_, s32[1,2]{1,0:T(1,128)S(1)} %copy-done.17, bf16[64,8192]{1,0:T(8,128)(2,1)S(1)} %bitcast.33, bf16[32,1024]{1,0:T(8,128)(2,1)S(1)} %bitcast.43, bf16[64,1024]{1,0:T(8,128)(2,1)S(1)} %bitcast.42, bf16[64,1024]{1,0:T(8,128)(2,1)S(1)} %copy-done.10, ...), custom_call_target="tpu_custom_call" | custom-call | flops 2214592512 | tf_op jit(solution)/shard_map/pallas_call | solution.py:28
  65.3 3.6 %shard_map.129 = (f32[128,2048]{1,0:T(8,128)S(1)}, bf16[128,1024]{1,0:T(8,128)(2,1)}, bf16[128,1024]{1,0:T(8,128)(2,1)}) custom-call(s32[8]{0:T(128)S(1)} %stack.43.refs_0_, bf16[128,4096]{1,0:T(8,128)(2,1)S(1)} %shard_map.128.refs_1_, bf16[64,4096]{1,0:T(8,128)(2,1)S(1)} %bitcast.32, bf16[1,2048]{1,0:T(2,128)(2,1)S(1)} %reshape.13.refs_3_, ...), custom_call_target="tpu_custom_call" | custom-call | flops 536870912 | tf_op jit(solution)/shard_map/pallas_call | solution.py:28
  69.0 2.9 %collective-permute-start.44 = (bf16[128,1024]{1,0:T(8,128)(2,1)}, bf16[128,1024]{1,0:T(8,128)(2,1)S(1)}, u32[]{:S(2)}, u32[]{:S(2)}) collective-permute-start(bf16[128,1024]{1,0:T(8,128)(2,1)} %get-tuple-element.73.refs_1_), channel_id=1, source_target_pairs={{0,8},{1,9},{2,10},{3,11},{4,12},{5,13},{6,14},{7,15},{8,0},{9,1},... | collective-permute-start | bytes 786440 | tf_op jit(solution)/shard_map/ppermute | solution.py:24
  73.5 2.9 %collective-permute-start.1 = (f32[128,12]{1,0:T(8,128)S(1)}, f32[128,12]{1,0:T(8,128)S(1)}, u32[]{:S(2)}, u32[]{:S(2)}) collective-permute-start(f32[128,12]{1,0:T(8,128)S(1)} %bitcast.35), channel_id=1, source_target_pairs={{0,8},{1,9},{2,10},{3,11},{4,12},{5,13},{6,14},{7,15},{8,0},{9,1},... | collective-permute-start | bytes 18440 | tf_op jit(solution)/shard_map/ppermute | solution.py:24
  76.4 6.6 %collective-permute-done.refs_1_ = f32[128,12]{1,0:T(8,128)S(1)} collective-permute-done((f32[128,12]{1,0:T(8,128)S(1)}, f32[128,12]{1,0:T(8,128)S(1)}, u32[]{:S(2)}, u32[]{:S(2)}) %collective-permute-start) | collective-permute-done | bytes 6176 | tf_op jit(solution)/shard_map/ppermute | solution.py:24
  83.0 15.3 %collective-permute-done.1.refs_2_ = f32[128,12]{1,0:T(8,128)S(1)} collective-permute-done((f32[128,12]{1,0:T(8,128)S(1)}, f32[128,12]{1,0:T(8,128)S(1)}, u32[]{:S(2)}, u32[]{:S(2)}) %collective-permute-start.1) | collective-permute-done | bytes 6176 | tf_op jit(solution)/shard_map/ppermute | solution.py:24
  98.3 2.1 %shard_map.127 = (bf16[128,448]{1,0:T(8,128)(2,1)S(1)}, bf16[128,448]{1,0:T(8,128)(2,1)S(1)}, bf16[128,224]{1,0:T(8,128)(2,1)S(1)}, bf16[128,224]{1,0:T(8,128)(2...) custom-call(s32[10]{0:T(128)S(1)} %pad_add_fusion.info.refs_0_, f32[128,12]{1,0:T(8,128)S(1)} %bitcast.36, ...), custom_call_target="tpu_custom_call" | custom-call | flops 29360128 | tf_op jit(solution)/shard_map/pallas_call | solution.py:28
  102.8 1.7 collective-permute-start.41
  111.5 2.3 %collective-permute-done.42.refs_9_ = bf16[400,128]{1,0:T(8,128)(2,1)S(1)} collective-permute-done((bf16[400,128]{1,0:T(8,128)(2,1)S(1)}, bf16[400,128]{1,0:T(8,128)(2,1)S(1)}, u32[]{:S(2)}, u32[]{:S(2)}) %collective-permute-start.42) | collective-permute-done | bytes 102432 | tf_op jit(solution)/shard_map/ppermute | solution.py:24
  115.1 1.8 collective-permute-start.50
  121.8 1.8 collective-permute-done.50.refs_17_
  126.7 1.8 copy-done.4
  128.5 1.8 copy-done.6
  130.3 6.8 %shard_map.136 = (bf16[400,128]{1,0:T(8,128)(2,1)S(1)}, bf16[400,128]{1,0:T(8,128)(2,1)S(1)}, bf16[400,128]{1,0:T(8,128)(2,1)S(1)}, bf16[400,128]{1,0:T(8,128)(2...) custom-call(bf16[1,704,2048]{2,1,0:T(8,128)(2,1)S(1)} %bitcast.44, ...), custom_call_target="tpu_custom_call" | custom-call | flops 3875536896 | tf_op jit(solution)/shard_map/pallas_call | solution.py:28
  139.1 1.7 collective-permute-start.64
  146.6 2.3 %collective-permute-done.65.refs_6_ = bf16[400,128]{1,0:T(8,128)(2,1)S(1)} collective-permute-done((bf16[400,128]{1,0:T(8,128)(2,1)S(1)}, bf16[400,128]{1,0:T(8,128)(2,1)S(1)}, u32[]{:S(2)}, u32[]{:S(2)}) %collective-permute-start.65) | collective-permute-done | bytes 102432 | tf_op jit(solution)/shard_map/ppermute | solution.py:24
  148.8 2.7 %collective-permute-done.66.refs_7_ = bf16[400,128]{1,0:T(8,128)(2,1)S(1)} collective-permute-done((bf16[400,128]{1,0:T(8,128)(2,1)S(1)}, bf16[400,128]{1,0:T(8,128)(2,1)S(1)}, u32[]{:S(2)}, u32[]{:S(2)}) %collective-permute-start.66) | collective-permute-done | bytes 102432 | tf_op jit(solution)/shard_map/ppermute | solution.py:24
  155.3 4.3 %collective-permute-done.28.refs_10_ = bf16[800,128]{1,0:T(8,128)(2,1)S(1)} collective-permute-done((bf16[800,128]{1,0:T(8,128)(2,1)S(1)}, bf16[800,128]{1,0:T(8,128)(2,1)S(1)}, u32[]{:S(2)}, u32[]{:S(2)}) %collective-permute-start.28) | collective-permute-done | bytes 204832 | tf_op jit(solution)/shard_map/ppermute | solution.py:24
  160.2 7.0 %shard_map.132 = (bf16[800,128]{1,0:T(8,128)(2,1)S(1)}, bf16[800,128]{1,0:T(8,128)(2,1)S(1)}, bf16[800,128]{1,0:T(8,128)(2,1)S(1)}, bf16[800,128]{1,0:T(8,128)(2...) custom-call(bf16[1,704,2048]{2,1,0:T(8,128)(2,1)S(1)} %bitcast.45, ...), custom_call_target="tpu_custom_call" | custom-call | flops 3875536896 | tf_op jit(solution)/shard_map/pallas_call | solution.py:28
  169.2 1.9 collective-permute-start.32
  172.2 6.7 %collective-permute-done.58.refs_7_ = bf16[400,128]{1,0:T(8,128)(2,1)S(1)} collective-permute-done((bf16[400,128]{1,0:T(8,128)(2,1)S(1)}, bf16[400,128]{1,0:T(8,128)(2,1)S(1)}, u32[]{:S(2)}, u32[]{:S(2)}) %collective-permute-start.58) | collective-permute-done | bytes 102432 | tf_op jit(solution)/shard_map/ppermute | solution.py:24
  184.9 1.7 collective-permute-start.35
  186.6 10.5 %collective-permute-done.33.refs_5_ = bf16[800,128]{1,0:T(8,128)(2,1)S(1)} collective-permute-done((bf16[800,128]{1,0:T(8,128)(2,1)S(1)}, bf16[800,128]{1,0:T(8,128)(2,1)S(1)}, u32[]{:S(2)}, u32[]{:S(2)}) %collective-permute-start.33) | collective-permute-done | bytes 204832 | tf_op jit(solution)/shard_map/ppermute | solution.py:24
  197.1 4.4 %collective-permute-done.34.refs_6_ = bf16[800,128]{1,0:T(8,128)(2,1)S(1)} collective-permute-done((bf16[800,128]{1,0:T(8,128)(2,1)S(1)}, bf16[800,128]{1,0:T(8,128)(2,1)S(1)}, u32[]{:S(2)}, u32[]{:S(2)}) %collective-permute-start.34) | collective-permute-done | bytes 204832 | tf_op jit(solution)/shard_map/ppermute | solution.py:24
  201.5 8.1 %collective-permute-done.35.refs_7_ = bf16[800,128]{1,0:T(8,128)(2,1)S(1)} collective-permute-done((bf16[800,128]{1,0:T(8,128)(2,1)S(1)}, bf16[800,128]{1,0:T(8,128)(2,1)S(1)}, u32[]{:S(2)}, u32[]{:S(2)}) %collective-permute-start.35) | collective-permute-done | bytes 204832 | tf_op jit(solution)/shard_map/ppermute | solution.py:24
  (183 shorter events, 67.8 us)
Async XLA Ops:
  1.5 26.2 %collective-permute-start.18 = (bf16[256,2048]{1,0:T(8,128)(2,1)S(1)}, bf16[256,2048]{1,0:T(8,128)(2,1)S(1)}, u32[]{:S(2)}, u32[]{:S(2)}) collective-permute-start(bf16[256,2048]{1,0:T(8,128)(2,1)S(1)} %constant_dynamic-slice_fusion), channel_id=1, source_target_pairs={{16,0},{0,16},{17,1},{1,17},{18,2},{2,18},{19,3},{3,19},{20,4},{4,... | collective-permute-start | bytes 3145736 | tf_op jit(solution)/shard_map/ppermute | solution.py:64
  5.4 28.2 %collective-permute-start.2 = (bf16[64,1024]{1,0:T(8,128)(2,1)S(1)}, bf16[64,1024]{1,0:T(8,128)(2,1)}, u32[]{:S(2)}, u32[]{:S(2)}) collective-permute-start(bf16[64,1024]{1,0:T(8,128)(2,1)S(1)} %bitcast.37), channel_id=1, source_target_pairs={{0,12},{1,13},{2,14},{3,15},{4,8},{5,9},{6,10},{7,11},{8,4},{9,5},... | collective-permute-start | bytes 393224 | tf_op jit(solution)/shard_map/ppermute | solution.py:24
  27.7 37.6 %collective-permute-start.20 = (bf16[256,2048]{1,0:T(8,128)(2,1)S(1)}, bf16[256,2048]{1,0:T(8,128)(2,1)}, u32[]{:S(2)}, u32[]{:S(2)}) collective-permute-start(bf16[256,2048]{1,0:T(8,128)(2,1)S(1)} %collective-permute-done.18.refs_7_), channel_id=1, source_target_pairs={{0,1},{1,0},{2,3},{3,2},{4,5},{5,4},{6,7},{7,6},{8,9},{9,8},{10,11... | collective-permute-start | bytes 3145736 | tf_op jit(solution)/shard_map/ppermute | solution.py:24
  27.7 10.0 %collective-permute-start.10 = (bf16[64,1024]{1,0:T(8,128)(2,1)S(1)}, bf16[64,1024]{1,0:T(8,128)(2,1)}, u32[]{:S(2)}, u32[]{:S(2)}) collective-permute-start(bf16[64,1024]{1,0:T(8,128)(2,1)S(1)} %bitcast.38), channel_id=1, source_target_pairs={{0,8},{1,9},{2,10},{3,11},{4,12},{5,13},{6,14},{7,15},{8,0},{9,1},... | collective-permute-start | bytes 393224 | tf_op jit(solution)/shard_map/ppermute | solution.py:24
  52.4 12.9 %collective-permute-start.19 = (bf16[2,512,128]{2,1,0:T(8,128)(2,1)S(1)}, bf16[2,512,128]{2,1,0:T(8,128)(2,1)}, u32[]{:S(2)}, u32[]{:S(2)}) collective-permute-start(bf16[2,512,128]{2,1,0:T(8,128)(2,1)S(1)} %collective-permute-done.17.refs_6_), channel_id=1, source_target_pairs={{0,1},{1,0},{2,3},{3,2},{4,5},{5,4},{6,7},{7,6},{8,9},{9,8},{10,11... | collective-permute-start | bytes 786440 | tf_op jit(solution)/shard_map/ppermute | solution.py:24
  68.9 31.5 %collective-permute-start.36 = (bf16[128,1024]{1,0:T(8,128)(2,1)}, bf16[128,1024]{1,0:T(8,128)(2,1)S(1)}, u32[]{:S(2)}, u32[]{:S(2)}) collective-permute-start(bf16[128,1024]{1,0:T(8,128)(2,1)} %get-tuple-element.72.refs_0_), channel_id=1, source_target_pairs={{0,8},{1,9},{2,10},{3,11},{4,12},{5,13},{6,14},{7,15},{8,0},{9,1},... | collective-permute-start | bytes 786440 | tf_op jit(solution)/shard_map/ppermute | solution.py:24
  69.0 33.8 %collective-permute-start.44 = (bf16[128,1024]{1,0:T(8,128)(2,1)}, bf16[128,1024]{1,0:T(8,128)(2,1)S(1)}, u32[]{:S(2)}, u32[]{:S(2)}) collective-permute-start(bf16[128,1024]{1,0:T(8,128)(2,1)} %get-tuple-element.73.refs_1_), channel_id=1, source_target_pairs={{0,8},{1,9},{2,10},{3,11},{4,12},{5,13},{6,14},{7,15},{8,0},{9,1},... | collective-permute-start | bytes 786440 | tf_op jit(solution)/shard_map/ppermute | solution.py:24
  72.0 11.0 %collective-permute-start = (f32[128,12]{1,0:T(8,128)S(1)}, f32[128,12]{1,0:T(8,128)S(1)}, u32[]{:S(2)}, u32[]{:S(2)}) collective-permute-start(f32[128,12]{1,0:T(8,128)S(1)} %bitcast.34), channel_id=1, source_target_pairs={{0,4},{1,5},{2,6},{3,7},{4,0},{5,1},{6,2},{7,3},{8,12},{9,13},{10,... | collective-permute-start | bytes 18440 | tf_op jit(solution)/shard_map/ppermute | solution.py:24
  73.5 24.8 %collective-permute-start.1 = (f32[128,12]{1,0:T(8,128)S(1)}, f32[128,12]{1,0:T(8,128)S(1)}, u32[]{:S(2)}, u32[]{:S(2)}) collective-permute-start(f32[128,12]{1,0:T(8,128)S(1)} %bitcast.35), channel_id=1, source_target_pairs={{0,8},{1,9},{2,10},{3,11},{4,12},{5,13},{6,14},{7,15},{8,0},{9,1},... | collective-permute-start | bytes 18440 | tf_op jit(solution)/shard_map/ppermute | solution.py:24
  109.9 9.8 %collective-permute-start.47 = (bf16[400,128]{1,0:T(8,128)(2,1)S(1)}, bf16[400,128]{1,0:T(8,128)(2,1)S(1)}, u32[]{:S(2)}, u32[]{:S(2)}) collective-permute-start(bf16[400,128]{1,0:T(8,128)(2,1)S(1)} %get-tuple-element.104), channel_id=1, source_target_pairs={{0,3},{1,2},{2,1},{3,0},{4,7},{5,6},{6,5},{7,4},{8,11},{9,10},{10,... | collective-permute-start | bytes 307208 | tf_op jit(solution)/shard_map/ppermute | solution.py:24
  119.7 19.4 %collective-permute-start.24 = (bf16[128,1024]{1,0:T(8,128)(2,1)}, bf16[128,1024]{1,0:T(8,128)(2,1)S(1)}, u32[]{:S(2)}, u32[]{:S(2)}) collective-permute-start(bf16[128,1024]{1,0:T(8,128)(2,1)} %get-tuple-element.72.refs_0_), channel_id=1, source_target_pairs={{0,4},{1,5},{2,6},{3,7},{4,0},{5,1},{6,2},{7,3},{8,12},{9,13},{10,... | collective-permute-start | bytes 786440 | tf_op jit(solution)/shard_map/ppermute | solution.py:24
  120.8 18.3 %collective-permute-start.25 = (bf16[128,1024]{1,0:T(8,128)(2,1)}, bf16[128,1024]{1,0:T(8,128)(2,1)S(1)}, u32[]{:S(2)}, u32[]{:S(2)}) collective-permute-start(bf16[128,1024]{1,0:T(8,128)(2,1)} %get-tuple-element.73.refs_1_), channel_id=1, source_target_pairs={{0,4},{1,5},{2,6},{3,7},{4,0},{5,1},{6,2},{7,3},{8,12},{9,13},{10,... | collective-permute-start | bytes 786440 | tf_op jit(solution)/shard_map/ppermute | solution.py:24
  121.8 15.3 %collective-permute-start.21 = (bf16[800,128]{1,0:T(8,128)(2,1)S(1)}, bf16[800,128]{1,0:T(8,128)(2,1)S(1)}, u32[]{:S(2)}, u32[]{:S(2)}) collective-permute-start(bf16[800,128]{1,0:T(8,128)(2,1)S(1)} %get-tuple-element.75), channel_id=1, source_target_pairs={{0,1},{1,0},{2,3},{3,2},{4,5},{5,4},{6,7},{7,6},{8,9},{9,8},{10,11... | collective-permute-start | bytes 614408 | tf_op jit(solution)/shard_map/ppermute | solution.py:24
  123.7 13.6 %collective-permute-start.22 = (bf16[800,128]{1,0:T(8,128)(2,1)S(1)}, bf16[800,128]{1,0:T(8,128)(2,1)S(1)}, u32[]{:S(2)}, u32[]{:S(2)}) collective-permute-start(bf16[800,128]{1,0:T(8,128)(2,1)S(1)} %get-tuple-element.76), channel_id=1, source_target_pairs={{0,2},{1,3},{2,0},{3,1},{4,6},{5,7},{6,4},{7,5},{8,10},{9,11},{10,... | collective-permute-start | bytes 614408 | tf_op jit(solution)/shard_map/ppermute | solution.py:24
  125.1 12.9 %collective-permute-start.23 = (bf16[800,128]{1,0:T(8,128)(2,1)S(1)}, bf16[800,128]{1,0:T(8,128)(2,1)S(1)}, u32[]{:S(2)}, u32[]{:S(2)}) collective-permute-start(bf16[800,128]{1,0:T(8,128)(2,1)S(1)} %get-tuple-element.77), channel_id=1, source_target_pairs={{0,3},{1,2},{2,1},{3,0},{4,7},{5,6},{6,5},{7,4},{8,11},{9,10},{10,... | collective-permute-start | bytes 614408 | tf_op jit(solution)/shard_map/ppermute | solution.py:24
  143.1 10.5 %collective-permute-start.26 = (bf16[800,128]{1,0:T(8,128)(2,1)S(1)}, bf16[800,128]{1,0:T(8,128)(2,1)S(1)}, u32[]{:S(2)}, u32[]{:S(2)}) collective-permute-start(bf16[800,128]{1,0:T(8,128)(2,1)S(1)} %get-tuple-element.80), channel_id=1, source_target_pairs={{0,1},{1,0},{2,3},{3,2},{4,5},{5,4},{6,7},{7,6},{8,9},{9,8},{10,11... | collective-permute-start | bytes 614408 | tf_op jit(solution)/shard_map/ppermute | solution.py:24
  144.2 11.1 %collective-permute-start.27 = (bf16[800,128]{1,0:T(8,128)(2,1)S(1)}, bf16[800,128]{1,0:T(8,128)(2,1)S(1)}, u32[]{:S(2)}, u32[]{:S(2)}) collective-permute-start(bf16[800,128]{1,0:T(8,128)(2,1)S(1)} %get-tuple-element.81), channel_id=1, source_target_pairs={{0,2},{1,3},{2,0},{3,1},{4,6},{5,7},{6,4},{7,5},{8,10},{9,11},{10,... | collective-permute-start | bytes 614408 | tf_op jit(solution)/shard_map/ppermute | solution.py:24
  144.9 14.8 %collective-permute-start.28 = (bf16[800,128]{1,0:T(8,128)(2,1)S(1)}, bf16[800,128]{1,0:T(8,128)(2,1)S(1)}, u32[]{:S(2)}, u32[]{:S(2)}) collective-permute-start(bf16[800,128]{1,0:T(8,128)(2,1)S(1)} %get-tuple-element.82), channel_id=1, source_target_pairs={{0,3},{1,2},{2,1},{3,0},{4,7},{5,6},{6,5},{7,4},{8,11},{9,10},{10,... | collective-permute-start | bytes 614408 | tf_op jit(solution)/shard_map/ppermute | solution.py:24
  151.5 15.7 %collective-permute-start.53 = (bf16[400,128]{1,0:T(8,128)(2,1)S(1)}, bf16[400,128]{1,0:T(8,128)(2,1)S(1)}, u32[]{:S(2)}, u32[]{:S(2)}) collective-permute-start(bf16[400,128]{1,0:T(8,128)(2,1)S(1)} %get-tuple-element.111), channel_id=1, source_target_pairs={{0,2},{1,3},{2,0},{3,1},{4,6},{5,7},{6,4},{7,5},{8,10},{9,11},{10,... | collective-permute-start | bytes 307208 | tf_op jit(solution)/shard_map/ppermute | solution.py:24
  152.2 15.6 %collective-permute-start.54 = (bf16[400,128]{1,0:T(8,128)(2,1)S(1)}, bf16[400,128]{1,0:T(8,128)(2,1)S(1)}, u32[]{:S(2)}, u32[]{:S(2)}) collective-permute-start(bf16[400,128]{1,0:T(8,128)(2,1)S(1)} %get-tuple-element.112), channel_id=1, source_target_pairs={{0,3},{1,2},{2,1},{3,0},{4,7},{5,6},{6,5},{7,4},{8,11},{9,10},{10,... | collective-permute-start | bytes 307208 | tf_op jit(solution)/shard_map/ppermute | solution.py:24
  153.6 15.1 %collective-permute-start.55 = (bf16[400,128]{1,0:T(8,128)(2,1)S(1)}, bf16[400,128]{1,0:T(8,128)(2,1)S(1)}, u32[]{:S(2)}, u32[]{:S(2)}) collective-permute-start(bf16[400,128]{1,0:T(8,128)(2,1)S(1)} %get-tuple-element.113), channel_id=1, source_target_pairs={{0,4},{1,5},{2,6},{3,7},{4,0},{5,1},{6,2},{7,3},{8,12},{9,13},{10,... | collective-permute-start | bytes 307208 | tf_op jit(solution)/shard_map/ppermute | solution.py:24
  155.3 13.9 %collective-permute-start.56 = (bf16[400,128]{1,0:T(8,128)(2,1)S(1)}, bf16[400,128]{1,0:T(8,128)(2,1)S(1)}, u32[]{:S(2)}, u32[]{:S(2)}) collective-permute-start(bf16[400,128]{1,0:T(8,128)(2,1)S(1)} %get-tuple-element.114), channel_id=1, source_target_pairs={{0,5},{1,4},{2,7},{3,6},{4,1},{5,0},{6,3},{7,2},{8,13},{9,12},{10,... | collective-permute-start | bytes 307208 | tf_op jit(solution)/shard_map/ppermute | solution.py:24
  159.7 11.5 %collective-permute-start.57 = (bf16[400,128]{1,0:T(8,128)(2,1)S(1)}, bf16[400,128]{1,0:T(8,128)(2,1)S(1)}, u32[]{:S(2)}, u32[]{:S(2)}) collective-permute-start(bf16[400,128]{1,0:T(8,128)(2,1)S(1)} %get-tuple-element.115), channel_id=1, source_target_pairs={{0,6},{1,7},{2,4},{3,5},{4,2},{5,3},{6,0},{7,1},{8,14},{9,15},{10,... | collective-permute-start | bytes 307208 | tf_op jit(solution)/shard_map/ppermute | solution.py:24
  167.3 13.6 %collective-permute-start.29 = (bf16[800,128]{1,0:T(8,128)(2,1)S(1)}, bf16[800,128]{1,0:T(8,128)(2,1)S(1)}, u32[]{:S(2)}, u32[]{:S(2)}) collective-permute-start(bf16[800,128]{1,0:T(8,128)(2,1)S(1)} %get-tuple-element.84), channel_id=1, source_target_pairs={{0,1},{1,0},{2,3},{3,2},{4,5},{5,4},{6,7},{7,6},{8,9},{9,8},{10,11... | collective-permute-start | bytes 614408 | tf_op jit(solution)/shard_map/ppermute | solution.py:24
  167.8 14.7 %collective-permute-start.30 = (bf16[800,128]{1,0:T(8,128)(2,1)S(1)}, bf16[800,128]{1,0:T(8,128)(2,1)S(1)}, u32[]{:S(2)}, u32[]{:S(2)}) collective-permute-start(bf16[800,128]{1,0:T(8,128)(2,1)S(1)} %get-tuple-element.85), channel_id=1, source_target_pairs={{0,2},{1,3},{2,0},{3,1},{4,6},{5,7},{6,4},{7,5},{8,10},{9,11},{10,... | collective-permute-start | bytes 614408 | tf_op jit(solution)/shard_map/ppermute | solution.py:24
  168.7 15.0 %collective-permute-start.31 = (bf16[800,128]{1,0:T(8,128)(2,1)S(1)}, bf16[800,128]{1,0:T(8,128)(2,1)S(1)}, u32[]{:S(2)}, u32[]{:S(2)}) collective-permute-start(bf16[800,128]{1,0:T(8,128)(2,1)S(1)} %get-tuple-element.86), channel_id=1, source_target_pairs={{0,3},{1,2},{2,1},{3,0},{4,7},{5,6},{6,5},{7,4},{8,11},{9,10},{10,... | collective-permute-start | bytes 614408 | tf_op jit(solution)/shard_map/ppermute | solution.py:24
  169.2 15.6 %collective-permute-start.32 = (bf16[800,128]{1,0:T(8,128)(2,1)S(1)}, bf16[800,128]{1,0:T(8,128)(2,1)S(1)}, u32[]{:S(2)}, u32[]{:S(2)}) collective-permute-start(bf16[800,128]{1,0:T(8,128)(2,1)S(1)} %get-tuple-element.87), channel_id=1, source_target_pairs={{0,4},{1,5},{2,6},{3,7},{4,0},{5,1},{6,2},{7,3},{8,12},{9,13},{10,... | collective-permute-start | bytes 614408 | tf_op jit(solution)/shard_map/ppermute | solution.py:24
  178.9 31.7 %collective-permute-start.67 = (bf16[128,1024]{1,0:T(8,128)(2,1)S(1)}, bf16[128,1024]{1,0:T(8,128)(2,1)S(1)}, u32[]{:S(2)}, u32[]{:S(2)}) collective-permute-start(bf16[128,1024]{1,0:T(8,128)(2,1)S(1)} %shard_map.138), channel_id=1, source_target_pairs={{0,8},{1,9},{2,10},{3,11},{4,12},{5,13},{6,14},{7,15},{8,0},{9,1},... | collective-permute-start | bytes 786440 | tf_op jit(solution)/shard_map/ppermute | solution.py:24
  180.9 29.7 %collective-permute-start.59 = (bf16[128,1024]{1,0:T(8,128)(2,1)S(1)}, bf16[128,1024]{1,0:T(8,128)(2,1)S(1)}, u32[]{:S(2)}, u32[]{:S(2)}) collective-permute-start(bf16[128,1024]{1,0:T(8,128)(2,1)S(1)} %shard_map.137), channel_id=1, source_target_pairs={{0,8},{1,9},{2,10},{3,11},{4,12},{5,13},{6,14},{7,15},{8,0},{9,1},... | collective-permute-start | bytes 786440 | tf_op jit(solution)/shard_map/ppermute | solution.py:24
  182.5 14.6 %collective-permute-start.33 = (bf16[800,128]{1,0:T(8,128)(2,1)S(1)}, bf16[800,128]{1,0:T(8,128)(2,1)S(1)}, u32[]{:S(2)}, u32[]{:S(2)}) collective-permute-start(bf16[800,128]{1,0:T(8,128)(2,1)S(1)} %get-tuple-element.88), channel_id=1, source_target_pairs={{0,5},{1,4},{2,7},{3,6},{4,1},{5,0},{6,3},{7,2},{8,13},{9,12},{10,... | collective-permute-start | bytes 614408 | tf_op jit(solution)/shard_map/ppermute | solution.py:24
  183.7 17.8 %collective-permute-start.34 = (bf16[800,128]{1,0:T(8,128)(2,1)S(1)}, bf16[800,128]{1,0:T(8,128)(2,1)S(1)}, u32[]{:S(2)}, u32[]{:S(2)}) collective-permute-start(bf16[800,128]{1,0:T(8,128)(2,1)S(1)} %get-tuple-element.89), channel_id=1, source_target_pairs={{0,6},{1,7},{2,4},{3,5},{4,2},{5,3},{6,0},{7,1},{8,14},{9,15},{10,... | collective-permute-start | bytes 614408 | tf_op jit(solution)/shard_map/ppermute | solution.py:24
  184.9 24.7 %collective-permute-start.35 = (bf16[800,128]{1,0:T(8,128)(2,1)S(1)}, bf16[800,128]{1,0:T(8,128)(2,1)S(1)}, u32[]{:S(2)}, u32[]{:S(2)}) collective-permute-start(bf16[800,128]{1,0:T(8,128)(2,1)S(1)} %get-tuple-element.90), channel_id=1, source_target_pairs={{0,7},{1,6},{2,5},{3,4},{4,3},{5,2},{6,1},{7,0},{8,15},{9,14},{10,... | collective-permute-start | bytes 614408 | tf_op jit(solution)/shard_map/ppermute | solution.py:24
  (61 other events, 590.9 us)

commit v2 on v1

--- a/solution.py
+++ b/solution.py
@@ -163,10 +163,11 @@
     return jnp.where(place, 1.0, 0.0).astype(bf16), jnp.where(place, weight, 0.0).astype(bf16)
 
 
-def routes_body(half, quarter, pitch, top, info, *refs):
-    count = len(refs) // 3
-    for i, here in enumerate((half, quarter, half)):
-        refs[count + 2 * i][...], refs[count + 2 * i + 1][...] = routes(info, refs[i], top, here, pitch)
+def routes_body(half, quarter, pitch, top, info, own, side, far, own_place, near_mix, side_place, far_place, far_mix):
+    placing, near_mix[...] = routes(info, own, top, half, pitch)
+    own_place[...] = placing[:, : quarter * pitch]
+    side_place[...], _ = routes(info, side, top, quarter, pitch)
+    far_place[...], far_mix[...] = routes(info, far, top, half, pitch)
 
 
 def place_body(pitch, capacity, cuts, placing, *refs):
@@ -202,30 +203,20 @@
         chunk[...] = scaled[:, c * step : (c + 1) * step]
 
 
-def expert_body(count, pitch, capacity, cuts, *refs):
-    gate_hbm, up_hbm, down_hbm = refs[:3]
-    taken = refs[3 : 3 + count * cuts]
-    given = refs[3 + count * cuts : -5]
-    gate, up, down, rows, sems = refs[-5:]
+def expert_body(count, pitch, capacity, cuts, gate, up, down, *refs):
+    taken = refs[: count * cuts]
+    given = refs[count * cuts : -1]
+    rows = refs[-1]
     step = rows.shape[1] // cuts
-    copies = [
-        pltpu.make_async_copy(source.at[0], target, sems.at[i])
-        for i, (source, target) in enumerate(((gate_hbm, gate), (up_hbm, up), (down_hbm, down)))
-    ]
-    for copy in copies:
-        copy.start()
     for c in range(cuts):
         for m in range(count):
             unpack(rows, m * pitch, c * step, taken[c * count + m], capacity)
     across = (((1,), (1,)), ((), ()))
-    copies[0].wait()
-    gate_h = lax.dot_general(rows[...], gate[...], across, preferred_element_type=f32)
-    copies[1].wait()
-    up_h = lax.dot_general(rows[...], up[...], across, preferred_element_type=f32)
+    gate_h = lax.dot_general(rows[...], gate[0], across, preferred_element_type=f32)
+    up_h = lax.dot_general(rows[...], up[0], across, preferred_element_type=f32)
     act = (gate_h / (1.0 + jnp.exp(-gate_h)) * up_h).astype(bf16)
-    copies[2].wait()
     for c in range(cuts):
-        out = jnp.dot(act, down[:, c * step : (c + 1) * step], preferred_element_type=f32).astype(bf16)
+        out = jnp.dot(act, down[0, :, c * step : (c + 1) * step], preferred_element_type=f32).astype(bf16)
         for m in range(count):
             pack(given[c * count + m], out[m * pitch : (m + 1) * pitch], capacity)
 
@@ -301,10 +292,10 @@
     side_table = flip(table, quarter, size)
     wide = half * pitch
     short = quarter * pitch
-    near_placing, near_mix, side_placing, _, far_placing, far_mix = call(
+    own_placing, near_mix, side_placing, far_placing, far_mix = call(
         functools.partial(routes_body, half, quarter, pitch, top),
         [SMEM] + [VMEM] * 3,
-        [((rows, wide), bf16)] * 2 + [((rows, short), bf16)] * 2 + [((rows, wide), bf16)] * 2,
+        [((rows, short), bf16), ((rows, wide), bf16), ((rows, short), bf16)] + [((rows, wide), bf16)] * 2,
         [info, table, side_table, far_table],
         flops=4 * rows * rows * wide,
     )
@@ -359,33 +350,33 @@
         count = len(blocks) // column_cuts
         return call(
             functools.partial(expert_body, count, pitch, capacity, column_cuts),
-            [ANY] * 3 + [VMEM] * len(blocks),
+            [VMEM] * (3 + len(blocks)),
             [(b.shape, bf16) for b in blocks],
             [jnp.swapaxes(w_gate, 1, 2), jnp.swapaxes(w_up, 1, 2), w_down, *blocks],
             flops=6 * wide * width * w_gate.shape[2],
-            scratch=[pltpu.VMEM(w_down.shape[1:], bf16)] * 3
-            + [pltpu.VMEM((count * pitch, width), bf16), pltpu.SemaphoreType.DMA((3,))],
-            limit=32,
+            scratch=[pltpu.VMEM((count * pitch, width), bf16)],
         )
 
     hops = [flip(normed[c], half, size) for c in range(cuts)]
     sides = [flip(normed[c], quarter, size) for c in range(cuts)]
-    near_in = swap(place(near_placing[:, :short], normed))
-    near_in += swap(place(side_placing, sides))
-    far_in = []
-    for c in range(cuts):
-        far_in += swap(place(far_placing, [hops[c]]))
-    near_out = experts(near_in, 1)
-    near_back = [near_out[0]] + [flip(near_out[m], m, size) for m in range(1, quarter)]
-    near_back += [flip(near_out[m], m, size) for m in range(quarter, half)]
-    far_out = experts(far_in, cuts)
+    own_in = swap(place(own_placing, normed))
+    side_in = swap(place(side_placing, sides))
+    far_in = [swap(place(far_placing, [hops[c]])) for c in range(cuts)]
+    own_out = experts(own_in, 1)
+    side_out = experts(side_in, 1)
+    near_back = [own_out[0]] + [flip(own_out[m], m, size) for m in range(1, quarter)]
+    near_back += [flip(side_out[m], m + quarter, size) for m in range(quarter)]
+    far_out = experts([b for chunk in far_in for b in chunk], cuts)
     others = []
     for c in range(cuts):
+        sent = far_out[c * half : (c + 1) * half]
+        got = [sent[0]] + [flip(sent[m], m, size) for m in range(1, quarter)]
+        got += [flip(sent[m], m, size) for m in range(quarter, half)]
         (far_sum,) = call(
             functools.partial(mix_body, half, pitch, capacity),
             [VMEM] * (1 + half),
             [((rows, step), bf16)],
-            [far_mix, *swap(far_out[c * half : (c + 1) * half])],
+            [far_mix, *got],
             flops=2 * rows * step * wide,
             scratch=[pltpu.VMEM((wide, step), bf16)],
         )

time: 212 us -> 211 us (level)
  Pallas kernels: 30.1 us -> 25.6 us
    pallas_call x13 -> x14, Pallas kernels: 30.1 us -> 25.6 us  [call(): pl.pallas_call(body, in_specs=in_specs, out_specs=[VMEM] * len(outs), out...]
  transfers between devices with their start and end apart: 68 -> 68, of which waited for: 26 -> 27; matrix products, arithmetic and copies ran while one was open for 2% -> 2% of each run, Pallas kernels for 12% -> 10%
where the time goes in v2:
time: 211 us
  waiting for transfers between devices  101 us (48%)
  starting transfers between devices  65 us (31%)
  Pallas kernels  25.6 us (12%)
  local copies, waits for them, and re-layouts  18.6 us (9%)
    ppermute x66, waiting for transfers between devices, flip(): return lax.ppermute(value, 'expert', [(i, i ^ mask) for i in range(size)])  82.1 us
    ppermute x66, starting transfers between devices, flip(): return lax.ppermute(value, 'expert', [(i, i ^ mask) for i in range(size)])  60.7 us
    pallas_call x14, Pallas kernels, call(): pl.pallas_call(body, in_specs=in_specs, out_specs=[VMEM] * len(outs), out...  25.6 us
    ppermute x1, waiting for transfers between devices, fetch_weights(): out_got = lax.ppermute(out_half, 'dp', source)  18.6 us
    unnamed x54, local copies, waits for them, and re-layouts  15.7 us
  transfers between devices with their start and end apart: 68, of which 27 were waited for; matrix products, arithmetic and copies ran while one was open for 2% of the time, Pallas kernels for 10%

profile of v2, /device:TPU:0, one launch (start us, length us, event | category | flops | bytes accessed | tf_op | source)
XLA Modules:
  0.0 211.0 jit_solution(8348994733226724678)
XLA Ops:
  1.5 3.0 %collective-permute-start.18 = (bf16[256,2048]{1,0:T(8,128)(2,1)S(1)}, bf16[256,2048]{1,0:T(8,128)(2,1)S(1)}, u32[]{:S(2)}, u32[]{:S(2)}) collective-permute-start(bf16[256,2048]{1,0:T(8,128)(2,1)S(1)} %constant_dynamic-slice_fusion), channel_id=1, source_target_pairs={{16,0},{0,16},{17,1},{1,17},{18,2},{2,18},{19,3},{3,19},{20,4},{4,... | collective-permute-start | bytes 3145736 | tf_op jit(solution)/shard_map/ppermute | solution.py:64
  5.4 3.7 %collective-permute-start.2 = (bf16[64,1024]{1,0:T(8,128)(2,1)S(1)}, bf16[64,1024]{1,0:T(8,128)(2,1)}, u32[]{:S(2)}, u32[]{:S(2)}) collective-permute-start(bf16[64,1024]{1,0:T(8,128)(2,1)S(1)} %bitcast.37), channel_id=1, source_target_pairs={{0,12},{1,13},{2,14},{3,15},{4,8},{5,9},{6,10},{7,11},{8,4},{9,5},... | collective-permute-start | bytes 393224 | tf_op jit(solution)/shard_map/ppermute | solution.py:24
  9.1 18.6 %collective-permute-done.18.refs_7_ = bf16[256,2048]{1,0:T(8,128)(2,1)S(1)} collective-permute-done((bf16[256,2048]{1,0:T(8,128)(2,1)S(1)}, bf16[256,2048]{1,0:T(8,128)(2,1)S(1)}, u32[]{:S(2)}, u32[]{:S(2)}) %collective-permute-start.18) | collective-permute-done | bytes 1048608 | tf_op jit(solution)/shard_map/ppermute | solution.py:64
  27.7 2.8 %collective-permute-start.10 = (bf16[64,1024]{1,0:T(8,128)(2,1)S(1)}, bf16[64,1024]{1,0:T(8,128)(2,1)}, u32[]{:S(2)}, u32[]{:S(2)}) collective-permute-start(bf16[64,1024]{1,0:T(8,128)(2,1)S(1)} %bitcast.38), channel_id=1, source_target_pairs={{0,8},{1,9},{2,10},{3,11},{4,12},{5,13},{6,14},{7,15},{8,0},{9,1},... | collective-permute-start | bytes 393224 | tf_op jit(solution)/shard_map/ppermute | solution.py:24
  35.0 2.7 %collective-permute-done.10.refs_12_ = bf16[64,1024]{1,0:T(8,128)(2,1)} collective-permute-done((bf16[64,1024]{1,0:T(8,128)(2,1)S(1)}, bf16[64,1024]{1,0:T(8,128)(2,1)}, u32[]{:S(2)}, u32[]{:S(2)}) %collective-permute-start.10) | collective-permute-done | bytes 131104 | tf_op jit(solution)/shard_map/ppermute | solution.py:24
  41.4 2.2 %collective-permute-done.15.refs_18_ = bf16[64,1024]{1,0:T(8,128)(2,1)} collective-permute-done((bf16[64,1024]{1,0:T(8,128)(2,1)}, bf16[64,1024]{1,0:T(8,128)(2,1)}, u32[]{:S(2)}, u32[]{:S(2)}) %collective-permute-start.15) | collective-permute-done | bytes 131104 | tf_op jit(solution)/shard_map/ppermute | solution.py:24
  46.4 2.3 %collective-permute-done.8.refs_10_ = bf16[64,1024]{1,0:T(8,128)(2,1)} collective-permute-done((bf16[64,1024]{1,0:T(8,128)(2,1)}, bf16[64,1024]{1,0:T(8,128)(2,1)}, u32[]{:S(2)}, u32[]{:S(2)}) %collective-permute-start.8) | collective-permute-done | bytes 131104 | tf_op jit(solution)/shard_map/ppermute | solution.py:24
  59.7 5.5 %shard_map.128.refs_1_ = bf16[128,4096]{1,0:T(8,128)(2,1)S(1)} custom-call(s32[10]{0:T(128)S(1)} %pad_add_fusion.info.refs_0_, s32[1,2]{1,0:T(1,128)S(1)} %copy-done.17, bf16[64,8192]{1,0:T(8,128)(2,1)S(1)} %bitcast.33, bf16[32,1024]{1,0:T(8,128)(2,1)S(1)} %bitcast.43, bf16[64,1024]{1,0:T(8,128)(2,1)S(1)} %bitcast.42, bf16[64,1024]{1,0:T(8,128)(2,1)S(1)} %copy-done.10, ...), custom_call_target="tpu_custom_call" | custom-call | flops 2214592512 | tf_op jit(solution)/shard_map/pallas_call | solution.py:28
  65.3 3.6 %shard_map.129 = (f32[128,2048]{1,0:T(8,128)S(1)}, bf16[128,1024]{1,0:T(8,128)(2,1)}, bf16[128,1024]{1,0:T(8,128)(2,1)}) custom-call(s32[8]{0:T(128)S(1)} %stack.43.refs_0_, bf16[128,4096]{1,0:T(8,128)(2,1)S(1)} %shard_map.128.refs_1_, bf16[64,4096]{1,0:T(8,128)(2,1)S(1)} %bitcast.32, bf16[1,2048]{1,0:T(2,128)(2,1)S(1)} %reshape.13.refs_3_, ...), custom_call_target="tpu_custom_call" | custom-call | flops 536870912 | tf_op jit(solution)/shard_map/pallas_call | solution.py:28
  69.0 2.9 %collective-permute-start.44 = (bf16[128,1024]{1,0:T(8,128)(2,1)}, bf16[128,1024]{1,0:T(8,128)(2,1)S(1)}, u32[]{:S(2)}, u32[]{:S(2)}) collective-permute-start(bf16[128,1024]{1,0:T(8,128)(2,1)} %get-tuple-element.73.refs_1_), channel_id=1, source_target_pairs={{0,8},{1,9},{2,10},{3,11},{4,12},{5,13},{6,14},{7,15},{8,0},{9,1},... | collective-permute-start | bytes 786440 | tf_op jit(solution)/shard_map/ppermute | solution.py:24
  73.4 2.9 %collective-permute-start.1 = (f32[128,12]{1,0:T(8,128)S(1)}, f32[128,12]{1,0:T(8,128)S(1)}, u32[]{:S(2)}, u32[]{:S(2)}) collective-permute-start(f32[128,12]{1,0:T(8,128)S(1)} %bitcast.35), channel_id=1, source_target_pairs={{0,8},{1,9},{2,10},{3,11},{4,12},{5,13},{6,14},{7,15},{8,0},{9,1},... | collective-permute-start | bytes 18440 | tf_op jit(solution)/shard_map/ppermute | solution.py:24
  76.3 6.6 %collective-permute-done.side = f32[128,12]{1,0:T(8,128)S(1)} collective-permute-done((f32[128,12]{1,0:T(8,128)S(1)}, f32[128,12]{1,0:T(8,128)S(1)}, u32[]{:S(2)}, u32[]{:S(2)}) %collective-permute-start) | collective-permute-done | bytes 6176 | tf_op jit(solution)/shard_map/ppermute | solution.py:24
  82.9 15.3 %collective-permute-done.1.far = f32[128,12]{1,0:T(8,128)S(1)} collective-permute-done((f32[128,12]{1,0:T(8,128)S(1)}, f32[128,12]{1,0:T(8,128)S(1)}, u32[]{:S(2)}, u32[]{:S(2)}) %collective-permute-start.1) | collective-permute-done | bytes 6176 | tf_op jit(solution)/shard_map/ppermute | solution.py:24
  111.0 2.3 %collective-permute-done.42.refs_6_ = bf16[400,128]{1,0:T(8,128)(2,1)S(1)} collective-permute-done((bf16[400,128]{1,0:T(8,128)(2,1)S(1)}, bf16[400,128]{1,0:T(8,128)(2,1)S(1)}, u32[]{:S(2)}, u32[]{:S(2)}) %collective-permute-start.42) | collective-permute-done | bytes 102432 | tf_op jit(solution)/shard_map/ppermute | solution.py:24
  114.6 1.8 collective-permute-start.50
  121.2 1.8 collective-permute-done.50.refs_14_
  126.1 1.8 copy-done.3
  127.9 1.8 copy-done.5
  129.7 1.8 copy-done.6
  131.6 4.7 %shard_map.137 = (bf16[400,128]{1,0:T(8,128)(2,1)S(1)}, bf16[400,128]{1,0:T(8,128)(2,1)S(1)}, bf16[400,128]{1,0:T(8,128)(2,1)S(1)}, bf16[400,128]{1,0:T(8,128)(2...) custom-call(bf16[1,704,2048]{2,1,0:T(8,128)(2,1)S(1)} %bitcast.44, ...), custom_call_target="tpu_custom_call" | custom-call | flops 3875536896 | tf_op jit(solution)/shard_map/pallas_call | solution.py:28
  138.3 1.7 collective-permute-start.64
  140.4 1.8 collective-permute-done.61.refs_2_
  146.2 2.3 %collective-permute-done.65.refs_6_ = bf16[400,128]{1,0:T(8,128)(2,1)S(1)} collective-permute-done((bf16[400,128]{1,0:T(8,128)(2,1)S(1)}, bf16[400,128]{1,0:T(8,128)(2,1)S(1)}, u32[]{:S(2)}, u32[]{:S(2)}) %collective-permute-start.65) | collective-permute-done | bytes 102432 | tf_op jit(solution)/shard_map/ppermute | solution.py:24
  150.9 2.6 %shard_map.131 = (bf16[800,128]{1,0:T(8,128)(2,1)S(1)}, bf16[800,128]{1,0:T(8,128)(2,1)S(1)}, bf16[800,128]{1,0:T(8,128)(2,1)S(1)}, bf16[800,128]{1,0:T(8,128)(2,1)S(1)}) custom-call(bf16[1,704,2048]{2,1,0:T(8,128)(2,1)S(1)} %bitcast.45, bf16[1,704,2048]{2,1,0:T(8,128)(2,1)S(1)} %bitcast.48, bf16[1,704,2048]{2,1,0:T(8,128)(2,1)S(1)} %copy-done.6, ...), custom_call_target="tpu_custom_call" | custom-call | flops 3875536896 | tf_op jit(solution)/shard_map/pallas_call | solution.py:28
  153.8 7.2 %collective-permute-done.53.refs_2_ = bf16[400,128]{1,0:T(8,128)(2,1)S(1)} collective-permute-done((bf16[400,128]{1,0:T(8,128)(2,1)S(1)}, bf16[400,128]{1,0:T(8,128)(2,1)S(1)}, u32[]{:S(2)}, u32[]{:S(2)}) %collective-permute-start.53) | collective-permute-done | bytes 102432 | tf_op jit(solution)/shard_map/ppermute | solution.py:24
  164.3 2.6 %shard_map.133 = (bf16[800,128]{1,0:T(8,128)(2,1)S(1)}, bf16[800,128]{1,0:T(8,128)(2,1)S(1)}, bf16[800,128]{1,0:T(8,128)(2,1)S(1)}, bf16[800,128]{1,0:T(8,128)(2,1)S(1)}) custom-call(bf16[1,704,2048]{2,1,0:T(8,128)(2,1)S(1)} %bitcast.46, bf16[1,704,2048]{2,1,0:T(8,128)(2,1)S(1)} %bitcast.49, bf16[1,704,2048]{2,1,0:T(8,128)(2,1)S(1)} %copy-done.6, ...), custom_call_target="tpu_custom_call" | custom-call | flops 3875536896 | tf_op jit(solution)/shard_map/pallas_call | solution.py:28
  170.0 1.9 collective-permute-done.57.refs_6_
  172.7 6.2 %collective-permute-done.58.refs_7_ = bf16[400,128]{1,0:T(8,128)(2,1)S(1)} collective-permute-done((bf16[400,128]{1,0:T(8,128)(2,1)S(1)}, bf16[400,128]{1,0:T(8,128)(2,1)S(1)}, u32[]{:S(2)}, u32[]{:S(2)}) %collective-permute-start.58) | collective-permute-done | bytes 102432 | tf_op jit(solution)/shard_map/ppermute | solution.py:24
  184.4 2.2 %collective-permute-start.35 = (bf16[800,128]{1,0:T(8,128)(2,1)S(1)}, bf16[800,128]{1,0:T(8,128)(2,1)S(1)}, u32[]{:S(2)}, u32[]{:S(2)}) collective-permute-start(bf16[800,128]{1,0:T(8,128)(2,1)S(1)} %get-tuple-element.90), channel_id=1, source_target_pairs={{0,7},{1,6},{2,5},{3,4},{4,3},{5,2},{6,1},{7,0},{8,15},{9,14},{10,... | collective-permute-start | bytes 614408 | tf_op jit(solution)/shard_map/ppermute | solution.py:24
  186.7 10.5 %collective-permute-done.33.refs_5_ = bf16[800,128]{1,0:T(8,128)(2,1)S(1)} collective-permute-done((bf16[800,128]{1,0:T(8,128)(2,1)S(1)}, bf16[800,128]{1,0:T(8,128)(2,1)S(1)}, u32[]{:S(2)}, u32[]{:S(2)}) %collective-permute-start.33) | collective-permute-done | bytes 204832 | tf_op jit(solution)/shard_map/ppermute | solution.py:24
  197.2 4.4 %collective-permute-done.34.refs_6_ = bf16[800,128]{1,0:T(8,128)(2,1)S(1)} collective-permute-done((bf16[800,128]{1,0:T(8,128)(2,1)S(1)}, bf16[800,128]{1,0:T(8,128)(2,1)S(1)}, u32[]{:S(2)}, u32[]{:S(2)}) %collective-permute-start.34) | collective-permute-done | bytes 204832 | tf_op jit(solution)/shard_map/ppermute | solution.py:24
  201.6 7.1 %collective-permute-done.35.refs_7_ = bf16[800,128]{1,0:T(8,128)(2,1)S(1)} collective-permute-done((bf16[800,128]{1,0:T(8,128)(2,1)S(1)}, bf16[800,128]{1,0:T(8,128)(2,1)S(1)}, u32[]{:S(2)}, u32[]{:S(2)}) %collective-permute-start.35) | collective-permute-done | bytes 204832 | tf_op jit(solution)/shard_map/ppermute | solution.py:24
  (183 shorter events, 71.8 us)
Async XLA Ops:
  1.5 26.2 %collective-permute-start.18 = (bf16[256,2048]{1,0:T(8,128)(2,1)S(1)}, bf16[256,2048]{1,0:T(8,128)(2,1)S(1)}, u32[]{:S(2)}, u32[]{:S(2)}) collective-permute-start(bf16[256,2048]{1,0:T(8,128)(2,1)S(1)} %constant_dynamic-slice_fusion), channel_id=1, source_target_pairs={{16,0},{0,16},{17,1},{1,17},{18,2},{2,18},{19,3},{3,19},{20,4},{4,... | collective-permute-start | bytes 3145736 | tf_op jit(solution)/shard_map/ppermute | solution.py:64
  5.4 28.2 %collective-permute-start.2 = (bf16[64,1024]{1,0:T(8,128)(2,1)S(1)}, bf16[64,1024]{1,0:T(8,128)(2,1)}, u32[]{:S(2)}, u32[]{:S(2)}) collective-permute-start(bf16[64,1024]{1,0:T(8,128)(2,1)S(1)} %bitcast.37), channel_id=1, source_target_pairs={{0,12},{1,13},{2,14},{3,15},{4,8},{5,9},{6,10},{7,11},{8,4},{9,5},... | collective-permute-start | bytes 393224 | tf_op jit(solution)/shard_map/ppermute | solution.py:24
  27.7 37.6 %collective-permute-start.20 = (bf16[256,2048]{1,0:T(8,128)(2,1)S(1)}, bf16[256,2048]{1,0:T(8,128)(2,1)}, u32[]{:S(2)}, u32[]{:S(2)}) collective-permute-start(bf16[256,2048]{1,0:T(8,128)(2,1)S(1)} %collective-permute-done.18.refs_7_), channel_id=1, source_target_pairs={{0,1},{1,0},{2,3},{3,2},{4,5},{5,4},{6,7},{7,6},{8,9},{9,8},{10,11... | collective-permute-start | bytes 3145736 | tf_op jit(solution)/shard_map/ppermute | solution.py:24
  27.7 10.0 %collective-permute-start.10 = (bf16[64,1024]{1,0:T(8,128)(2,1)S(1)}, bf16[64,1024]{1,0:T(8,128)(2,1)}, u32[]{:S(2)}, u32[]{:S(2)}) collective-permute-start(bf16[64,1024]{1,0:T(8,128)(2,1)S(1)} %bitcast.38), channel_id=1, source_target_pairs={{0,8},{1,9},{2,10},{3,11},{4,12},{5,13},{6,14},{7,15},{8,0},{9,1},... | collective-permute-start | bytes 393224 | tf_op jit(solution)/shard_map/ppermute | solution.py:24
  30.5 8.8 %collective-permute-start.6 = (bf16[64,1024]{1,0:T(8,128)(2,1)S(1)}, bf16[64,1024]{1,0:T(8,128)(2,1)}, u32[]{:S(2)}, u32[]{:S(2)}) collective-permute-start(bf16[64,1024]{1,0:T(8,128)(2,1)S(1)} %bitcast.39), channel_id=1, source_target_pairs={{0,4},{1,5},{2,6},{3,7},{4,0},{5,1},{6,2},{7,3},{8,12},{9,13},{10,... | collective-permute-start | bytes 393224 | tf_op jit(solution)/shard_map/ppermute | solution.py:24
  39.8 9.0 %collective-permute-start.8 = (bf16[64,1024]{1,0:T(8,128)(2,1)}, bf16[64,1024]{1,0:T(8,128)(2,1)}, u32[]{:S(2)}, u32[]{:S(2)}) collective-permute-start(bf16[64,1024]{1,0:T(8,128)(2,1)} %collective-permute-done.6.refs_8_), channel_id=1, source_target_pairs={{0,2},{1,3},{2,0},{3,1},{4,6},{5,7},{6,4},{7,5},{8,10},{9,11},{10,... | collective-permute-start | bytes 393224 | tf_op jit(solution)/shard_map/ppermute | solution.py:24
  52.4 12.9 %collective-permute-start.19 = (bf16[2,512,128]{2,1,0:T(8,128)(2,1)S(1)}, bf16[2,512,128]{2,1,0:T(8,128)(2,1)}, u32[]{:S(2)}, u32[]{:S(2)}) collective-permute-start(bf16[2,512,128]{2,1,0:T(8,128)(2,1)S(1)} %collective-permute-done.17.refs_6_), channel_id=1, source_target_pairs={{0,1},{1,0},{2,3},{3,2},{4,5},{5,4},{6,7},{7,6},{8,9},{9,8},{10,11... | collective-permute-start | bytes 786440 | tf_op jit(solution)/shard_map/ppermute | solution.py:24
  68.9 30.9 %collective-permute-start.36 = (bf16[128,1024]{1,0:T(8,128)(2,1)}, bf16[128,1024]{1,0:T(8,128)(2,1)S(1)}, u32[]{:S(2)}, u32[]{:S(2)}) collective-permute-start(bf16[128,1024]{1,0:T(8,128)(2,1)} %get-tuple-element.72.refs_0_), channel_id=1, source_target_pairs={{0,8},{1,9},{2,10},{3,11},{4,12},{5,13},{6,14},{7,15},{8,0},{9,1},... | collective-permute-start | bytes 786440 | tf_op jit(solution)/shard_map/ppermute | solution.py:24
  69.0 33.2 %collective-permute-start.44 = (bf16[128,1024]{1,0:T(8,128)(2,1)}, bf16[128,1024]{1,0:T(8,128)(2,1)S(1)}, u32[]{:S(2)}, u32[]{:S(2)}) collective-permute-start(bf16[128,1024]{1,0:T(8,128)(2,1)} %get-tuple-element.73.refs_1_), channel_id=1, source_target_pairs={{0,8},{1,9},{2,10},{3,11},{4,12},{5,13},{6,14},{7,15},{8,0},{9,1},... | collective-permute-start | bytes 786440 | tf_op jit(solution)/shard_map/ppermute | solution.py:24
  71.9 11.0 %collective-permute-start = (f32[128,12]{1,0:T(8,128)S(1)}, f32[128,12]{1,0:T(8,128)S(1)}, u32[]{:S(2)}, u32[]{:S(2)}) collective-permute-start(f32[128,12]{1,0:T(8,128)S(1)} %bitcast.34), channel_id=1, source_target_pairs={{0,4},{1,5},{2,6},{3,7},{4,0},{5,1},{6,2},{7,3},{8,12},{9,13},{10,... | collective-permute-start | bytes 18440 | tf_op jit(solution)/shard_map/ppermute | solution.py:24
  73.4 24.8 %collective-permute-start.1 = (f32[128,12]{1,0:T(8,128)S(1)}, f32[128,12]{1,0:T(8,128)S(1)}, u32[]{:S(2)}, u32[]{:S(2)}) collective-permute-start(f32[128,12]{1,0:T(8,128)S(1)} %bitcast.35), channel_id=1, source_target_pairs={{0,8},{1,9},{2,10},{3,11},{4,12},{5,13},{6,14},{7,15},{8,0},{9,1},... | collective-permute-start | bytes 18440 | tf_op jit(solution)/shard_map/ppermute | solution.py:24
  104.3 8.9 %collective-permute-start.42 = (bf16[400,128]{1,0:T(8,128)(2,1)S(1)}, bf16[400,128]{1,0:T(8,128)(2,1)S(1)}, u32[]{:S(2)}, u32[]{:S(2)}) collective-permute-start(bf16[400,128]{1,0:T(8,128)(2,1)S(1)} %get-tuple-element.99), channel_id=1, source_target_pairs={{0,6},{1,7},{2,4},{3,5},{4,2},{5,3},{6,0},{7,1},{8,14},{9,15},{10,... | collective-permute-start | bytes 307208 | tf_op jit(solution)/shard_map/ppermute | solution.py:24
  107.9 9.1 %collective-permute-start.46 = (bf16[400,128]{1,0:T(8,128)(2,1)S(1)}, bf16[400,128]{1,0:T(8,128)(2,1)S(1)}, u32[]{:S(2)}, u32[]{:S(2)}) collective-permute-start(bf16[400,128]{1,0:T(8,128)(2,1)S(1)} %get-tuple-element.103), channel_id=1, source_target_pairs={{0,2},{1,3},{2,0},{3,1},{4,6},{5,7},{6,4},{7,5},{8,10},{9,11},{10,... | collective-permute-start | bytes 307208 | tf_op jit(solution)/shard_map/ppermute | solution.py:24
  109.3 9.8 %collective-permute-start.47 = (bf16[400,128]{1,0:T(8,128)(2,1)S(1)}, bf16[400,128]{1,0:T(8,128)(2,1)S(1)}, u32[]{:S(2)}, u32[]{:S(2)}) collective-permute-start(bf16[400,128]{1,0:T(8,128)(2,1)S(1)} %get-tuple-element.104), channel_id=1, source_target_pairs={{0,3},{1,2},{2,1},{3,0},{4,7},{5,6},{6,5},{7,4},{8,11},{9,10},{10,... | collective-permute-start | bytes 307208 | tf_op jit(solution)/shard_map/ppermute | solution.py:24
  119.1 19.1 %collective-permute-start.27 = (bf16[128,1024]{1,0:T(8,128)(2,1)}, bf16[128,1024]{1,0:T(8,128)(2,1)S(1)}, u32[]{:S(2)}, u32[]{:S(2)}) collective-permute-start(bf16[128,1024]{1,0:T(8,128)(2,1)} %get-tuple-element.72.refs_0_), channel_id=1, source_target_pairs={{0,4},{1,5},{2,6},{3,7},{4,0},{5,1},{6,2},{7,3},{8,12},{9,13},{10,... | collective-permute-start | bytes 786440 | tf_op jit(solution)/shard_map/ppermute | solution.py:24
  120.2 18.1 %collective-permute-start.28 = (bf16[128,1024]{1,0:T(8,128)(2,1)}, bf16[128,1024]{1,0:T(8,128)(2,1)S(1)}, u32[]{:S(2)}, u32[]{:S(2)}) collective-permute-start(bf16[128,1024]{1,0:T(8,128)(2,1)} %get-tuple-element.73.refs_1_), channel_id=1, source_target_pairs={{0,4},{1,5},{2,6},{3,7},{4,0},{5,1},{6,2},{7,3},{8,12},{9,13},{10,... | collective-permute-start | bytes 786440 | tf_op jit(solution)/shard_map/ppermute | solution.py:24
  121.2 15.1 %collective-permute-start.21 = (bf16[800,128]{1,0:T(8,128)(2,1)S(1)}, bf16[800,128]{1,0:T(8,128)(2,1)S(1)}, u32[]{:S(2)}, u32[]{:S(2)}) collective-permute-start(bf16[800,128]{1,0:T(8,128)(2,1)S(1)} %get-tuple-element.75), channel_id=1, source_target_pairs={{0,1},{1,0},{2,3},{3,2},{4,5},{5,4},{6,7},{7,6},{8,9},{9,8},{10,11... | collective-permute-start | bytes 614408 | tf_op jit(solution)/shard_map/ppermute | solution.py:24
  123.1 13.3 %collective-permute-start.22 = (bf16[800,128]{1,0:T(8,128)(2,1)S(1)}, bf16[800,128]{1,0:T(8,128)(2,1)S(1)}, u32[]{:S(2)}, u32[]{:S(2)}) collective-permute-start(bf16[800,128]{1,0:T(8,128)(2,1)S(1)} %get-tuple-element.76), channel_id=1, source_target_pairs={{0,2},{1,3},{2,0},{3,1},{4,6},{5,7},{6,4},{7,5},{8,10},{9,11},{10,... | collective-permute-start | bytes 614408 | tf_op jit(solution)/shard_map/ppermute | solution.py:24
  124.5 12.6 %collective-permute-start.23 = (bf16[800,128]{1,0:T(8,128)(2,1)S(1)}, bf16[800,128]{1,0:T(8,128)(2,1)S(1)}, u32[]{:S(2)}, u32[]{:S(2)}) collective-permute-start(bf16[800,128]{1,0:T(8,128)(2,1)S(1)} %get-tuple-element.77), channel_id=1, source_target_pairs={{0,3},{1,2},{2,1},{3,0},{4,7},{5,6},{6,5},{7,4},{8,11},{9,10},{10,... | collective-permute-start | bytes 614408 | tf_op jit(solution)/shard_map/ppermute | solution.py:24
  143.3 18.3 %collective-permute-start.29 = (bf16[800,128]{1,0:T(8,128)(2,1)S(1)}, bf16[800,128]{1,0:T(8,128)(2,1)S(1)}, u32[]{:S(2)}, u32[]{:S(2)}) collective-permute-start(bf16[800,128]{1,0:T(8,128)(2,1)S(1)} %get-tuple-element.84), channel_id=1, source_target_pairs={{0,1},{1,0},{2,3},{3,2},{4,5},{5,4},{6,7},{7,6},{8,9},{9,8},{10,11... | collective-permute-start | bytes 614408 | tf_op jit(solution)/shard_map/ppermute | solution.py:24
  144.0 18.3 %collective-permute-start.30 = (bf16[800,128]{1,0:T(8,128)(2,1)S(1)}, bf16[800,128]{1,0:T(8,128)(2,1)S(1)}, u32[]{:S(2)}, u32[]{:S(2)}) collective-permute-start(bf16[800,128]{1,0:T(8,128)(2,1)S(1)} %get-tuple-element.85), channel_id=1, source_target_pairs={{0,2},{1,3},{2,0},{3,1},{4,6},{5,7},{6,4},{7,5},{8,10},{9,11},{10,... | collective-permute-start | bytes 614408 | tf_op jit(solution)/shard_map/ppermute | solution.py:24
  145.0 18.7 %collective-permute-start.31 = (bf16[800,128]{1,0:T(8,128)(2,1)S(1)}, bf16[800,128]{1,0:T(8,128)(2,1)S(1)}, u32[]{:S(2)}, u32[]{:S(2)}) collective-permute-start(bf16[800,128]{1,0:T(8,128)(2,1)S(1)} %get-tuple-element.86), channel_id=1, source_target_pairs={{0,3},{1,2},{2,1},{3,0},{4,7},{5,6},{6,5},{7,4},{8,11},{9,10},{10,... | collective-permute-start | bytes 614408 | tf_op jit(solution)/shard_map/ppermute | solution.py:24
  149.5 11.5 %collective-permute-start.53 = (bf16[400,128]{1,0:T(8,128)(2,1)S(1)}, bf16[400,128]{1,0:T(8,128)(2,1)S(1)}, u32[]{:S(2)}, u32[]{:S(2)}) collective-permute-start(bf16[400,128]{1,0:T(8,128)(2,1)S(1)} %get-tuple-element.111), channel_id=1, source_target_pairs={{0,2},{1,3},{2,0},{3,1},{4,6},{5,7},{6,4},{7,5},{8,10},{9,11},{10,... | collective-permute-start | bytes 307208 | tf_op jit(solution)/shard_map/ppermute | solution.py:24
  153.6 27.4 %collective-permute-start.24 = (bf16[800,128]{1,0:T(8,128)(2,1)S(1)}, bf16[800,128]{1,0:T(8,128)(2,1)S(1)}, u32[]{:S(2)}, u32[]{:S(2)}) collective-permute-start(bf16[800,128]{1,0:T(8,128)(2,1)S(1)} %get-tuple-element.79), channel_id=1, source_target_pairs={{0,1},{1,0},{2,3},{3,2},{4,5},{5,4},{6,7},{7,6},{8,9},{9,8},{10,11... | collective-permute-start | bytes 614408 | tf_op jit(solution)/shard_map/ppermute | solution.py:24
  166.9 15.6 %collective-permute-start.25 = (bf16[800,128]{1,0:T(8,128)(2,1)S(1)}, bf16[800,128]{1,0:T(8,128)(2,1)S(1)}, u32[]{:S(2)}, u32[]{:S(2)}) collective-permute-start(bf16[800,128]{1,0:T(8,128)(2,1)S(1)} %get-tuple-element.80), channel_id=1, source_target_pairs={{0,2},{1,3},{2,0},{3,1},{4,6},{5,7},{6,4},{7,5},{8,10},{9,11},{10,... | collective-permute-start | bytes 614408 | tf_op jit(solution)/shard_map/ppermute | solution.py:24
  168.3 15.1 %collective-permute-start.26 = (bf16[800,128]{1,0:T(8,128)(2,1)S(1)}, bf16[800,128]{1,0:T(8,128)(2,1)S(1)}, u32[]{:S(2)}, u32[]{:S(2)}) collective-permute-start(bf16[800,128]{1,0:T(8,128)(2,1)S(1)} %get-tuple-element.81), channel_id=1, source_target_pairs={{0,3},{1,2},{2,1},{3,0},{4,7},{5,6},{6,5},{7,4},{8,11},{9,10},{10,... | collective-permute-start | bytes 614408 | tf_op jit(solution)/shard_map/ppermute | solution.py:24
  169.0 15.4 %collective-permute-start.32 = (bf16[800,128]{1,0:T(8,128)(2,1)S(1)}, bf16[800,128]{1,0:T(8,128)(2,1)S(1)}, u32[]{:S(2)}, u32[]{:S(2)}) collective-permute-start(bf16[800,128]{1,0:T(8,128)(2,1)S(1)} %get-tuple-element.87), channel_id=1, source_target_pairs={{0,4},{1,5},{2,6},{3,7},{4,0},{5,1},{6,2},{7,3},{8,12},{9,13},{10,... | collective-permute-start | bytes 614408 | tf_op jit(solution)/shard_map/ppermute | solution.py:24
  179.0 30.7 %collective-permute-start.67 = (bf16[128,1024]{1,0:T(8,128)(2,1)S(1)}, bf16[128,1024]{1,0:T(8,128)(2,1)S(1)}, u32[]{:S(2)}, u32[]{:S(2)}) collective-permute-start(bf16[128,1024]{1,0:T(8,128)(2,1)S(1)} %shard_map.139), channel_id=1, source_target_pairs={{0,8},{1,9},{2,10},{3,11},{4,12},{5,13},{6,14},{7,15},{8,0},{9,1},... | collective-permute-start | bytes 786440 | tf_op jit(solution)/shard_map/ppermute | solution.py:24
  181.0 28.7 %collective-permute-start.59 = (bf16[128,1024]{1,0:T(8,128)(2,1)S(1)}, bf16[128,1024]{1,0:T(8,128)(2,1)S(1)}, u32[]{:S(2)}, u32[]{:S(2)}) collective-permute-start(bf16[128,1024]{1,0:T(8,128)(2,1)S(1)} %shard_map.138), channel_id=1, source_target_pairs={{0,8},{1,9},{2,10},{3,11},{4,12},{5,13},{6,14},{7,15},{8,0},{9,1},... | collective-permute-start | bytes 786440 | tf_op jit(solution)/shard_map/ppermute | solution.py:24
  182.5 14.6 %collective-permute-start.33 = (bf16[800,128]{1,0:T(8,128)(2,1)S(1)}, bf16[800,128]{1,0:T(8,128)(2,1)S(1)}, u32[]{:S(2)}, u32[]{:S(2)}) collective-permute-start(bf16[800,128]{1,0:T(8,128)(2,1)S(1)} %get-tuple-element.88), channel_id=1, source_target_pairs={{0,5},{1,4},{2,7},{3,6},{4,1},{5,0},{6,3},{7,2},{8,13},{9,12},{10,... | collective-permute-start | bytes 614408 | tf_op jit(solution)/shard_map/ppermute | solution.py:24
  183.4 18.2 %collective-permute-start.34 = (bf16[800,128]{1,0:T(8,128)(2,1)S(1)}, bf16[800,128]{1,0:T(8,128)(2,1)S(1)}, u32[]{:S(2)}, u32[]{:S(2)}) collective-permute-start(bf16[800,128]{1,0:T(8,128)(2,1)S(1)} %get-tuple-element.89), channel_id=1, source_target_pairs={{0,6},{1,7},{2,4},{3,5},{4,2},{5,3},{6,0},{7,1},{8,14},{9,15},{10,... | collective-permute-start | bytes 614408 | tf_op jit(solution)/shard_map/ppermute | solution.py:24
  184.4 24.3 %collective-permute-start.35 = (bf16[800,128]{1,0:T(8,128)(2,1)S(1)}, bf16[800,128]{1,0:T(8,128)(2,1)S(1)}, u32[]{:S(2)}, u32[]{:S(2)}) collective-permute-start(bf16[800,128]{1,0:T(8,128)(2,1)S(1)} %get-tuple-element.90), channel_id=1, source_target_pairs={{0,7},{1,6},{2,5},{3,4},{4,3},{5,2},{6,1},{7,0},{8,15},{9,14},{10,... | collective-permute-start | bytes 614408 | tf_op jit(solution)/shard_map/ppermute | solution.py:24
  (61 other events, 522.3 us)

commit v3 on v2

--- a/solution.py
+++ b/solution.py
@@ -24,7 +24,7 @@
     return lax.ppermute(value, "expert", [(i, i ^ mask) for i in range(size)])
 
 
-def call(body, in_specs, outs, operands, flops=0, scratch=(), limit=24):
+def call(body, in_specs, outs, operands, flops=0, scratch=(), limit=16):
     return pl.pallas_call(
         body,
         in_specs=in_specs,
@@ -80,9 +80,9 @@
 
 
 def attend_body(size, local_len, seq_count, latent, heads, group, *refs):
-    info, lengths, queries, memory = refs[:4]
-    pieces = refs[4 : 4 + size]
-    out, keys, rows = refs[4 + size :]
+    info, queries, memory = refs[:3]
+    pieces = refs[3 : 3 + size]
+    out, keys, rows = refs[3 + size :]
     seg_len = size * local_len
     total_len = seg_len + memory.shape[0]
     shift = local_len.bit_length() - 1
@@ -99,7 +99,7 @@
         for m in range(size):
             keys[pl.ds(m * local_len, local_len), :] = pieces[m][:, cols]
         keys[pl.ds(seg_len, memory.shape[0]), :] = memory[:, cols]
-        bias = jnp.where(causal & (pos < lengths[0, s]), 0.0, -jnp.inf)
+        bias = jnp.where(causal & (pos < info[2 + size // 2 + s]), 0.0, -jnp.inf)
         bias = jnp.concatenate([bias] * group, axis=0)
         for first in range(0, heads, group):
             for h in range(group):
@@ -241,9 +241,8 @@
     others, out = refs[:-1], refs[-1]
     other = jnp.concatenate([o[...] for o in others], axis=1).astype(f32)
     done = (total[...] + other).astype(bf16)
-    width = done.shape[1]
     for s in range(seq_count):
-        out[:, s * width : (s + 1) * width] = done[s * local_len : (s + 1) * local_len]
+        out[:, s, :] = done[s * local_len : (s + 1) * local_len]
 
 
 def layer(
@@ -275,7 +274,7 @@
     lanes = 128
     index_here = index % half
     owners = index - index_here + (index_here ^ jnp.arange(half, dtype=i32))
-    info = jnp.concatenate([jnp.stack([index, core]).astype(i32), owners])
+    info = jnp.concatenate([jnp.stack([index, core]).astype(i32), owners, lengths[0]])
 
     quarter = half // 2
     parts = fetch_weights(w_uv, w_out, core, size)
@@ -300,22 +299,21 @@
         flops=4 * rows * rows * wide,
     )
 
-    group = max(1, min(heads, 256 // local_len))
+    group = max(1, min(heads, 512 // local_len))
     total_len = size * local_len + mem_latents.shape[1]
     (attended,) = call(
         functools.partial(attend_body, size, local_len, seq_count, latent, heads, group),
-        [SMEM, SMEM, VMEM, VMEM] + [VMEM] * size,
+        [SMEM, VMEM, VMEM] + [VMEM] * size,
         [((rows, heads * latent), bf16)],
         [
             info,
-            lengths,
             query_rows,
             memory,
             *pieces,
         ],
         flops=4 * rows * heads * latent * total_len,
         scratch=[pltpu.VMEM((total_len, latent), bf16), pltpu.VMEM((group * local_len, latent), bf16)],
-        limit=16 + total_len * 9 // 1024,
+        limit=6 + total_len * 9 // 1024 + size // 8,
     )
     step = width // cuts
     residual, *normed = call(
@@ -392,7 +390,7 @@
     (out,) = call(
         functools.partial(last_body, local_len, seq_count),
         [VMEM] * (1 + cuts),
-        [((local_len, seq_count * width), bf16)],
+        [((local_len, seq_count, width), bf16)],
         [total, *others],
         flops=8 * rows * width,
     )

time: 211 us -> 210 us (level)
    unnamed x54 -> x52, local copies, waits for them, and re-layouts: 15.7 us -> 15.3 us
  transfers between devices with their start and end apart: 68 -> 68, of which waited for: 27 -> 26; matrix products, arithmetic and copies ran while one was open for 2% -> 2% of each run, Pallas kernels for 10% -> 10%
where the time goes in v3:
time: 210 us
  waiting for transfers between devices  99.9 us (48%)
  starting transfers between devices  65 us (31%)
  Pallas kernels  26.3 us (13%)
  local copies, waits for them, and re-layouts  17 us (8%)
    ppermute x66, waiting for transfers between devices, flip(): return lax.ppermute(value, 'expert', [(i, i ^ mask) for i in range(size)])  81.3 us
    ppermute x66, starting transfers between devices, flip(): return lax.ppermute(value, 'expert', [(i, i ^ mask) for i in range(size)])  60.7 us
    pallas_call x14, Pallas kernels, call(): pl.pallas_call(body, in_specs=in_specs, out_specs=[VMEM] * len(outs), out...  26.3 us
    ppermute x1, waiting for transfers between devices, fetch_weights(): out_got = lax.ppermute(out_half, 'dp', source)  18.6 us
    unnamed x52, local copies, waits for them, and re-layouts  15.3 us
  transfers between devices with their start and end apart: 68, of which 26 were waited for; matrix products, arithmetic and copies ran while one was open for 2% of the time, Pallas kernels for 10%

profile of v3, /device:TPU:0, one launch (start us, length us, event | category | flops | bytes accessed | tf_op | source)
XLA Modules:
  0.0 210.0 jit_solution(17853877048869542509)
XLA Ops:
  1.5 3.0 %collective-permute-start.18 = (bf16[256,2048]{1,0:T(8,128)(2,1)S(1)}, bf16[256,2048]{1,0:T(8,128)(2,1)S(1)}, u32[]{:S(2)}, u32[]{:S(2)}) collective-permute-start(bf16[256,2048]{1,0:T(8,128)(2,1)S(1)} %constant_dynamic-slice_fusion), channel_id=1, source_target_pairs={{16,0},{0,16},{17,1},{1,17},{18,2},{2,18},{19,3},{3,19},{20,4},{4,... | collective-permute-start | bytes 3145736 | tf_op jit(solution)/shard_map/ppermute | solution.py:64
  5.4 3.7 %collective-permute-start.2 = (bf16[64,1024]{1,0:T(8,128)(2,1)S(1)}, bf16[64,1024]{1,0:T(8,128)(2,1)}, u32[]{:S(2)}, u32[]{:S(2)}) collective-permute-start(bf16[64,1024]{1,0:T(8,128)(2,1)S(1)} %bitcast.39), channel_id=1, source_target_pairs={{0,12},{1,13},{2,14},{3,15},{4,8},{5,9},{6,10},{7,11},{8,4},{9,5},... | collective-permute-start | bytes 393224 | tf_op jit(solution)/shard_map/ppermute | solution.py:24
  9.1 18.6 %collective-permute-done.18.refs_7_ = bf16[256,2048]{1,0:T(8,128)(2,1)S(1)} collective-permute-done((bf16[256,2048]{1,0:T(8,128)(2,1)S(1)}, bf16[256,2048]{1,0:T(8,128)(2,1)S(1)}, u32[]{:S(2)}, u32[]{:S(2)}) %collective-permute-start.18) | collective-permute-done | bytes 1048608 | tf_op jit(solution)/shard_map/ppermute | solution.py:64
  27.7 2.8 %collective-permute-start.10 = (bf16[64,1024]{1,0:T(8,128)(2,1)S(1)}, bf16[64,1024]{1,0:T(8,128)(2,1)}, u32[]{:S(2)}, u32[]{:S(2)}) collective-permute-start(bf16[64,1024]{1,0:T(8,128)(2,1)S(1)} %bitcast.40), channel_id=1, source_target_pairs={{0,8},{1,9},{2,10},{3,11},{4,12},{5,13},{6,14},{7,15},{8,0},{9,1},... | collective-permute-start | bytes 393224 | tf_op jit(solution)/shard_map/ppermute | solution.py:24
  35.1 2.7 %collective-permute-done.10.refs_11_ = bf16[64,1024]{1,0:T(8,128)(2,1)} collective-permute-done((bf16[64,1024]{1,0:T(8,128)(2,1)S(1)}, bf16[64,1024]{1,0:T(8,128)(2,1)}, u32[]{:S(2)}, u32[]{:S(2)}) %collective-permute-start.10) | collective-permute-done | bytes 131104 | tf_op jit(solution)/shard_map/ppermute | solution.py:24
  41.4 2.2 %collective-permute-done.15.refs_17_ = bf16[64,1024]{1,0:T(8,128)(2,1)} collective-permute-done((bf16[64,1024]{1,0:T(8,128)(2,1)}, bf16[64,1024]{1,0:T(8,128)(2,1)}, u32[]{:S(2)}, u32[]{:S(2)}) %collective-permute-start.15) | collective-permute-done | bytes 131104 | tf_op jit(solution)/shard_map/ppermute | solution.py:24
  46.4 2.3 %collective-permute-done.8.refs_9_ = bf16[64,1024]{1,0:T(8,128)(2,1)} collective-permute-done((bf16[64,1024]{1,0:T(8,128)(2,1)}, bf16[64,1024]{1,0:T(8,128)(2,1)}, u32[]{:S(2)}, u32[]{:S(2)}) %collective-permute-start.8) | collective-permute-done | bytes 131104 | tf_op jit(solution)/shard_map/ppermute | solution.py:24
  59.3 5.2 %shard_map.128.refs_1_ = bf16[128,4096]{1,0:T(8,128)(2,1)S(1)} custom-call(s32[12]{0:T(128)S(1)} %pad_add_fusion.info.refs_0_, bf16[64,8192]{1,0:T(8,128)(2,1)S(1)} %bitcast.35, bf16[32,1024]{1,0:T(8,128)(2,1)S(1)} %bitcast.45, bf16[64,1024]{1,0:T(8,128)(2,1)S(1)} %bitcast.44, bf16[64,1024]{1,0:T(8,128)(2,1)S(1)} %copy-done.10, ...), custom_call_target="tpu_custom_call" | custom-call | flops 2214592512 | tf_op jit(solution)/shard_map/pallas_call | solution.py:28
  64.5 3.6 %shard_map.129 = (f32[128,2048]{1,0:T(8,128)S(1)}, bf16[128,1024]{1,0:T(8,128)(2,1)}, bf16[128,1024]{1,0:T(8,128)(2,1)}) custom-call(s32[8]{0:T(128)S(1)} %stack.43.refs_0_, bf16[128,4096]{1,0:T(8,128)(2,1)S(1)} %shard_map.128.refs_1_, bf16[64,4096]{1,0:T(8,128)(2,1)S(1)} %bitcast.34, bf16[1,2048]{1,0:T(2,128)(2,1)S(1)} %reshape.13.refs_3_, ...), custom_call_target="tpu_custom_call" | custom-call | flops 536870912 | tf_op jit(solution)/shard_map/pallas_call | solution.py:28
  68.2 2.9 %collective-permute-start.44 = (bf16[128,1024]{1,0:T(8,128)(2,1)}, bf16[128,1024]{1,0:T(8,128)(2,1)S(1)}, u32[]{:S(2)}, u32[]{:S(2)}) collective-permute-start(bf16[128,1024]{1,0:T(8,128)(2,1)} %get-tuple-element.73.refs_1_), channel_id=1, source_target_pairs={{0,8},{1,9},{2,10},{3,11},{4,12},{5,13},{6,14},{7,15},{8,0},{9,1},... | collective-permute-start | bytes 786440 | tf_op jit(solution)/shard_map/ppermute | solution.py:24
  72.7 2.9 %collective-permute-start.1 = (f32[128,12]{1,0:T(8,128)S(1)}, f32[128,12]{1,0:T(8,128)S(1)}, u32[]{:S(2)}, u32[]{:S(2)}) collective-permute-start(f32[128,12]{1,0:T(8,128)S(1)} %bitcast.37), channel_id=1, source_target_pairs={{0,8},{1,9},{2,10},{3,11},{4,12},{5,13},{6,14},{7,15},{8,0},{9,1},... | collective-permute-start | bytes 18440 | tf_op jit(solution)/shard_map/ppermute | solution.py:24
  75.6 6.6 %collective-permute-done.side = f32[128,12]{1,0:T(8,128)S(1)} collective-permute-done((f32[128,12]{1,0:T(8,128)S(1)}, f32[128,12]{1,0:T(8,128)S(1)}, u32[]{:S(2)}, u32[]{:S(2)}) %collective-permute-start) | collective-permute-done | bytes 6176 | tf_op jit(solution)/shard_map/ppermute | solution.py:24
  82.2 15.3 %collective-permute-done.1.far = f32[128,12]{1,0:T(8,128)S(1)} collective-permute-done((f32[128,12]{1,0:T(8,128)S(1)}, f32[128,12]{1,0:T(8,128)S(1)}, u32[]{:S(2)}, u32[]{:S(2)}) %collective-permute-start.1) | collective-permute-done | bytes 6176 | tf_op jit(solution)/shard_map/ppermute | solution.py:24
  110.1 2.3 %collective-permute-done.42.refs_6_ = bf16[400,128]{1,0:T(8,128)(2,1)S(1)} collective-permute-done((bf16[400,128]{1,0:T(8,128)(2,1)S(1)}, bf16[400,128]{1,0:T(8,128)(2,1)S(1)}, u32[]{:S(2)}, u32[]{:S(2)}) %collective-permute-start.42) | collective-permute-done | bytes 102432 | tf_op jit(solution)/shard_map/ppermute | solution.py:24
  113.7 1.8 collective-permute-start.50
  120.4 1.8 collective-permute-done.50.refs_14_
  125.3 1.8 copy-done.3
  127.1 1.8 copy-done.5
  128.9 1.8 copy-done.6
  130.7 4.7 %shard_map.137 = (bf16[400,128]{1,0:T(8,128)(2,1)S(1)}, bf16[400,128]{1,0:T(8,128)(2,1)S(1)}, bf16[400,128]{1,0:T(8,128)(2,1)S(1)}, bf16[400,128]{1,0:T(8,128)(2...) custom-call(bf16[1,704,2048]{2,1,0:T(8,128)(2,1)S(1)} %bitcast.46, ...), custom_call_target="tpu_custom_call" | custom-call | flops 3875536896 | tf_op jit(solution)/shard_map/pallas_call | solution.py:28
  137.4 1.7 collective-permute-start.64
  139.6 1.8 collective-permute-done.61.refs_2_
  145.4 2.3 %collective-permute-done.65.refs_6_ = bf16[400,128]{1,0:T(8,128)(2,1)S(1)} collective-permute-done((bf16[400,128]{1,0:T(8,128)(2,1)S(1)}, bf16[400,128]{1,0:T(8,128)(2,1)S(1)}, u32[]{:S(2)}, u32[]{:S(2)}) %collective-permute-start.65) | collective-permute-done | bytes 102432 | tf_op jit(solution)/shard_map/ppermute | solution.py:24
  150.1 2.6 %shard_map.131 = (bf16[800,128]{1,0:T(8,128)(2,1)S(1)}, bf16[800,128]{1,0:T(8,128)(2,1)S(1)}, bf16[800,128]{1,0:T(8,128)(2,1)S(1)}, bf16[800,128]{1,0:T(8,128)(2,1)S(1)}) custom-call(bf16[1,704,2048]{2,1,0:T(8,128)(2,1)S(1)} %bitcast.47, bf16[1,704,2048]{2,1,0:T(8,128)(2,1)S(1)} %bitcast.50, bf16[1,704,2048]{2,1,0:T(8,128)(2,1)S(1)} %copy-done.6, ...), custom_call_target="tpu_custom_call" | custom-call | flops 3875536896 | tf_op jit(solution)/shard_map/pallas_call | solution.py:28
  152.9 7.3 %collective-permute-done.53.refs_2_ = bf16[400,128]{1,0:T(8,128)(2,1)S(1)} collective-permute-done((bf16[400,128]{1,0:T(8,128)(2,1)S(1)}, bf16[400,128]{1,0:T(8,128)(2,1)S(1)}, u32[]{:S(2)}, u32[]{:S(2)}) %collective-permute-start.53) | collective-permute-done | bytes 102432 | tf_op jit(solution)/shard_map/ppermute | solution.py:24
  163.5 2.6 %shard_map.133 = (bf16[800,128]{1,0:T(8,128)(2,1)S(1)}, bf16[800,128]{1,0:T(8,128)(2,1)S(1)}, bf16[800,128]{1,0:T(8,128)(2,1)S(1)}, bf16[800,128]{1,0:T(8,128)(2,1)S(1)}) custom-call(bf16[1,704,2048]{2,1,0:T(8,128)(2,1)S(1)} %bitcast.48, bf16[1,704,2048]{2,1,0:T(8,128)(2,1)S(1)} %bitcast.51, bf16[1,704,2048]{2,1,0:T(8,128)(2,1)S(1)} %copy-done.6, ...), custom_call_target="tpu_custom_call" | custom-call | flops 3875536896 | tf_op jit(solution)/shard_map/pallas_call | solution.py:28
  169.2 1.8 collective-permute-done.57.refs_6_
  171.9 6.3 %collective-permute-done.58.refs_7_ = bf16[400,128]{1,0:T(8,128)(2,1)S(1)} collective-permute-done((bf16[400,128]{1,0:T(8,128)(2,1)S(1)}, bf16[400,128]{1,0:T(8,128)(2,1)S(1)}, u32[]{:S(2)}, u32[]{:S(2)}) %collective-permute-start.58) | collective-permute-done | bytes 102432 | tf_op jit(solution)/shard_map/ppermute | solution.py:24
  183.6 2.2 %collective-permute-start.35 = (bf16[800,128]{1,0:T(8,128)(2,1)S(1)}, bf16[800,128]{1,0:T(8,128)(2,1)S(1)}, u32[]{:S(2)}, u32[]{:S(2)}) collective-permute-start(bf16[800,128]{1,0:T(8,128)(2,1)S(1)} %get-tuple-element.90), channel_id=1, source_target_pairs={{0,7},{1,6},{2,5},{3,4},{4,3},{5,2},{6,1},{7,0},{8,15},{9,14},{10,... | collective-permute-start | bytes 614408 | tf_op jit(solution)/shard_map/ppermute | solution.py:24
  185.8 10.5 %collective-permute-done.33.refs_5_ = bf16[800,128]{1,0:T(8,128)(2,1)S(1)} collective-permute-done((bf16[800,128]{1,0:T(8,128)(2,1)S(1)}, bf16[800,128]{1,0:T(8,128)(2,1)S(1)}, u32[]{:S(2)}, u32[]{:S(2)}) %collective-permute-start.33) | collective-permute-done | bytes 204832 | tf_op jit(solution)/shard_map/ppermute | solution.py:24
  196.4 4.4 %collective-permute-done.34.refs_6_ = bf16[800,128]{1,0:T(8,128)(2,1)S(1)} collective-permute-done((bf16[800,128]{1,0:T(8,128)(2,1)S(1)}, bf16[800,128]{1,0:T(8,128)(2,1)S(1)}, u32[]{:S(2)}, u32[]{:S(2)}) %collective-permute-start.34) | collective-permute-done | bytes 204832 | tf_op jit(solution)/shard_map/ppermute | solution.py:24
  200.7 7.1 %collective-permute-done.35.refs_7_ = bf16[800,128]{1,0:T(8,128)(2,1)S(1)} collective-permute-done((bf16[800,128]{1,0:T(8,128)(2,1)S(1)}, bf16[800,128]{1,0:T(8,128)(2,1)S(1)}, u32[]{:S(2)}, u32[]{:S(2)}) %collective-permute-start.35) | collective-permute-done | bytes 204832 | tf_op jit(solution)/shard_map/ppermute | solution.py:24
  (180 shorter events, 71.2 us)
Async XLA Ops:
  1.5 26.2 %collective-permute-start.18 = (bf16[256,2048]{1,0:T(8,128)(2,1)S(1)}, bf16[256,2048]{1,0:T(8,128)(2,1)S(1)}, u32[]{:S(2)}, u32[]{:S(2)}) collective-permute-start(bf16[256,2048]{1,0:T(8,128)(2,1)S(1)} %constant_dynamic-slice_fusion), channel_id=1, source_target_pairs={{16,0},{0,16},{17,1},{1,17},{18,2},{2,18},{19,3},{3,19},{20,4},{4,... | collective-permute-start | bytes 3145736 | tf_op jit(solution)/shard_map/ppermute | solution.py:64
  5.4 28.2 %collective-permute-start.2 = (bf16[64,1024]{1,0:T(8,128)(2,1)S(1)}, bf16[64,1024]{1,0:T(8,128)(2,1)}, u32[]{:S(2)}, u32[]{:S(2)}) collective-permute-start(bf16[64,1024]{1,0:T(8,128)(2,1)S(1)} %bitcast.39), channel_id=1, source_target_pairs={{0,12},{1,13},{2,14},{3,15},{4,8},{5,9},{6,10},{7,11},{8,4},{9,5},... | collective-permute-start | bytes 393224 | tf_op jit(solution)/shard_map/ppermute | solution.py:24
  27.7 36.8 %collective-permute-start.20 = (bf16[256,2048]{1,0:T(8,128)(2,1)S(1)}, bf16[256,2048]{1,0:T(8,128)(2,1)}, u32[]{:S(2)}, u32[]{:S(2)}) collective-permute-start(bf16[256,2048]{1,0:T(8,128)(2,1)S(1)} %collective-permute-done.18.refs_7_), channel_id=1, source_target_pairs={{0,1},{1,0},{2,3},{3,2},{4,5},{5,4},{6,7},{7,6},{8,9},{9,8},{10,11... | collective-permute-start | bytes 3145736 | tf_op jit(solution)/shard_map/ppermute | solution.py:24
  27.7 10.0 %collective-permute-start.10 = (bf16[64,1024]{1,0:T(8,128)(2,1)S(1)}, bf16[64,1024]{1,0:T(8,128)(2,1)}, u32[]{:S(2)}, u32[]{:S(2)}) collective-permute-start(bf16[64,1024]{1,0:T(8,128)(2,1)S(1)} %bitcast.40), channel_id=1, source_target_pairs={{0,8},{1,9},{2,10},{3,11},{4,12},{5,13},{6,14},{7,15},{8,0},{9,1},... | collective-permute-start | bytes 393224 | tf_op jit(solution)/shard_map/ppermute | solution.py:24
  39.8 9.0 %collective-permute-start.8 = (bf16[64,1024]{1,0:T(8,128)(2,1)}, bf16[64,1024]{1,0:T(8,128)(2,1)}, u32[]{:S(2)}, u32[]{:S(2)}) collective-permute-start(bf16[64,1024]{1,0:T(8,128)(2,1)} %collective-permute-done.6.refs_7_), channel_id=1, source_target_pairs={{0,2},{1,3},{2,0},{3,1},{4,6},{5,7},{6,4},{7,5},{8,10},{9,11},{10,... | collective-permute-start | bytes 393224 | tf_op jit(solution)/shard_map/ppermute | solution.py:24
  43.6 8.8 %collective-permute-start.17 = (bf16[2,512,128]{2,1,0:T(8,128)(2,1)S(1)}, bf16[2,512,128]{2,1,0:T(8,128)(2,1)S(1)}, u32[]{:S(2)}, u32[]{:S(2)}) collective-permute-start(bf16[2,512,128]{2,1,0:T(8,128)(2,1)S(1)} %constant_dynamic-slice_fusion.1), channel_id=1, source_target_pairs={{16,0},{0,16},{17,1},{1,17},{18,2},{2,18},{19,3},{3,19},{20,4},{4,... | collective-permute-start | bytes 786440 | tf_op jit(solution)/shard_map/ppermute | solution.py:63
  52.4 12.1 %collective-permute-start.19 = (bf16[2,512,128]{2,1,0:T(8,128)(2,1)S(1)}, bf16[2,512,128]{2,1,0:T(8,128)(2,1)}, u32[]{:S(2)}, u32[]{:S(2)}) collective-permute-start(bf16[2,512,128]{2,1,0:T(8,128)(2,1)S(1)} %collective-permute-done.17.refs_6_), channel_id=1, source_target_pairs={{0,1},{1,0},{2,3},{3,2},{4,5},{5,4},{6,7},{7,6},{8,9},{9,8},{10,11... | collective-permute-start | bytes 786440 | tf_op jit(solution)/shard_map/ppermute | solution.py:24
  68.1 30.9 %collective-permute-start.36 = (bf16[128,1024]{1,0:T(8,128)(2,1)}, bf16[128,1024]{1,0:T(8,128)(2,1)S(1)}, u32[]{:S(2)}, u32[]{:S(2)}) collective-permute-start(bf16[128,1024]{1,0:T(8,128)(2,1)} %get-tuple-element.72.refs_0_), channel_id=1, source_target_pairs={{0,8},{1,9},{2,10},{3,11},{4,12},{5,13},{6,14},{7,15},{8,0},{9,1},... | collective-permute-start | bytes 786440 | tf_op jit(solution)/shard_map/ppermute | solution.py:24
  68.2 33.2 %collective-permute-start.44 = (bf16[128,1024]{1,0:T(8,128)(2,1)}, bf16[128,1024]{1,0:T(8,128)(2,1)S(1)}, u32[]{:S(2)}, u32[]{:S(2)}) collective-permute-start(bf16[128,1024]{1,0:T(8,128)(2,1)} %get-tuple-element.73.refs_1_), channel_id=1, source_target_pairs={{0,8},{1,9},{2,10},{3,11},{4,12},{5,13},{6,14},{7,15},{8,0},{9,1},... | collective-permute-start | bytes 786440 | tf_op jit(solution)/shard_map/ppermute | solution.py:24
  71.2 11.0 %collective-permute-start = (f32[128,12]{1,0:T(8,128)S(1)}, f32[128,12]{1,0:T(8,128)S(1)}, u32[]{:S(2)}, u32[]{:S(2)}) collective-permute-start(f32[128,12]{1,0:T(8,128)S(1)} %bitcast.36), channel_id=1, source_target_pairs={{0,4},{1,5},{2,6},{3,7},{4,0},{5,1},{6,2},{7,3},{8,12},{9,13},{10,... | collective-permute-start | bytes 18440 | tf_op jit(solution)/shard_map/ppermute | solution.py:24
  72.7 24.8 %collective-permute-start.1 = (f32[128,12]{1,0:T(8,128)S(1)}, f32[128,12]{1,0:T(8,128)S(1)}, u32[]{:S(2)}, u32[]{:S(2)}) collective-permute-start(f32[128,12]{1,0:T(8,128)S(1)} %bitcast.37), channel_id=1, source_target_pairs={{0,8},{1,9},{2,10},{3,11},{4,12},{5,13},{6,14},{7,15},{8,0},{9,1},... | collective-permute-start | bytes 18440 | tf_op jit(solution)/shard_map/ppermute | solution.py:24
  103.5 8.9 %collective-permute-start.42 = (bf16[400,128]{1,0:T(8,128)(2,1)S(1)}, bf16[400,128]{1,0:T(8,128)(2,1)S(1)}, u32[]{:S(2)}, u32[]{:S(2)}) collective-permute-start(bf16[400,128]{1,0:T(8,128)(2,1)S(1)} %get-tuple-element.99), channel_id=1, source_target_pairs={{0,6},{1,7},{2,4},{3,5},{4,2},{5,3},{6,0},{7,1},{8,14},{9,15},{10,... | collective-permute-start | bytes 307208 | tf_op jit(solution)/shard_map/ppermute | solution.py:24
  107.1 9.1 %collective-permute-start.46 = (bf16[400,128]{1,0:T(8,128)(2,1)S(1)}, bf16[400,128]{1,0:T(8,128)(2,1)S(1)}, u32[]{:S(2)}, u32[]{:S(2)}) collective-permute-start(bf16[400,128]{1,0:T(8,128)(2,1)S(1)} %get-tuple-element.103), channel_id=1, source_target_pairs={{0,2},{1,3},{2,0},{3,1},{4,6},{5,7},{6,4},{7,5},{8,10},{9,11},{10,... | collective-permute-start | bytes 307208 | tf_op jit(solution)/shard_map/ppermute | solution.py:24
  108.5 9.8 %collective-permute-start.47 = (bf16[400,128]{1,0:T(8,128)(2,1)S(1)}, bf16[400,128]{1,0:T(8,128)(2,1)S(1)}, u32[]{:S(2)}, u32[]{:S(2)}) collective-permute-start(bf16[400,128]{1,0:T(8,128)(2,1)S(1)} %get-tuple-element.104), channel_id=1, source_target_pairs={{0,3},{1,2},{2,1},{3,0},{4,7},{5,6},{6,5},{7,4},{8,11},{9,10},{10,... | collective-permute-start | bytes 307208 | tf_op jit(solution)/shard_map/ppermute | solution.py:24
  118.3 19.1 %collective-permute-start.27 = (bf16[128,1024]{1,0:T(8,128)(2,1)}, bf16[128,1024]{1,0:T(8,128)(2,1)S(1)}, u32[]{:S(2)}, u32[]{:S(2)}) collective-permute-start(bf16[128,1024]{1,0:T(8,128)(2,1)} %get-tuple-element.72.refs_0_), channel_id=1, source_target_pairs={{0,4},{1,5},{2,6},{3,7},{4,0},{5,1},{6,2},{7,3},{8,12},{9,13},{10,... | collective-permute-start | bytes 786440 | tf_op jit(solution)/shard_map/ppermute | solution.py:24
  119.4 18.0 %collective-permute-start.28 = (bf16[128,1024]{1,0:T(8,128)(2,1)}, bf16[128,1024]{1,0:T(8,128)(2,1)S(1)}, u32[]{:S(2)}, u32[]{:S(2)}) collective-permute-start(bf16[128,1024]{1,0:T(8,128)(2,1)} %get-tuple-element.73.refs_1_), channel_id=1, source_target_pairs={{0,4},{1,5},{2,6},{3,7},{4,0},{5,1},{6,2},{7,3},{8,12},{9,13},{10,... | collective-permute-start | bytes 786440 | tf_op jit(solution)/shard_map/ppermute | solution.py:24
  120.4 15.1 %collective-permute-start.21 = (bf16[800,128]{1,0:T(8,128)(2,1)S(1)}, bf16[800,128]{1,0:T(8,128)(2,1)S(1)}, u32[]{:S(2)}, u32[]{:S(2)}) collective-permute-start(bf16[800,128]{1,0:T(8,128)(2,1)S(1)} %get-tuple-element.75), channel_id=1, source_target_pairs={{0,1},{1,0},{2,3},{3,2},{4,5},{5,4},{6,7},{7,6},{8,9},{9,8},{10,11... | collective-permute-start | bytes 614408 | tf_op jit(solution)/shard_map/ppermute | solution.py:24
  122.3 13.3 %collective-permute-start.22 = (bf16[800,128]{1,0:T(8,128)(2,1)S(1)}, bf16[800,128]{1,0:T(8,128)(2,1)S(1)}, u32[]{:S(2)}, u32[]{:S(2)}) collective-permute-start(bf16[800,128]{1,0:T(8,128)(2,1)S(1)} %get-tuple-element.76), channel_id=1, source_target_pairs={{0,2},{1,3},{2,0},{3,1},{4,6},{5,7},{6,4},{7,5},{8,10},{9,11},{10,... | collective-permute-start | bytes 614408 | tf_op jit(solution)/shard_map/ppermute | solution.py:24
  123.7 12.6 %collective-permute-start.23 = (bf16[800,128]{1,0:T(8,128)(2,1)S(1)}, bf16[800,128]{1,0:T(8,128)(2,1)S(1)}, u32[]{:S(2)}, u32[]{:S(2)}) collective-permute-start(bf16[800,128]{1,0:T(8,128)(2,1)S(1)} %get-tuple-element.77), channel_id=1, source_target_pairs={{0,3},{1,2},{2,1},{3,0},{4,7},{5,6},{6,5},{7,4},{8,11},{9,10},{10,... | collective-permute-start | bytes 614408 | tf_op jit(solution)/shard_map/ppermute | solution.py:24
  142.5 18.3 %collective-permute-start.29 = (bf16[800,128]{1,0:T(8,128)(2,1)S(1)}, bf16[800,128]{1,0:T(8,128)(2,1)S(1)}, u32[]{:S(2)}, u32[]{:S(2)}) collective-permute-start(bf16[800,128]{1,0:T(8,128)(2,1)S(1)} %get-tuple-element.84), channel_id=1, source_target_pairs={{0,1},{1,0},{2,3},{3,2},{4,5},{5,4},{6,7},{7,6},{8,9},{9,8},{10,11... | collective-permute-start | bytes 614408 | tf_op jit(solution)/shard_map/ppermute | solution.py:24
  143.2 18.3 %collective-permute-start.30 = (bf16[800,128]{1,0:T(8,128)(2,1)S(1)}, bf16[800,128]{1,0:T(8,128)(2,1)S(1)}, u32[]{:S(2)}, u32[]{:S(2)}) collective-permute-start(bf16[800,128]{1,0:T(8,128)(2,1)S(1)} %get-tuple-element.85), channel_id=1, source_target_pairs={{0,2},{1,3},{2,0},{3,1},{4,6},{5,7},{6,4},{7,5},{8,10},{9,11},{10,... | collective-permute-start | bytes 614408 | tf_op jit(solution)/shard_map/ppermute | solution.py:24
  144.2 18.7 %collective-permute-start.31 = (bf16[800,128]{1,0:T(8,128)(2,1)S(1)}, bf16[800,128]{1,0:T(8,128)(2,1)S(1)}, u32[]{:S(2)}, u32[]{:S(2)}) collective-permute-start(bf16[800,128]{1,0:T(8,128)(2,1)S(1)} %get-tuple-element.86), channel_id=1, source_target_pairs={{0,3},{1,2},{2,1},{3,0},{4,7},{5,6},{6,5},{7,4},{8,11},{9,10},{10,... | collective-permute-start | bytes 614408 | tf_op jit(solution)/shard_map/ppermute | solution.py:24
  148.7 11.5 %collective-permute-start.53 = (bf16[400,128]{1,0:T(8,128)(2,1)S(1)}, bf16[400,128]{1,0:T(8,128)(2,1)S(1)}, u32[]{:S(2)}, u32[]{:S(2)}) collective-permute-start(bf16[400,128]{1,0:T(8,128)(2,1)S(1)} %get-tuple-element.111), channel_id=1, source_target_pairs={{0,2},{1,3},{2,0},{3,1},{4,6},{5,7},{6,4},{7,5},{8,10},{9,11},{10,... | collective-permute-start | bytes 307208 | tf_op jit(solution)/shard_map/ppermute | solution.py:24
  152.7 27.5 %collective-permute-start.24 = (bf16[800,128]{1,0:T(8,128)(2,1)S(1)}, bf16[800,128]{1,0:T(8,128)(2,1)S(1)}, u32[]{:S(2)}, u32[]{:S(2)}) collective-permute-start(bf16[800,128]{1,0:T(8,128)(2,1)S(1)} %get-tuple-element.79), channel_id=1, source_target_pairs={{0,1},{1,0},{2,3},{3,2},{4,5},{5,4},{6,7},{7,6},{8,9},{9,8},{10,11... | collective-permute-start | bytes 614408 | tf_op jit(solution)/shard_map/ppermute | solution.py:24
  166.1 15.6 %collective-permute-start.25 = (bf16[800,128]{1,0:T(8,128)(2,1)S(1)}, bf16[800,128]{1,0:T(8,128)(2,1)S(1)}, u32[]{:S(2)}, u32[]{:S(2)}) collective-permute-start(bf16[800,128]{1,0:T(8,128)(2,1)S(1)} %get-tuple-element.80), channel_id=1, source_target_pairs={{0,2},{1,3},{2,0},{3,1},{4,6},{5,7},{6,4},{7,5},{8,10},{9,11},{10,... | collective-permute-start | bytes 614408 | tf_op jit(solution)/shard_map/ppermute | solution.py:24
  167.5 15.1 %collective-permute-start.26 = (bf16[800,128]{1,0:T(8,128)(2,1)S(1)}, bf16[800,128]{1,0:T(8,128)(2,1)S(1)}, u32[]{:S(2)}, u32[]{:S(2)}) collective-permute-start(bf16[800,128]{1,0:T(8,128)(2,1)S(1)} %get-tuple-element.81), channel_id=1, source_target_pairs={{0,3},{1,2},{2,1},{3,0},{4,7},{5,6},{6,5},{7,4},{8,11},{9,10},{10,... | collective-permute-start | bytes 614408 | tf_op jit(solution)/shard_map/ppermute | solution.py:24
  168.2 15.4 %collective-permute-start.32 = (bf16[800,128]{1,0:T(8,128)(2,1)S(1)}, bf16[800,128]{1,0:T(8,128)(2,1)S(1)}, u32[]{:S(2)}, u32[]{:S(2)}) collective-permute-start(bf16[800,128]{1,0:T(8,128)(2,1)S(1)} %get-tuple-element.87), channel_id=1, source_target_pairs={{0,4},{1,5},{2,6},{3,7},{4,0},{5,1},{6,2},{7,3},{8,12},{9,13},{10,... | collective-permute-start | bytes 614408 | tf_op jit(solution)/shard_map/ppermute | solution.py:24
  178.1 30.7 %collective-permute-start.67 = (bf16[128,1024]{1,0:T(8,128)(2,1)S(1)}, bf16[128,1024]{1,0:T(8,128)(2,1)S(1)}, u32[]{:S(2)}, u32[]{:S(2)}) collective-permute-start(bf16[128,1024]{1,0:T(8,128)(2,1)S(1)} %shard_map.139), channel_id=1, source_target_pairs={{0,8},{1,9},{2,10},{3,11},{4,12},{5,13},{6,14},{7,15},{8,0},{9,1},... | collective-permute-start | bytes 786440 | tf_op jit(solution)/shard_map/ppermute | solution.py:24
  180.2 28.6 %collective-permute-start.59 = (bf16[128,1024]{1,0:T(8,128)(2,1)S(1)}, bf16[128,1024]{1,0:T(8,128)(2,1)S(1)}, u32[]{:S(2)}, u32[]{:S(2)}) collective-permute-start(bf16[128,1024]{1,0:T(8,128)(2,1)S(1)} %shard_map.138), channel_id=1, source_target_pairs={{0,8},{1,9},{2,10},{3,11},{4,12},{5,13},{6,14},{7,15},{8,0},{9,1},... | collective-permute-start | bytes 786440 | tf_op jit(solution)/shard_map/ppermute | solution.py:24
  181.7 14.6 %collective-permute-start.33 = (bf16[800,128]{1,0:T(8,128)(2,1)S(1)}, bf16[800,128]{1,0:T(8,128)(2,1)S(1)}, u32[]{:S(2)}, u32[]{:S(2)}) collective-permute-start(bf16[800,128]{1,0:T(8,128)(2,1)S(1)} %get-tuple-element.88), channel_id=1, source_target_pairs={{0,5},{1,4},{2,7},{3,6},{4,1},{5,0},{6,3},{7,2},{8,13},{9,12},{10,... | collective-permute-start | bytes 614408 | tf_op jit(solution)/shard_map/ppermute | solution.py:24
  182.6 18.2 %collective-permute-start.34 = (bf16[800,128]{1,0:T(8,128)(2,1)S(1)}, bf16[800,128]{1,0:T(8,128)(2,1)S(1)}, u32[]{:S(2)}, u32[]{:S(2)}) collective-permute-start(bf16[800,128]{1,0:T(8,128)(2,1)S(1)} %get-tuple-element.89), channel_id=1, source_target_pairs={{0,6},{1,7},{2,4},{3,5},{4,2},{5,3},{6,0},{7,1},{8,14},{9,15},{10,... | collective-permute-start | bytes 614408 | tf_op jit(solution)/shard_map/ppermute | solution.py:24
  183.6 24.2 %collective-permute-start.35 = (bf16[800,128]{1,0:T(8,128)(2,1)S(1)}, bf16[800,128]{1,0:T(8,128)(2,1)S(1)}, u32[]{:S(2)}, u32[]{:S(2)}) collective-permute-start(bf16[800,128]{1,0:T(8,128)(2,1)S(1)} %get-tuple-element.90), channel_id=1, source_target_pairs={{0,7},{1,6},{2,5},{3,4},{4,3},{5,2},{6,1},{7,0},{8,15},{9,14},{10,... | collective-permute-start | bytes 614408 | tf_op jit(solution)/shard_map/ppermute | solution.py:24
  (60 other events, 522.3 us)

commit v4 on v3

--- a/solution.py
+++ b/solution.py
@@ -281,10 +281,11 @@
     beside = (
         queries[0].reshape(local_len, seq_count * heads * latent),
         hidden[0].reshape(local_len, seq_count * width),
-        mem_latents[0].reshape(-1, seq_count * latent),
-    )
+    )
+    memory = mem_latents[0].reshape(-1, seq_count * latent)
     own_latents = latents[0].reshape(local_len, seq_count * latent)
-    pieces, (query_rows, hidden_rows, memory) = gather_latents(own_latents, size, beside)
+    own_latents, memory = lax.optimization_barrier((own_latents, memory))
+    pieces, (query_rows, hidden_rows) = gather_latents(own_latents, size, beside)
     table = jnp.concatenate([ids[0].astype(f32), gates[0].astype(f32)], axis=2)
     table = jnp.transpose(table, (1, 0, 2)).reshape(rows, 2 * top)
     far_table = flip(table, half, size)

time: 210 us -> 210 us (level)
    unnamed x52 -> x50, local copies, waits for them, and re-layouts: 15.3 us -> 16.1 us
where the time goes in v4:
time: 210 us
  waiting for transfers between devices  99.2 us (47%)
  starting transfers between devices  65 us (31%)
  Pallas kernels  26.3 us (13%)
  local copies, waits for them, and re-layouts  17.8 us (8%)
    ppermute x66, waiting for transfers between devices, flip(): return lax.ppermute(value, 'expert', [(i, i ^ mask) for i in range(size)])  82 us
    ppermute x66, starting transfers between devices, flip(): return lax.ppermute(value, 'expert', [(i, i ^ mask) for i in range(size)])  60.7 us
    pallas_call x14, Pallas kernels, call(): pl.pallas_call(body, in_specs=in_specs, out_specs=[VMEM] * len(outs), out...  26.3 us
    ppermute x1, waiting for transfers between devices, fetch_weights(): out_got = lax.ppermute(out_half, 'dp', source)  17.2 us
    unnamed x50, local copies, waits for them, and re-layouts  16.1 us
  transfers between devices with their start and end apart: 68, of which 26 were waited for; matrix products, arithmetic and copies ran while one was open for 2% of the time, Pallas kernels for 10%

profile of v4, /device:TPU:0, one launch (start us, length us, event | category | flops | bytes accessed | tf_op | source)
XLA Modules:
  0.0 210.0 jit_solution(4662122436226712412)
XLA Ops:
  1.5 3.0 %collective-permute-start.18 = (bf16[256,2048]{1,0:T(8,128)(2,1)S(1)}, bf16[256,2048]{1,0:T(8,128)(2,1)S(1)}, u32[]{:S(2)}, u32[]{:S(2)}) collective-permute-start(bf16[256,2048]{1,0:T(8,128)(2,1)S(1)} %constant_dynamic-slice_fusion), channel_id=1, source_target_pairs={{16,0},{0,16},{17,1},{1,17},{18,2},{2,18},{19,3},{3,19},{20,4},{4,... | collective-permute-start | bytes 3145736 | tf_op jit(solution)/shard_map/ppermute | solution.py:64
  6.9 3.6 %collective-permute-start.2 = (bf16[64,1024]{1,0:T(8,128)(2,1)S(1)}, bf16[64,1024]{1,0:T(8,128)(2,1)}, u32[]{:S(2)}, u32[]{:S(2)}) collective-permute-start(bf16[64,1024]{1,0:T(8,128)(2,1)S(1)} %bitcast.39), channel_id=1, source_target_pairs={{0,12},{1,13},{2,14},{3,15},{4,8},{5,9},{6,10},{7,11},{8,4},{9,5},... | collective-permute-start | bytes 393224 | tf_op jit(solution)/shard_map/ppermute | solution.py:24
  10.5 17.2 %collective-permute-done.18.refs_7_ = bf16[256,2048]{1,0:T(8,128)(2,1)S(1)} collective-permute-done((bf16[256,2048]{1,0:T(8,128)(2,1)S(1)}, bf16[256,2048]{1,0:T(8,128)(2,1)S(1)}, u32[]{:S(2)}, u32[]{:S(2)}) %collective-permute-start.18) | collective-permute-done | bytes 1048608 | tf_op jit(solution)/shard_map/ppermute | solution.py:64
  27.7 2.8 %collective-permute-start.10 = (bf16[64,1024]{1,0:T(8,128)(2,1)S(1)}, bf16[64,1024]{1,0:T(8,128)(2,1)}, u32[]{:S(2)}, u32[]{:S(2)}) collective-permute-start(bf16[64,1024]{1,0:T(8,128)(2,1)S(1)} %bitcast.40), channel_id=1, source_target_pairs={{0,8},{1,9},{2,10},{3,11},{4,12},{5,13},{6,14},{7,15},{8,0},{9,1},... | collective-permute-start | bytes 393224 | tf_op jit(solution)/shard_map/ppermute | solution.py:24
  34.4 3.3 %collective-permute-done.10.refs_11_ = bf16[64,1024]{1,0:T(8,128)(2,1)} collective-permute-done((bf16[64,1024]{1,0:T(8,128)(2,1)S(1)}, bf16[64,1024]{1,0:T(8,128)(2,1)}, u32[]{:S(2)}, u32[]{:S(2)}) %collective-permute-start.10) | collective-permute-done | bytes 131104 | tf_op jit(solution)/shard_map/ppermute | solution.py:24
  41.4 2.2 %collective-permute-done.15.refs_17_ = bf16[64,1024]{1,0:T(8,128)(2,1)} collective-permute-done((bf16[64,1024]{1,0:T(8,128)(2,1)}, bf16[64,1024]{1,0:T(8,128)(2,1)}, u32[]{:S(2)}, u32[]{:S(2)}) %collective-permute-start.15) | collective-permute-done | bytes 131104 | tf_op jit(solution)/shard_map/ppermute | solution.py:24
  46.4 2.3 %collective-permute-done.8.refs_9_ = bf16[64,1024]{1,0:T(8,128)(2,1)} collective-permute-done((bf16[64,1024]{1,0:T(8,128)(2,1)}, bf16[64,1024]{1,0:T(8,128)(2,1)}, u32[]{:S(2)}, u32[]{:S(2)}) %collective-permute-start.8) | collective-permute-done | bytes 131104 | tf_op jit(solution)/shard_map/ppermute | solution.py:24
  59.3 5.2 %shard_map.128.refs_1_ = bf16[128,4096]{1,0:T(8,128)(2,1)S(1)} custom-call(s32[12]{0:T(128)S(1)} %pad_add_fusion.info.refs_0_, bf16[64,8192]{1,0:T(8,128)(2,1)S(1)} %bitcast.35, bf16[32,1024]{1,0:T(8,128)(2,1)S(1)} %bitcast.45, bf16[64,1024]{1,0:T(8,128)(2,1)S(1)} %bitcast.44, bf16[64,1024]{1,0:T(8,128)(2,1)S(1)} %copy-done.10, ...), custom_call_target="tpu_custom_call" | custom-call | flops 2214592512 | tf_op jit(solution)/shard_map/pallas_call | solution.py:28
  64.5 3.6 %shard_map.129 = (f32[128,2048]{1,0:T(8,128)S(1)}, bf16[128,1024]{1,0:T(8,128)(2,1)}, bf16[128,1024]{1,0:T(8,128)(2,1)}) custom-call(s32[8]{0:T(128)S(1)} %stack.43.refs_0_, bf16[128,4096]{1,0:T(8,128)(2,1)S(1)} %shard_map.128.refs_1_, bf16[64,4096]{1,0:T(8,128)(2,1)S(1)} %bitcast.34, bf16[1,2048]{1,0:T(2,128)(2,1)S(1)} %reshape.13.refs_3_, ...), custom_call_target="tpu_custom_call" | custom-call | flops 536870912 | tf_op jit(solution)/shard_map/pallas_call | solution.py:28
  68.2 2.9 %collective-permute-start.44 = (bf16[128,1024]{1,0:T(8,128)(2,1)}, bf16[128,1024]{1,0:T(8,128)(2,1)S(1)}, u32[]{:S(2)}, u32[]{:S(2)}) collective-permute-start(bf16[128,1024]{1,0:T(8,128)(2,1)} %get-tuple-element.75.refs_1_), channel_id=1, source_target_pairs={{0,8},{1,9},{2,10},{3,11},{4,12},{5,13},{6,14},{7,15},{8,0},{9,1},... | collective-permute-start | bytes 786440 | tf_op jit(solution)/shard_map/ppermute | solution.py:24
  72.7 2.9 %collective-permute-start.1 = (f32[128,12]{1,0:T(8,128)S(1)}, f32[128,12]{1,0:T(8,128)S(1)}, u32[]{:S(2)}, u32[]{:S(2)}) collective-permute-start(f32[128,12]{1,0:T(8,128)S(1)} %bitcast.37), channel_id=1, source_target_pairs={{0,8},{1,9},{2,10},{3,11},{4,12},{5,13},{6,14},{7,15},{8,0},{9,1},... | collective-permute-start | bytes 18440 | tf_op jit(solution)/shard_map/ppermute | solution.py:24
  75.6 6.6 %collective-permute-done.side = f32[128,12]{1,0:T(8,128)S(1)} collective-permute-done((f32[128,12]{1,0:T(8,128)S(1)}, f32[128,12]{1,0:T(8,128)S(1)}, u32[]{:S(2)}, u32[]{:S(2)}) %collective-permute-start) | collective-permute-done | bytes 6176 | tf_op jit(solution)/shard_map/ppermute | solution.py:24
  82.2 15.3 %collective-permute-done.1.far = f32[128,12]{1,0:T(8,128)S(1)} collective-permute-done((f32[128,12]{1,0:T(8,128)S(1)}, f32[128,12]{1,0:T(8,128)S(1)}, u32[]{:S(2)}, u32[]{:S(2)}) %collective-permute-start.1) | collective-permute-done | bytes 6176 | tf_op jit(solution)/shard_map/ppermute | solution.py:24
  110.1 2.3 %collective-permute-done.42.refs_6_ = bf16[400,128]{1,0:T(8,128)(2,1)S(1)} collective-permute-done((bf16[400,128]{1,0:T(8,128)(2,1)S(1)}, bf16[400,128]{1,0:T(8,128)(2,1)S(1)}, u32[]{:S(2)}, u32[]{:S(2)}) %collective-permute-start.42) | collective-permute-done | bytes 102432 | tf_op jit(solution)/shard_map/ppermute | solution.py:24
  113.7 1.8 collective-permute-start.50
  120.4 1.8 collective-permute-done.50.refs_14_
  125.3 1.8 copy-done.3
  127.1 1.8 copy-done.5
  128.9 1.8 copy-done.6
  130.7 4.7 %shard_map.137 = (bf16[400,128]{1,0:T(8,128)(2,1)S(1)}, bf16[400,128]{1,0:T(8,128)(2,1)S(1)}, bf16[400,128]{1,0:T(8,128)(2,1)S(1)}, bf16[400,128]{1,0:T(8,128)(2...) custom-call(bf16[1,704,2048]{2,1,0:T(8,128)(2,1)S(1)} %bitcast.46, ...), custom_call_target="tpu_custom_call" | custom-call | flops 3875536896 | tf_op jit(solution)/shard_map/pallas_call | solution.py:28
  137.4 1.7 collective-permute-start.64
  139.6 1.8 collective-permute-done.61.refs_2_
  145.4 2.3 %collective-permute-done.65.refs_6_ = bf16[400,128]{1,0:T(8,128)(2,1)S(1)} collective-permute-done((bf16[400,128]{1,0:T(8,128)(2,1)S(1)}, bf16[400,128]{1,0:T(8,128)(2,1)S(1)}, u32[]{:S(2)}, u32[]{:S(2)}) %collective-permute-start.65) | collective-permute-done | bytes 102432 | tf_op jit(solution)/shard_map/ppermute | solution.py:24
  150.1 2.6 %shard_map.131 = (bf16[800,128]{1,0:T(8,128)(2,1)S(1)}, bf16[800,128]{1,0:T(8,128)(2,1)S(1)}, bf16[800,128]{1,0:T(8,128)(2,1)S(1)}, bf16[800,128]{1,0:T(8,128)(2,1)S(1)}) custom-call(bf16[1,704,2048]{2,1,0:T(8,128)(2,1)S(1)} %bitcast.47, bf16[1,704,2048]{2,1,0:T(8,128)(2,1)S(1)} %bitcast.50, bf16[1,704,2048]{2,1,0:T(8,128)(2,1)S(1)} %copy-done.6, ...), custom_call_target="tpu_custom_call" | custom-call | flops 3875536896 | tf_op jit(solution)/shard_map/pallas_call | solution.py:28
  152.9 7.2 %collective-permute-done.53.refs_2_ = bf16[400,128]{1,0:T(8,128)(2,1)S(1)} collective-permute-done((bf16[400,128]{1,0:T(8,128)(2,1)S(1)}, bf16[400,128]{1,0:T(8,128)(2,1)S(1)}, u32[]{:S(2)}, u32[]{:S(2)}) %collective-permute-start.53) | collective-permute-done | bytes 102432 | tf_op jit(solution)/shard_map/ppermute | solution.py:24
  163.5 2.6 %shard_map.133 = (bf16[800,128]{1,0:T(8,128)(2,1)S(1)}, bf16[800,128]{1,0:T(8,128)(2,1)S(1)}, bf16[800,128]{1,0:T(8,128)(2,1)S(1)}, bf16[800,128]{1,0:T(8,128)(2,1)S(1)}) custom-call(bf16[1,704,2048]{2,1,0:T(8,128)(2,1)S(1)} %bitcast.48, bf16[1,704,2048]{2,1,0:T(8,128)(2,1)S(1)} %bitcast.51, bf16[1,704,2048]{2,1,0:T(8,128)(2,1)S(1)} %copy-done.6, ...), custom_call_target="tpu_custom_call" | custom-call | flops 3875536896 | tf_op jit(solution)/shard_map/pallas_call | solution.py:28
  169.2 1.8 collective-permute-done.57.refs_6_
  171.9 6.3 %collective-permute-done.58.refs_7_ = bf16[400,128]{1,0:T(8,128)(2,1)S(1)} collective-permute-done((bf16[400,128]{1,0:T(8,128)(2,1)S(1)}, bf16[400,128]{1,0:T(8,128)(2,1)S(1)}, u32[]{:S(2)}, u32[]{:S(2)}) %collective-permute-start.58) | collective-permute-done | bytes 102432 | tf_op jit(solution)/shard_map/ppermute | solution.py:24
  183.6 2.2 %collective-permute-start.35 = (bf16[800,128]{1,0:T(8,128)(2,1)S(1)}, bf16[800,128]{1,0:T(8,128)(2,1)S(1)}, u32[]{:S(2)}, u32[]{:S(2)}) collective-permute-start(bf16[800,128]{1,0:T(8,128)(2,1)S(1)} %get-tuple-element.92), channel_id=1, source_target_pairs={{0,7},{1,6},{2,5},{3,4},{4,3},{5,2},{6,1},{7,0},{8,15},{9,14},{10,... | collective-permute-start | bytes 614408 | tf_op jit(solution)/shard_map/ppermute | solution.py:24
  185.8 10.5 %collective-permute-done.33.refs_5_ = bf16[800,128]{1,0:T(8,128)(2,1)S(1)} collective-permute-done((bf16[800,128]{1,0:T(8,128)(2,1)S(1)}, bf16[800,128]{1,0:T(8,128)(2,1)S(1)}, u32[]{:S(2)}, u32[]{:S(2)}) %collective-permute-start.33) | collective-permute-done | bytes 204832 | tf_op jit(solution)/shard_map/ppermute | solution.py:24
  196.4 4.4 %collective-permute-done.34.refs_6_ = bf16[800,128]{1,0:T(8,128)(2,1)S(1)} collective-permute-done((bf16[800,128]{1,0:T(8,128)(2,1)S(1)}, bf16[800,128]{1,0:T(8,128)(2,1)S(1)}, u32[]{:S(2)}, u32[]{:S(2)}) %collective-permute-start.34) | collective-permute-done | bytes 204832 | tf_op jit(solution)/shard_map/ppermute | solution.py:24
  200.7 7.0 %collective-permute-done.35.refs_7_ = bf16[800,128]{1,0:T(8,128)(2,1)S(1)} collective-permute-done((bf16[800,128]{1,0:T(8,128)(2,1)S(1)}, bf16[800,128]{1,0:T(8,128)(2,1)S(1)}, u32[]{:S(2)}, u32[]{:S(2)}) %collective-permute-start.35) | collective-permute-done | bytes 204832 | tf_op jit(solution)/shard_map/ppermute | solution.py:24
  (178 shorter events, 72.1 us)
Async XLA Ops:
  1.5 26.2 %collective-permute-start.18 = (bf16[256,2048]{1,0:T(8,128)(2,1)S(1)}, bf16[256,2048]{1,0:T(8,128)(2,1)S(1)}, u32[]{:S(2)}, u32[]{:S(2)}) collective-permute-start(bf16[256,2048]{1,0:T(8,128)(2,1)S(1)} %constant_dynamic-slice_fusion), channel_id=1, source_target_pairs={{16,0},{0,16},{17,1},{1,17},{18,2},{2,18},{19,3},{3,19},{20,4},{4,... | collective-permute-start | bytes 3145736 | tf_op jit(solution)/shard_map/ppermute | solution.py:64
  6.9 26.7 %collective-permute-start.2 = (bf16[64,1024]{1,0:T(8,128)(2,1)S(1)}, bf16[64,1024]{1,0:T(8,128)(2,1)}, u32[]{:S(2)}, u32[]{:S(2)}) collective-permute-start(bf16[64,1024]{1,0:T(8,128)(2,1)S(1)} %bitcast.39), channel_id=1, source_target_pairs={{0,12},{1,13},{2,14},{3,15},{4,8},{5,9},{6,10},{7,11},{8,4},{9,5},... | collective-permute-start | bytes 393224 | tf_op jit(solution)/shard_map/ppermute | solution.py:24
  27.7 36.8 %collective-permute-start.20 = (bf16[256,2048]{1,0:T(8,128)(2,1)S(1)}, bf16[256,2048]{1,0:T(8,128)(2,1)}, u32[]{:S(2)}, u32[]{:S(2)}) collective-permute-start(bf16[256,2048]{1,0:T(8,128)(2,1)S(1)} %collective-permute-done.18.refs_7_), channel_id=1, source_target_pairs={{0,1},{1,0},{2,3},{3,2},{4,5},{5,4},{6,7},{7,6},{8,9},{9,8},{10,11... | collective-permute-start | bytes 3145736 | tf_op jit(solution)/shard_map/ppermute | solution.py:24
  27.7 10.0 %collective-permute-start.10 = (bf16[64,1024]{1,0:T(8,128)(2,1)S(1)}, bf16[64,1024]{1,0:T(8,128)(2,1)}, u32[]{:S(2)}, u32[]{:S(2)}) collective-permute-start(bf16[64,1024]{1,0:T(8,128)(2,1)S(1)} %bitcast.40), channel_id=1, source_target_pairs={{0,8},{1,9},{2,10},{3,11},{4,12},{5,13},{6,14},{7,15},{8,0},{9,1},... | collective-permute-start | bytes 393224 | tf_op jit(solution)/shard_map/ppermute | solution.py:24
  39.8 9.0 %collective-permute-start.8 = (bf16[64,1024]{1,0:T(8,128)(2,1)}, bf16[64,1024]{1,0:T(8,128)(2,1)}, u32[]{:S(2)}, u32[]{:S(2)}) collective-permute-start(bf16[64,1024]{1,0:T(8,128)(2,1)} %collective-permute-done.6.refs_7_), channel_id=1, source_target_pairs={{0,2},{1,3},{2,0},{3,1},{4,6},{5,7},{6,4},{7,5},{8,10},{9,11},{10,... | collective-permute-start | bytes 393224 | tf_op jit(solution)/shard_map/ppermute | solution.py:24
  43.6 8.8 %collective-permute-start.17 = (bf16[2,512,128]{2,1,0:T(8,128)(2,1)S(1)}, bf16[2,512,128]{2,1,0:T(8,128)(2,1)S(1)}, u32[]{:S(2)}, u32[]{:S(2)}) collective-permute-start(bf16[2,512,128]{2,1,0:T(8,128)(2,1)S(1)} %constant_dynamic-slice_fusion.1), channel_id=1, source_target_pairs={{16,0},{0,16},{17,1},{1,17},{18,2},{2,18},{19,3},{3,19},{20,4},{4,... | collective-permute-start | bytes 786440 | tf_op jit(solution)/shard_map/ppermute | solution.py:63
  52.4 12.1 %collective-permute-start.19 = (bf16[2,512,128]{2,1,0:T(8,128)(2,1)S(1)}, bf16[2,512,128]{2,1,0:T(8,128)(2,1)}, u32[]{:S(2)}, u32[]{:S(2)}) collective-permute-start(bf16[2,512,128]{2,1,0:T(8,128)(2,1)S(1)} %collective-permute-done.17.refs_6_), channel_id=1, source_target_pairs={{0,1},{1,0},{2,3},{3,2},{4,5},{5,4},{6,7},{7,6},{8,9},{9,8},{10,11... | collective-permute-start | bytes 786440 | tf_op jit(solution)/shard_map/ppermute | solution.py:24
  68.1 30.9 %collective-permute-start.36 = (bf16[128,1024]{1,0:T(8,128)(2,1)}, bf16[128,1024]{1,0:T(8,128)(2,1)S(1)}, u32[]{:S(2)}, u32[]{:S(2)}) collective-permute-start(bf16[128,1024]{1,0:T(8,128)(2,1)} %get-tuple-element.74.refs_0_), channel_id=1, source_target_pairs={{0,8},{1,9},{2,10},{3,11},{4,12},{5,13},{6,14},{7,15},{8,0},{9,1},... | collective-permute-start | bytes 786440 | tf_op jit(solution)/shard_map/ppermute | solution.py:24
  68.2 33.2 %collective-permute-start.44 = (bf16[128,1024]{1,0:T(8,128)(2,1)}, bf16[128,1024]{1,0:T(8,128)(2,1)S(1)}, u32[]{:S(2)}, u32[]{:S(2)}) collective-permute-start(bf16[128,1024]{1,0:T(8,128)(2,1)} %get-tuple-element.75.refs_1_), channel_id=1, source_target_pairs={{0,8},{1,9},{2,10},{3,11},{4,12},{5,13},{6,14},{7,15},{8,0},{9,1},... | collective-permute-start | bytes 786440 | tf_op jit(solution)/shard_map/ppermute | solution.py:24
  71.2 11.0 %collective-permute-start = (f32[128,12]{1,0:T(8,128)S(1)}, f32[128,12]{1,0:T(8,128)S(1)}, u32[]{:S(2)}, u32[]{:S(2)}) collective-permute-start(f32[128,12]{1,0:T(8,128)S(1)} %bitcast.36), channel_id=1, source_target_pairs={{0,4},{1,5},{2,6},{3,7},{4,0},{5,1},{6,2},{7,3},{8,12},{9,13},{10,... | collective-permute-start | bytes 18440 | tf_op jit(solution)/shard_map/ppermute | solution.py:24
  72.7 24.8 %collective-permute-start.1 = (f32[128,12]{1,0:T(8,128)S(1)}, f32[128,12]{1,0:T(8,128)S(1)}, u32[]{:S(2)}, u32[]{:S(2)}) collective-permute-start(f32[128,12]{1,0:T(8,128)S(1)} %bitcast.37), channel_id=1, source_target_pairs={{0,8},{1,9},{2,10},{3,11},{4,12},{5,13},{6,14},{7,15},{8,0},{9,1},... | collective-permute-start | bytes 18440 | tf_op jit(solution)/shard_map/ppermute | solution.py:24
  103.5 8.9 %collective-permute-start.42 = (bf16[400,128]{1,0:T(8,128)(2,1)S(1)}, bf16[400,128]{1,0:T(8,128)(2,1)S(1)}, u32[]{:S(2)}, u32[]{:S(2)}) collective-permute-start(bf16[400,128]{1,0:T(8,128)(2,1)S(1)} %get-tuple-element.101), channel_id=1, source_target_pairs={{0,6},{1,7},{2,4},{3,5},{4,2},{5,3},{6,0},{7,1},{8,14},{9,15},{10,... | collective-permute-start | bytes 307208 | tf_op jit(solution)/shard_map/ppermute | solution.py:24
  107.1 9.1 %collective-permute-start.46 = (bf16[400,128]{1,0:T(8,128)(2,1)S(1)}, bf16[400,128]{1,0:T(8,128)(2,1)S(1)}, u32[]{:S(2)}, u32[]{:S(2)}) collective-permute-start(bf16[400,128]{1,0:T(8,128)(2,1)S(1)} %get-tuple-element.105), channel_id=1, source_target_pairs={{0,2},{1,3},{2,0},{3,1},{4,6},{5,7},{6,4},{7,5},{8,10},{9,11},{10,... | collective-permute-start | bytes 307208 | tf_op jit(solution)/shard_map/ppermute | solution.py:24
  108.5 9.8 %collective-permute-start.47 = (bf16[400,128]{1,0:T(8,128)(2,1)S(1)}, bf16[400,128]{1,0:T(8,128)(2,1)S(1)}, u32[]{:S(2)}, u32[]{:S(2)}) collective-permute-start(bf16[400,128]{1,0:T(8,128)(2,1)S(1)} %get-tuple-element.106), channel_id=1, source_target_pairs={{0,3},{1,2},{2,1},{3,0},{4,7},{5,6},{6,5},{7,4},{8,11},{9,10},{10,... | collective-permute-start | bytes 307208 | tf_op jit(solution)/shard_map/ppermute | solution.py:24
  118.3 19.1 %collective-permute-start.27 = (bf16[128,1024]{1,0:T(8,128)(2,1)}, bf16[128,1024]{1,0:T(8,128)(2,1)S(1)}, u32[]{:S(2)}, u32[]{:S(2)}) collective-permute-start(bf16[128,1024]{1,0:T(8,128)(2,1)} %get-tuple-element.74.refs_0_), channel_id=1, source_target_pairs={{0,4},{1,5},{2,6},{3,7},{4,0},{5,1},{6,2},{7,3},{8,12},{9,13},{10,... | collective-permute-start | bytes 786440 | tf_op jit(solution)/shard_map/ppermute | solution.py:24
  119.4 18.1 %collective-permute-start.28 = (bf16[128,1024]{1,0:T(8,128)(2,1)}, bf16[128,1024]{1,0:T(8,128)(2,1)S(1)}, u32[]{:S(2)}, u32[]{:S(2)}) collective-permute-start(bf16[128,1024]{1,0:T(8,128)(2,1)} %get-tuple-element.75.refs_1_), channel_id=1, source_target_pairs={{0,4},{1,5},{2,6},{3,7},{4,0},{5,1},{6,2},{7,3},{8,12},{9,13},{10,... | collective-permute-start | bytes 786440 | tf_op jit(solution)/shard_map/ppermute | solution.py:24
  120.4 15.0 %collective-permute-start.21 = (bf16[800,128]{1,0:T(8,128)(2,1)S(1)}, bf16[800,128]{1,0:T(8,128)(2,1)S(1)}, u32[]{:S(2)}, u32[]{:S(2)}) collective-permute-start(bf16[800,128]{1,0:T(8,128)(2,1)S(1)} %get-tuple-element.77), channel_id=1, source_target_pairs={{0,1},{1,0},{2,3},{3,2},{4,5},{5,4},{6,7},{7,6},{8,9},{9,8},{10,11... | collective-permute-start | bytes 614408 | tf_op jit(solution)/shard_map/ppermute | solution.py:24
  122.2 13.3 %collective-permute-start.22 = (bf16[800,128]{1,0:T(8,128)(2,1)S(1)}, bf16[800,128]{1,0:T(8,128)(2,1)S(1)}, u32[]{:S(2)}, u32[]{:S(2)}) collective-permute-start(bf16[800,128]{1,0:T(8,128)(2,1)S(1)} %get-tuple-element.78), channel_id=1, source_target_pairs={{0,2},{1,3},{2,0},{3,1},{4,6},{5,7},{6,4},{7,5},{8,10},{9,11},{10,... | collective-permute-start | bytes 614408 | tf_op jit(solution)/shard_map/ppermute | solution.py:24
  123.7 12.6 %collective-permute-start.23 = (bf16[800,128]{1,0:T(8,128)(2,1)S(1)}, bf16[800,128]{1,0:T(8,128)(2,1)S(1)}, u32[]{:S(2)}, u32[]{:S(2)}) collective-permute-start(bf16[800,128]{1,0:T(8,128)(2,1)S(1)} %get-tuple-element.79), channel_id=1, source_target_pairs={{0,3},{1,2},{2,1},{3,0},{4,7},{5,6},{6,5},{7,4},{8,11},{9,10},{10,... | collective-permute-start | bytes 614408 | tf_op jit(solution)/shard_map/ppermute | solution.py:24
  142.5 18.3 %collective-permute-start.29 = (bf16[800,128]{1,0:T(8,128)(2,1)S(1)}, bf16[800,128]{1,0:T(8,128)(2,1)S(1)}, u32[]{:S(2)}, u32[]{:S(2)}) collective-permute-start(bf16[800,128]{1,0:T(8,128)(2,1)S(1)} %get-tuple-element.86), channel_id=1, source_target_pairs={{0,1},{1,0},{2,3},{3,2},{4,5},{5,4},{6,7},{7,6},{8,9},{9,8},{10,11... | collective-permute-start | bytes 614408 | tf_op jit(solution)/shard_map/ppermute | solution.py:24
  143.2 18.3 %collective-permute-start.30 = (bf16[800,128]{1,0:T(8,128)(2,1)S(1)}, bf16[800,128]{1,0:T(8,128)(2,1)S(1)}, u32[]{:S(2)}, u32[]{:S(2)}) collective-permute-start(bf16[800,128]{1,0:T(8,128)(2,1)S(1)} %get-tuple-element.87), channel_id=1, source_target_pairs={{0,2},{1,3},{2,0},{3,1},{4,6},{5,7},{6,4},{7,5},{8,10},{9,11},{10,... | collective-permute-start | bytes 614408 | tf_op jit(solution)/shard_map/ppermute | solution.py:24
  144.2 18.7 %collective-permute-start.31 = (bf16[800,128]{1,0:T(8,128)(2,1)S(1)}, bf16[800,128]{1,0:T(8,128)(2,1)S(1)}, u32[]{:S(2)}, u32[]{:S(2)}) collective-permute-start(bf16[800,128]{1,0:T(8,128)(2,1)S(1)} %get-tuple-element.88), channel_id=1, source_target_pairs={{0,3},{1,2},{2,1},{3,0},{4,7},{5,6},{6,5},{7,4},{8,11},{9,10},{10,... | collective-permute-start | bytes 614408 | tf_op jit(solution)/shard_map/ppermute | solution.py:24
  148.7 11.5 %collective-permute-start.53 = (bf16[400,128]{1,0:T(8,128)(2,1)S(1)}, bf16[400,128]{1,0:T(8,128)(2,1)S(1)}, u32[]{:S(2)}, u32[]{:S(2)}) collective-permute-start(bf16[400,128]{1,0:T(8,128)(2,1)S(1)} %get-tuple-element.113), channel_id=1, source_target_pairs={{0,2},{1,3},{2,0},{3,1},{4,6},{5,7},{6,4},{7,5},{8,10},{9,11},{10,... | collective-permute-start | bytes 307208 | tf_op jit(solution)/shard_map/ppermute | solution.py:24
  152.7 27.5 %collective-permute-start.24 = (bf16[800,128]{1,0:T(8,128)(2,1)S(1)}, bf16[800,128]{1,0:T(8,128)(2,1)S(1)}, u32[]{:S(2)}, u32[]{:S(2)}) collective-permute-start(bf16[800,128]{1,0:T(8,128)(2,1)S(1)} %get-tuple-element.81), channel_id=1, source_target_pairs={{0,1},{1,0},{2,3},{3,2},{4,5},{5,4},{6,7},{7,6},{8,9},{9,8},{10,11... | collective-permute-start | bytes 614408 | tf_op jit(solution)/shard_map/ppermute | solution.py:24
  166.1 15.6 %collective-permute-start.25 = (bf16[800,128]{1,0:T(8,128)(2,1)S(1)}, bf16[800,128]{1,0:T(8,128)(2,1)S(1)}, u32[]{:S(2)}, u32[]{:S(2)}) collective-permute-start(bf16[800,128]{1,0:T(8,128)(2,1)S(1)} %get-tuple-element.82), channel_id=1, source_target_pairs={{0,2},{1,3},{2,0},{3,1},{4,6},{5,7},{6,4},{7,5},{8,10},{9,11},{10,... | collective-permute-start | bytes 614408 | tf_op jit(solution)/shard_map/ppermute | solution.py:24
  167.5 15.1 %collective-permute-start.26 = (bf16[800,128]{1,0:T(8,128)(2,1)S(1)}, bf16[800,128]{1,0:T(8,128)(2,1)S(1)}, u32[]{:S(2)}, u32[]{:S(2)}) collective-permute-start(bf16[800,128]{1,0:T(8,128)(2,1)S(1)} %get-tuple-element.83), channel_id=1, source_target_pairs={{0,3},{1,2},{2,1},{3,0},{4,7},{5,6},{6,5},{7,4},{8,11},{9,10},{10,... | collective-permute-start | bytes 614408 | tf_op jit(solution)/shard_map/ppermute | solution.py:24
  168.2 15.4 %collective-permute-start.32 = (bf16[800,128]{1,0:T(8,128)(2,1)S(1)}, bf16[800,128]{1,0:T(8,128)(2,1)S(1)}, u32[]{:S(2)}, u32[]{:S(2)}) collective-permute-start(bf16[800,128]{1,0:T(8,128)(2,1)S(1)} %get-tuple-element.89), channel_id=1, source_target_pairs={{0,4},{1,5},{2,6},{3,7},{4,0},{5,1},{6,2},{7,3},{8,12},{9,13},{10,... | collective-permute-start | bytes 614408 | tf_op jit(solution)/shard_map/ppermute | solution.py:24
  178.1 30.7 %collective-permute-start.67 = (bf16[128,1024]{1,0:T(8,128)(2,1)S(1)}, bf16[128,1024]{1,0:T(8,128)(2,1)S(1)}, u32[]{:S(2)}, u32[]{:S(2)}) collective-permute-start(bf16[128,1024]{1,0:T(8,128)(2,1)S(1)} %shard_map.139), channel_id=1, source_target_pairs={{0,8},{1,9},{2,10},{3,11},{4,12},{5,13},{6,14},{7,15},{8,0},{9,1},... | collective-permute-start | bytes 786440 | tf_op jit(solution)/shard_map/ppermute | solution.py:24
  180.2 28.6 %collective-permute-start.59 = (bf16[128,1024]{1,0:T(8,128)(2,1)S(1)}, bf16[128,1024]{1,0:T(8,128)(2,1)S(1)}, u32[]{:S(2)}, u32[]{:S(2)}) collective-permute-start(bf16[128,1024]{1,0:T(8,128)(2,1)S(1)} %shard_map.138), channel_id=1, source_target_pairs={{0,8},{1,9},{2,10},{3,11},{4,12},{5,13},{6,14},{7,15},{8,0},{9,1},... | collective-permute-start | bytes 786440 | tf_op jit(solution)/shard_map/ppermute | solution.py:24
  181.7 14.6 %collective-permute-start.33 = (bf16[800,128]{1,0:T(8,128)(2,1)S(1)}, bf16[800,128]{1,0:T(8,128)(2,1)S(1)}, u32[]{:S(2)}, u32[]{:S(2)}) collective-permute-start(bf16[800,128]{1,0:T(8,128)(2,1)S(1)} %get-tuple-element.90), channel_id=1, source_target_pairs={{0,5},{1,4},{2,7},{3,6},{4,1},{5,0},{6,3},{7,2},{8,13},{9,12},{10,... | collective-permute-start | bytes 614408 | tf_op jit(solution)/shard_map/ppermute | solution.py:24
  182.6 18.2 %collective-permute-start.34 = (bf16[800,128]{1,0:T(8,128)(2,1)S(1)}, bf16[800,128]{1,0:T(8,128)(2,1)S(1)}, u32[]{:S(2)}, u32[]{:S(2)}) collective-permute-start(bf16[800,128]{1,0:T(8,128)(2,1)S(1)} %get-tuple-element.91), channel_id=1, source_target_pairs={{0,6},{1,7},{2,4},{3,5},{4,2},{5,3},{6,0},{7,1},{8,14},{9,15},{10,... | collective-permute-start | bytes 614408 | tf_op jit(solution)/shard_map/ppermute | solution.py:24
  183.6 24.2 %collective-permute-start.35 = (bf16[800,128]{1,0:T(8,128)(2,1)S(1)}, bf16[800,128]{1,0:T(8,128)(2,1)S(1)}, u32[]{:S(2)}, u32[]{:S(2)}) collective-permute-start(bf16[800,128]{1,0:T(8,128)(2,1)S(1)} %get-tuple-element.92), channel_id=1, source_target_pairs={{0,7},{1,6},{2,5},{3,4},{4,3},{5,2},{6,1},{7,0},{8,15},{9,14},{10,... | collective-permute-start | bytes 614408 | tf_op jit(solution)/shard_map/ppermute | solution.py:24
  (59 other events, 487.9 us)
